TPU v7x, 128 devices: a whole 4x4x4 slice. The times are simulated.
128 devices in a mesh: fsdp: 64 (over z, y, x), cp: 2 (over core).
Axes of the slice: x: 4, y: 4, z: 4, core: 2. Of those that a mesh axis runs over, the one named last changes fastest.
Arguments:
- hidden: bfloat16 [64, 1024, 2048], P('fsdp', 'cp')
- doc_ids: int32 [64, 1024], P('fsdp', 'cp')
- doc_pos: int32 [64, 1024], P('fsdp', 'cp')
- grad_out: bfloat16 [64, 1024, 2048], P('fsdp', 'cp')
- w_query: bfloat16 [2048, 8, 256], P('fsdp')
- w_key: bfloat16 [2048, 1, 256], P('fsdp')
- w_value: bfloat16 [2048, 1, 256], P('fsdp')
- w_out: bfloat16 [8, 256, 2048], P(None, None, 'fsdp')
- gain_pre: bfloat16 [2048], P('fsdp')
- gain_post: bfloat16 [2048], P('fsdp')
Outputs:
- output 1: bfloat16 [64, 1024, 2048], P('fsdp', 'cp')
- output 2: bfloat16 [64, 1024, 2048], P('fsdp', 'cp')
- output 3: float32 [2048, 8, 256], P('fsdp')
- output 4: float32 [2048, 1, 256], P('fsdp')
- output 5: float32 [2048, 1, 256], P('fsdp')
- output 6: float32 [8, 256, 2048], P(None, None, 'fsdp')
- output 7: float32 [2048], P('fsdp')
- output 8: float32 [2048], P('fsdp')
All inputs are finite; a program needn't handle non-finite values.
Results may differ from a plain program's by a relative error of at most 0.0170023.
Values are sent between devices in bfloat16 or wider.
A program may use at most 1 GiB of HBM per device.

v0:
```python
import jax
import jax.numpy as jnp
from jax import lax
from jax.sharding import PartitionSpec as P

SOFT_CAP = 50.0
NORM_EPS = 1e-6
ROPE_BASE = 10000.0


def query_scale(model_dim, n_heads, head_dim):
    pre_scalar = head_dim if head_dim >= 256 else model_dim // n_heads
    return pre_scalar ** -0.5


def rope_tables(pos_ids, head_dim):
    half_dim = head_dim // 2
    inv_freq = ROPE_BASE ** (-2.0 * jnp.arange(half_dim, dtype=jnp.float32) / head_dim)
    angles = pos_ids.astype(jnp.float32)[..., None] * inv_freq
    return jnp.cos(angles)[..., None, :], jnp.sin(angles)[..., None, :]


def rotate(values, cos_t, sin_t):
    half_dim = values.shape[-1] // 2
    first_half = values[..., :half_dim].astype(jnp.float32)
    second_half = values[..., half_dim:].astype(jnp.float32)
    rotated = jnp.concatenate([first_half * cos_t - second_half * sin_t,
                               second_half * cos_t + first_half * sin_t], axis=-1)
    return rotated.astype(jnp.bfloat16)


def rotate_back(grads, cos_t, sin_t):
    half_dim = grads.shape[-1] // 2
    first_half = grads[..., :half_dim].astype(jnp.float32)
    second_half = grads[..., half_dim:].astype(jnp.float32)
    rotated = jnp.concatenate([first_half * cos_t + second_half * sin_t,
                               second_half * cos_t - first_half * sin_t], axis=-1)
    return rotated.astype(jnp.bfloat16)


def norm_forward(values, gain_vec):
    values_f = values.astype(jnp.float32)
    inv_rms = lax.rsqrt(jnp.mean(values_f * values_f, axis=-1, keepdims=True) + NORM_EPS)
    normed = values_f * inv_rms * (1.0 + gain_vec.astype(jnp.float32))
    return normed.astype(jnp.bfloat16), inv_rms


def norm_backward(values, inv_rms, gain_vec, grads):
    values_f = values.astype(jnp.float32)
    grads_f = grads.astype(jnp.float32)
    scaled = grads_f * (1.0 + gain_vec.astype(jnp.float32))
    d_values = inv_rms * scaled - values_f * inv_rms ** 3 * jnp.mean(scaled * values_f, axis=-1, keepdims=True)
    d_gain = jnp.sum(grads_f * values_f * inv_rms, axis=(0, 1))
    return d_values, d_gain


def attention_forward(q_rot, k_all, v_all, visible, q_scale):
    n_batch, n_tok, n_heads, head_dim = q_rot.shape
    kv_heads = k_all.shape[2]
    q_grp = q_rot.reshape(n_batch, n_tok, kv_heads, n_heads // kv_heads, head_dim)
    scores = jnp.einsum('bqkgh,btkh->bkgqt', q_grp, k_all, preferred_element_type=jnp.float32) * q_scale
    tanh_s = jnp.tanh(scores / SOFT_CAP)
    capped = jnp.where(visible, SOFT_CAP * tanh_s, -1e30)
    row_peak = jnp.max(capped, axis=-1, keepdims=True)
    weights = jnp.exp(capped - row_peak)
    attn_prob = weights / jnp.sum(weights, axis=-1, keepdims=True)
    prob_low = attn_prob.astype(jnp.bfloat16)
    mixed = jnp.einsum('bkgqt,btkh->bqkgh', prob_low, v_all, preferred_element_type=jnp.float32)
    attn_out = mixed.astype(jnp.bfloat16).reshape(n_batch, n_tok, n_heads, head_dim)
    return attn_out, attn_prob, prob_low, tanh_s


def gather_rows(shard, axis_pos):
    return lax.all_gather(shard, 'fsdp', axis=axis_pos, tiled=True)


def reduce_grad(full, axis_pos):
    return lax.psum(lax.psum_scatter(full, 'fsdp', scatter_dimension=axis_pos, tiled=True), 'cp')


def solution(mesh):
    tok_spec = P('fsdp', 'cp', None)
    ids_spec = P('fsdp', 'cp')
    in_spec = P('fsdp', None, None)
    out_spec = P(None, None, 'fsdp')
    gain_spec = P('fsdp')

    def layer_local(hidden, doc_ids, doc_pos, grad_out, w_query, w_key, w_value, w_out, gain_pre, gain_post):
        n_batch, n_tok, model_dim = hidden.shape
        wq_full = gather_rows(w_query, 0)
        wk_full = gather_rows(w_key, 0)
        wv_full = gather_rows(w_value, 0)
        wo_full = gather_rows(w_out, 2)
        pre_full = gather_rows(gain_pre, 0)
        post_full = gather_rows(gain_post, 0)
        n_heads, head_dim = wq_full.shape[1], wq_full.shape[2]
        kv_heads = wk_full.shape[1]
        groups = n_heads // kv_heads
        q_scale = query_scale(model_dim, n_heads, head_dim)

        normed, inv_pre = norm_forward(hidden, pre_full)
        q_proj = jnp.einsum('btd,dnh->btnh', normed, wq_full, preferred_element_type=jnp.float32).astype(jnp.bfloat16)
        k_proj = jnp.einsum('btd,dnh->btnh', normed, wk_full, preferred_element_type=jnp.float32).astype(jnp.bfloat16)
        v_proj = jnp.einsum('btd,dnh->btnh', normed, wv_full, preferred_element_type=jnp.float32).astype(jnp.bfloat16)
        cos_t, sin_t = rope_tables(doc_pos, head_dim)
        q_rot = rotate(q_proj, cos_t, sin_t)
        k_rot = rotate(k_proj, cos_t, sin_t)

        k_all = lax.all_gather(k_rot, 'cp', axis=1, tiled=True)
        v_all = lax.all_gather(v_proj, 'cp', axis=1, tiled=True)
        ids_all = lax.all_gather(doc_ids, 'cp', axis=1, tiled=True)
        q_index = lax.axis_index('cp') * n_tok + jnp.arange(n_tok)
        k_index = jnp.arange(k_all.shape[1])
        visible = (doc_ids[:, :, None] == ids_all[:, None, :]) & (k_index[None, None, :] <= q_index[None, :, None])
        visible = visible[:, None, None]
        attn_out, attn_prob, prob_low, tanh_s = attention_forward(q_rot, k_all, v_all, visible, q_scale)
        proj_out = jnp.einsum('btnh,nhd->btd', attn_out, wo_full, preferred_element_type=jnp.float32).astype(jnp.bfloat16)
        post_out, inv_post = norm_forward(proj_out, post_full)
        out_hidden = (hidden.astype(jnp.float32) + post_out.astype(jnp.float32)).astype(jnp.bfloat16)

        d_proj, d_gain_post = norm_backward(proj_out, inv_post, post_full, grad_out)
        d_proj = d_proj.astype(jnp.bfloat16)
        d_attn = jnp.einsum('btd,nhd->btnh', d_proj, wo_full, preferred_element_type=jnp.float32).astype(jnp.bfloat16)
        d_w_out = jnp.einsum('btnh,btd->nhd', attn_out, d_proj, preferred_element_type=jnp.float32)

        q_grp = q_rot.reshape(n_batch, n_tok, kv_heads, groups, head_dim)
        d_grp = d_attn.reshape(n_batch, n_tok, kv_heads, groups, head_dim)
        d_prob = jnp.einsum('bqkgh,btkh->bkgqt', d_grp, v_all, preferred_element_type=jnp.float32)
        row_dot = jnp.sum(attn_prob * d_prob, axis=-1, keepdims=True)
        d_score = (attn_prob * (d_prob - row_dot) * (1.0 - tanh_s * tanh_s) * q_scale).astype(jnp.bfloat16)
        d_q_rot = jnp.einsum('bkgqt,btkh->bqkgh', d_score, k_all, preferred_element_type=jnp.float32)
        d_q_rot = d_q_rot.astype(jnp.bfloat16).reshape(n_batch, n_tok, n_heads, head_dim)
        d_k_part = jnp.einsum('bkgqt,bqkgh->btkh', d_score, q_grp, preferred_element_type=jnp.float32).astype(jnp.bfloat16)
        d_v_part = jnp.einsum('bkgqt,bqkgh->btkh', prob_low, d_grp, preferred_element_type=jnp.float32).astype(jnp.bfloat16)
        d_k_rot = lax.psum_scatter(d_k_part, 'cp', scatter_dimension=1, tiled=True)
        d_v_proj = lax.psum_scatter(d_v_part, 'cp', scatter_dimension=1, tiled=True)
        d_q_proj = rotate_back(d_q_rot, cos_t, sin_t)
        d_k_proj = rotate_back(d_k_rot, cos_t, sin_t)

        d_normed = (jnp.einsum('btnh,dnh->btd', d_q_proj, wq_full, preferred_element_type=jnp.float32)
                    + jnp.einsum('btnh,dnh->btd', d_k_proj, wk_full, preferred_element_type=jnp.float32)
                    + jnp.einsum('btnh,dnh->btd', d_v_proj, wv_full, preferred_element_type=jnp.float32)).astype(jnp.bfloat16)
        d_w_query = jnp.einsum('btd,btnh->dnh', normed, d_q_proj, preferred_element_type=jnp.float32)
        d_w_key = jnp.einsum('btd,btnh->dnh', normed, d_k_proj, preferred_element_type=jnp.float32)
        d_w_value = jnp.einsum('btd,btnh->dnh', normed, d_v_proj, preferred_element_type=jnp.float32)
        d_hidden, d_gain_pre = norm_backward(hidden, inv_pre, pre_full, d_normed)
        grad_hidden = (grad_out.astype(jnp.float32) + d_hidden).astype(jnp.bfloat16)
        return (out_hidden, grad_hidden, reduce_grad(d_w_query, 0), reduce_grad(d_w_key, 0),
                reduce_grad(d_w_value, 0), reduce_grad(d_w_out, 2), reduce_grad(d_gain_pre, 0),
                reduce_grad(d_gain_post, 0))

    return jax.shard_map(layer_local, mesh=mesh,
                         in_specs=(tok_spec, ids_spec, ids_spec, tok_spec, in_spec, in_spec, in_spec, out_spec, gain_spec, gain_spec),
                         out_specs=(tok_spec, tok_spec, in_spec, in_spec, in_spec, out_spec, gain_spec, gain_spec),
                         check_vma=False)
```

profile of v0, /device:TPU:1, one launch (start us, length us, event | category | flops | bytes accessed | tf_op | source)
XLA Modules:
  0.0 1942.8 jit_solution(6172802792153551494)
XLA Ops:
  8.7 1.6 copy.36
  11.6 1.3 fusion.141
  15.3 2.8 all_gather.32
  18.1 154.8 %all-reduce.7 = (bf16[2048]{0:T(1024)(128)(2,1)S(1)}, bf16[2048]{0:T(1024)(128)(2,1)S(1)}) all-reduce(bf16[2048]{0:T(1024)(128)(2,1)S(1)} %dynamic-update-slice, bf16[2048]{0:T(1024)(128)(2,1)S(1)} %dynamic-update-slice.1), channel_id=1, replica_groups=mesh['fsdp'=64,'cp'=2] {'fsdp'}, use_global_device_ids=true, to_apply=%add | all-reduce | flops 4096 | bytes 16384
  173.0 2.1 fusion.30
  176.7 1.2 fusion.63
  177.9 2.8 fusion.88
  180.7 1.2 fusion.114
  181.9 30.2 %all_gather.35 = bf16[1,1024,1,256]{1,3,2,0:T(8,128)(2,1)} all-gather(bf16[1,512,1,256]{1,3,2,0:T(8,128)(2,1)S(1)} %pad_maximum_fusion.10), channel_id=1, replica_groups=mesh['fsdp'=64,'cp'=2] {'cp'}, dimensions={1}, use_global_device_ids=true | all-gather | bytes 786432 | tf_op jit(solution)/shard_map/all_gather | solution.py:109
  212.1 2.0 fusion.82
  214.1 2.7 all-gather
  216.8 7.5 all-gather.10.cloned.1.call-done
  224.2 10.5 convert_bitcast_fusion.3
  235.8 4.6 fusion.6
  240.4 5.8 fusion.5
  246.3 7.7 fusion.64
  254.0 53.8 %all-gather.12.cloned.1.call-done = bf16[8,256,2048]{1,2,0:T(8,128)(2,1)} async-done(((bf16[8,256,32]{1,2,0:T(8,128)(2,1)}), bf16[8,256,2048]{1,2,0:T(8,128)(2,1)}) %all-gather.12.cloned.1.call-update) | async-done | bytes 8388624 | tf_op jit(solution)/shard_map/all_gather | solution.py:74
  307.8 8.8 fusion.25
  316.6 3.3 fusion.24
  320.0 8.8 convolution_convert_fusion
  328.8 1.3 copy-done.23
  330.2 7.8 fusion.78
  338.0 17.4 fusion.2
  355.5 13.9 fusion.7
  369.4 3.3 copy-done.3
  372.7 3.2 fusion.81
  376.0 3.2 convolution_bitcast_fusion
  379.3 7.6 reduce-scatter.7.cloned.1.call-done
  386.9 2.1 fusion.124
  389.0 2.4 convolution_bitcast_fusion.1
  391.9 13.6 fusion.50
  406.5 5.7 convert_bitcast_fusion.2
  414.2 8.4 fusion.53
  423.9 7.4 fusion.72
  432.5 3.2 fusion.37
  435.8 299.1 %all-reduce.4 = (f32[2048]{0:T(1024)S(1)}, f32[2048]{0:T(1024)S(1)}) all-reduce(f32[2048]{0:T(1024)S(1)} %get-tuple-element.26, f32[2048]{0:T(1024)S(1)} %get-tuple-element.24), channel_id=9, replica_groups=mesh['fsdp'=64,'cp'=2] {'fsdp'}, use_global_device_ids=true, to_apply=%region_18.19.clone | all-reduce | flops 4096 | bytes 32768
  736.0 313.8 %reduce-scatter.13.cloned.1.call-done = f32[32,1,256]{2,0,1:T(8,128)} async-done(((f32[2048,1,256]{2,0,1:T(8,128)}), f32[32,1,256]{2,0,1:T(8,128)}) %reduce-scatter.13.cloned.1.call-update) | async-done | bytes 32784 | tf_op jit(solution)/shard_map/reduce_scatter | solution.py:78
  1049.9 393.9 %reduce-scatter.17.cloned.1.call-done = f32[8,256,32]{1,2,0:T(8,128)} async-done(((f32[8,256,2048]{1,2,0:T(8,128)}), f32[8,256,32]{1,2,0:T(8,128)}) %reduce-scatter.17.cloned.1.call-update) | async-done | bytes 262160 | tf_op jit(solution)/shard_map/reduce_scatter | solution.py:78
  1443.7 387.4 %reduce-scatter.11.cloned.1.call-done = f32[32,8,256]{2,0,1:T(8,128)} async-done(((f32[2048,8,256]{2,0,1:T(8,128)}), f32[32,8,256]{2,0,1:T(8,128)}) %reduce-scatter.11.cloned.1.call-update) | async-done | bytes 262160 | tf_op jit(solution)/shard_map/reduce_scatter | solution.py:78
  1831.1 4.9 fusion.22
  1836.0 66.2 %all-reduce.11.cloned.1.call-done = (f32[32,1,256]{2,0,1:T(8,128)}, f32[32,1,256]{2,0,1:T(8,128)}, f32[32]{0:T(128)}, f32[32]{0:T(128)}) async-done(((f32[32,1,256]{2,0,1:T(8,128)}, f32[32,1,256]{2,0,1:T(8,128)}, f32[32]{0:T(128)}, f32[32]{0:T(128)}), (f32[32,1,256]{2,0,1:T(8,128)}, f32[32,1,256]{2,0,1:T(8,128)}, f32[32]{0:T(128)}, f32[32]{0:T(128)})) %all-reduce.11.cloned.1.call-update) | async-done | bytes 65808 | tf_op jit(solution)/shard_map/psum | solution.py:78
  1902.2 1.4 copy.52
  1903.6 1.4 copy.53
  1905.0 25.0 %all-reduce.13.cloned.1.call-done = (f32[32,8,256]{2,0,1:T(8,128)}, f32[8,256,32]{1,2,0:T(8,128)}) async-done(((f32[32,8,256]{2,0,1:T(8,128)}, f32[8,256,32]{1,2,0:T(8,128)}), (f32[32,8,256]{2,0,1:T(8,128)}, f32[8,256,32]{1,2,0:T(8,128)})) %all-reduce.13.cloned.1.call-update) | async-done | bytes 524304 | tf_op jit(solution)/shard_map/psum | solution.py:78
  1930.0 1.8 copy.51
  1931.8 1.7 copy.80
  1933.5 1.1 copy.81
  1934.6 1.1 copy.82
  (103 shorter events, 13.8 us)
Async XLA Ops:
  7.2 170.7 %all-gather.8.cloned.1.call-start = ((), (), s32[]{:S(2)}) async-start(), calls=%async_computation.7 | async-start | bytes 1064960 | tf_op jit(solution)/shard_map/all_gather | solution.py:74
  7.9 204.2 %all-gather.6.cloned.1.call-start = ((), (), s32[]{:S(2)}) async-start(), calls=%async_computation.6 | async-start | bytes 1064960 | tf_op jit(solution)/shard_map/all_gather | solution.py:74
  8.7 215.6 %all-gather.10.cloned.1.call-start = ((), (), s32[]{:S(2)}) async-start(), calls=%async_computation.8 | async-start | bytes 8519680 | tf_op jit(solution)/shard_map/all_gather | solution.py:74
  10.3 297.5 %all-gather.12.cloned.1.call-start = ((), (), s32[]{:S(2)}) async-start(), calls=%async_computation.9 | async-start | bytes 8519680 | tf_op jit(solution)/shard_map/all_gather | solution.py:74
  10.9 365.1 %reduce-scatter.9.cloned.1.call-start = ((), (), s32[]{:S(2)}) async-start(), calls=%async_computation.11 | async-start | bytes 786432 | tf_op jit(solution)/shard_map/reduce_scatter | solution.py:136
  175.0 37.1 %copy-start.1 = (bf16[1,512,2048]{2,1,0:T(8,128)(2,1)S(1)}, bf16[1,512,2048]{2,1,0:T(8,128)(2,1)}, u32[]{:S(2)}) copy-start(bf16[1,512,2048]{2,1,0:T(8,128)(2,1)} %param.10) | copy-start | bytes 6291460
  176.6 58.1 %copy-start.4 = (f32[512,128]{0,1:T(8,128)}, f32[512,128]{0,1:T(8,128)S(1)}, u32[]{:S(2)}) copy-start(f32[512,128]{0,1:T(8,128)S(1)} %get-tuple-element.47) | copy-start | bytes 786436
  176.6 58.1 %copy-start.6 = (f32[512,128]{0,1:T(8,128)}, f32[512,128]{0,1:T(8,128)S(1)}, u32[]{:S(2)}) copy-start(f32[512,128]{0,1:T(8,128)S(1)} %get-tuple-element.48) | copy-start | bytes 786436
  234.8 1.0 copy-start.18
  235.5 4.9 copy-start.11
  235.5 4.9 copy-start.13
  240.4 5.8 copy-start
  240.4 5.8 copy-start.20
  307.8 8.8 copy-start.2
  316.6 3.4 copy-start.8
  316.6 13.6 slice-start
  320.0 10.2 slice-start.1
  320.0 10.2 slice-start.2
  320.0 10.2 slice-start.3
  328.8 1.3 copy-start.23
  355.5 31.5 %reduce-scatter.7.cloned.1.call-start = ((), (), s32[]{:S(2)}) async-start(), calls=%async_computation.10 | async-start | bytes 786432 | tf_op jit(solution)/shard_map/reduce_scatter | solution.py:135
  355.5 17.2 copy-start.12
  355.5 17.2 copy-start.14
  369.4 3.3 copy-start.3
  375.9 360.1 %reduce-scatter.15.cloned.1.call-start = ((), (), s32[]{:S(2)}) async-start(), calls=%async_computation.14 | async-start | bytes 2129920 | tf_op jit(solution)/shard_map/reduce_scatter | solution.py:78
  379.3 670.5 %reduce-scatter.13.cloned.1.call-start = ((), (), s32[]{:S(2)}) async-start(), calls=%async_computation.13 | async-start | bytes 2129920 | tf_op jit(solution)/shard_map/reduce_scatter | solution.py:78
  391.4 1052.3 %reduce-scatter.17.cloned.1.call-start = ((), (), s32[]{:S(2)}) async-start(), calls=%async_computation.15 | async-start | bytes 17039360 | tf_op jit(solution)/shard_map/reduce_scatter | solution.py:78
  405.5 1.0 copy-start.19
  405.5 6.7 copy-start.5
  405.5 6.7 copy-start.7
  405.5 1425.6 %reduce-scatter.11.cloned.1.call-start = ((), (), s32[]{:S(2)}) async-start(), calls=%async_computation.12 | async-start | bytes 17039360 | tf_op jit(solution)/shard_map/reduce_scatter | solution.py:78
  412.9 1.0 copy-start.15
  412.9 1.3 copy-start.17
  422.6 1.2 copy-start.16
  422.7 1479.6 %all-reduce.11.cloned.1.call-start = ((), (), s32[]{:S(2)}) async-start(), calls=%async_computation.16 | async-start | bytes 133120 | tf_op jit(solution)/shard_map/psum | solution.py:78
  423.9 7.4 copy-start.10
  431.3 1.2 copy-start.9
  431.3 1.3 copy-start.21
  432.5 1398.6 %copy-start.22 = (f32[512]{0:T(512)S(1)}, f32[512]{0:T(512)}, u32[]{:S(2)}) copy-start(f32[512]{0:T(512)} %get-tuple-element.49) | copy-start | bytes 6148
  1049.8 880.2 %all-reduce.13.cloned.1.call-start = ((), (), s32[]{:S(2)}) async-start(), calls=%async_computation.17 | async-start | bytes 1048576 | tf_op jit(solution)/shard_map/psum | solution.py:78
Sparse Core Ops, SparseCore 0:
  10.8 65.4 all-gather.7
  79.2 61.3 all-gather.5
  144.1 80.0 all-gather.9
  227.0 80.7 all-gather.11
  355.6 10.8 reduce-scatter.8
  376.0 10.8 reduce-scatter.6
  389.3 306.8 reduce-scatter.14
  698.5 351.1 reduce-scatter.12
  1052.2 391.4 reduce-scatter.16
  1446.0 385.0 reduce-scatter.10
  1834.3 67.8 all-reduce.10
  1904.6 25.3 all-reduce.12
where the time goes:
time: 1950 us; the launch traced here: 1940 us
  waiting for transfers between devices  1260 us (65%)
  blocking collectives  490 us (25%)
  matrix products  118 us (6%)
  other arithmetic  38.1 us (2%)
  local copies, waits for them, and re-layouts  22.3 us (1%)
    reduce_scatter x4, waiting for transfers between devices, reduce_grad(): lax.psum_scatter(full, 'fsdp', scatter_dimension=axis_pos, tiled=True)  1090 us
    unnamed x2, blocking collectives  454 us
    psum x2, waiting for transfers between devices, reduce_grad(): lax.psum(lax.psum_scatter(full, 'fsdp', scatter_dimension=axis_pos, tiled...  91.2 us
    all_gather x4, waiting for transfers between devices, gather_rows(): return lax.all_gather(shard, 'fsdp', axis=axis_pos, tiled=True)  61.3 us
  transfers between devices with their start and end apart: 12, of which 8 were waited for; matrix products, arithmetic and copies ran while one was open for 6% of the time, Pallas kernels for 0%

commit v1 on v0

v1 whole, which is shorter than its diff:
```python
import functools

import jax
import jax.numpy as jnp
from jax import lax
from jax.experimental import pallas as pl
from jax.experimental.pallas import tpu as pltpu
from jax.sharding import PartitionSpec as P

SOFT_CAP = 50.0
NORM_EPS = 1e-6
ROPE_BASE = 10000.0
MESH = pl.DeviceIdType.MESH
SIDE = 4
VMEM_MAX = 67_043_328

STREAMS = ((0, 0, 0, 512), (0, 1, 512, 384), (0, 2, 896, 384),
           (1, 0, 0, 256), (1, 1, 256, 384), (1, 2, 640, 384))


def place():
    f = lax.axis_index('fsdp')
    return (f // 16, lax.rem(f // 4, 4), lax.rem(f, 4)), lax.axis_index('cp')


def shifted(coords, dim, delta):
    out = list(coords)
    out[dim] = lax.rem(coords[dim] + delta + SIDE, SIDE)
    return tuple(out)


def device(coords, core):
    return (coords[0] * 16 + coords[1] * 4 + coords[2], core)


def greet(coords, core):
    barrier = pltpu.get_barrier_semaphore()
    for dim in range(3):
        for delta in (1, -1):
            pl.semaphore_signal(barrier, inc=1, device_id=device(shifted(coords, dim, delta), core), device_id_type=MESH)
    pl.semaphore_signal(barrier, inc=1, device_id=device(coords, 1 - core), device_id_type=MESH)
    pl.semaphore_wait(barrier, 7)


def order_of(colour):
    return tuple((colour + i) % 3 for i in range(3))


def region(ref, full, coords, rows, cols):
    idx = [pl.ds(0, SIDE) if d in full else coords[d] for d in range(3)]
    return ref.at[idx[0], idx[1], idx[2], pl.ds(*rows), pl.ds(*cols)]


def gather_kernel(in0, in1, out0, out1, send, recv, sib_send, sib_recv, own_sem):
    coords, core = place()
    greet(coords, core)
    ins, outs = (in0, in1), (out0, out1)
    owns = []
    for g in range(2):
        copy = pltpu.make_async_copy(ins[g], outs[g].at[coords[0], coords[1], coords[2]], own_sem.at[g])
        copy.start()
        owns.append(copy)
    whole, low, high = (0, 32), (0, 16), (16, 16)
    sent, given = [], []

    def cols_of(s, side):
        g, _, off, width = STREAMS[s]
        half = outs[g].shape[-1] // 2
        return (pl.multiple_of(side * half + off, 128), width)

    def send_to(s, p, kind, src, rows, at, to):
        g, colour, _, _ = STREAMS[s]
        full = order_of(colour)[:p]
        cols = cols_of(s, core)
        dst = region(outs[g], full, at, rows, cols)
        copy = pltpu.make_async_remote_copy(
            src if src is not None else dst, dst, send.at[s, p, kind], recv.at[s, p, kind],
            device_id=device(to, core), device_id_type=MESH)
        copy.start()
        sent.append(copy)

    def arrived(s, p, kind):
        g, colour, _, _ = STREAMS[s]
        order = order_of(colour)
        at = shifted(coords, order[p], (-1, 1, -2, 2)[kind])
        rows = (whole, whole, low, high)[kind]
        here = region(outs[g], order[:p], at, rows, cols_of(s, core))
        pltpu.make_async_remote_copy(here, here, send.at[s, p, kind], recv.at[s, p, kind],
                                     device_id=device(coords, 1 - core), device_id_type=MESH).wait_recv()
        copy = pltpu.make_async_remote_copy(here, here, sib_send.at[s, p, kind], sib_recv.at[s, p, kind],
                                            device_id=device(coords, 1 - core), device_id_type=MESH)
        copy.start()
        there = region(outs[g], order[:p], at, rows, cols_of(s, 1 - core))
        given.append((copy, pltpu.make_async_remote_copy(
            there, there, sib_send.at[s, p, kind], sib_recv.at[s, p, kind],
            device_id=device(coords, 1 - core), device_id_type=MESH)))
        return at

    for p in range(3):
        for s, (g, colour, _, _) in enumerate(STREAMS):
            dim = order_of(colour)[p]
            if p > 0:
                arrived(s, p - 1, 2)
                arrived(s, p - 1, 3)
                if s in (0, 3) and p == 1:
                    owns[g].wait()
            src = ins[g].at[:, pl.ds(*cols_of(s, core))] if p == 0 else None
            send_to(s, p, 0, src, whole, coords, shifted(coords, dim, 1))
            send_to(s, p, 1, src, whole, coords, shifted(coords, dim, -1))
        for s, (g, colour, _, _) in enumerate(STREAMS):
            dim = order_of(colour)[p]
            send_to(s, p, 2, None, low, arrived(s, p, 0), shifted(coords, dim, 1))
            send_to(s, p, 3, None, high, arrived(s, p, 1), shifted(coords, dim, -1))
    for s in range(len(STREAMS)):
        arrived(s, 2, 2)
        arrived(s, 2, 3)
    for copy in sent:
        copy.wait_send()
    for out_copy, in_copy in given:
        out_copy.wait_send()
        in_copy.wait_recv()


def gather_weights(w0, w1):
    ns = len(STREAMS)
    shapes = [jax.ShapeDtypeStruct((SIDE, SIDE, SIDE, 32, w.shape[1]), w.dtype) for w in (w0, w1)]
    dma = pltpu.SemaphoreType.DMA
    return pl.pallas_call(
        gather_kernel, name="gather_weights",
        out_shape=shapes,
        in_specs=[pl.BlockSpec(memory_space=pltpu.VMEM)] * 2,
        out_specs=[pl.BlockSpec(memory_space=pl.ANY)] * 2,
        scratch_shapes=[dma((ns, 3, 4))] * 4 + [dma((2,))],
        compiler_params=pltpu.CompilerParams(collective_id=1, has_side_effects=True),
    )(w0, w1)


def scatter_kernel(own0, own1, own_g, sib0, sib1, sib_g, out0, out1, out_g, *scratch):
    ns = len(STREAMS) + 1
    scratch = list(scratch)
    sib_bufs = scratch[:3]
    acc = [[scratch[3 + s * 3 + q] for q in range(3)] for s in range(ns)]
    base = 3 + ns * 3
    sbuf = [[scratch[base + s * 3 + q] for q in range(3)] for s in range(ns)]
    base += ns * 3
    rbuf = [[scratch[base + s * 3 + q] for q in range(3)] for s in range(ns)]
    base += ns * 3
    send, recv, sib_send, sib_recv, fin_send, fin_recv = scratch[base:]
    coords, core = place()
    sibling = device(coords, 1 - core)
    greet(coords, core)
    owns, sibs, outs = (own0, own1, own_g), (sib0, sib1, sib_g), (out0, out1, out_g)
    gifts = []
    for g in range(3):
        copy = pltpu.make_async_remote_copy(sibs[g], sib_bufs[g], sib_send.at[g], sib_recv.at[g],
                                            device_id=sibling, device_id_type=MESH)
        copy.start()
        gifts.append(copy)
    streams = [(2, 0, 0, 128)] + list(STREAMS)
    sent = []

    def lead(order, q, at, n):
        full = order[:2 - q]
        idx = list(at)
        digits = (n // SIDE, lax.rem(n, SIDE)) if len(full) == 2 else (n,)
        for d, digit in zip(sorted(full), digits):
            idx[d] = digit
        return tuple(idx)

    def value(s, q, at, n, r0, nr):
        g, colour, off, width = streams[s]
        order = order_of(colour)
        idx = lead(order, q, at, n)
        if q == 0:
            where = idx + (pl.ds(r0, nr), pl.ds(off, width))
            return owns[g][where] + sib_bufs[g][where].astype(jnp.float32)
        kept = sorted(order[:3 - q])
        m = 0
        for d in kept:
            m = m * SIDE + idx[d]
        return acc[s][q - 1][m, pl.ds(r0, nr), :]

    def step_one(s, q):
        g, colour, _, width = streams[s]
        order = order_of(colour)
        dim = order[2 - q]
        half = rows_of(g) // 2
        n_blocks = SIDE ** (2 - q)
        far, right, left = shifted(coords, dim, 2), shifted(coords, dim, 1), shifted(coords, dim, -1)
        dt = sbuf[s][q].dtype

        def body(n, carry):
            sbuf[s][q][0, n] = value(s, q, far, n, 0, half).astype(dt)
            sbuf[s][q][1, n] = value(s, q, right, n, half, half).astype(dt)
            sbuf[s][q][2, n] = value(s, q, far, n, half, half).astype(dt)
            sbuf[s][q][3, n] = value(s, q, left, n, 0, half).astype(dt)
            return carry
        lax.fori_loop(0, n_blocks, body, 0)
        go(s, q, 0, (0, 2), right)
        go(s, q, 1, (2, 2), left)

    def go(s, q, kind, part, to):
        copy = pltpu.make_async_remote_copy(
            sbuf[s][q].at[pl.ds(*part)], rbuf[s][q].at[pl.ds(*part)], send.at[s, q, kind], recv.at[s, q, kind],
            device_id=device(to, core), device_id_type=MESH)
        copy.start()
        sent.append(copy)

    def got(s, q, kind, part):
        here = rbuf[s][q].at[pl.ds(*part)]
        pltpu.make_async_remote_copy(here, here, send.at[s, q, kind], recv.at[s, q, kind],
                                     device_id=sibling, device_id_type=MESH).wait_recv()

    def step_two(s, q):
        g, colour, _, width = streams[s]
        dim = order_of(colour)[2 - q]
        half = rows_of(g) // 2
        n_blocks = SIDE ** (2 - q)
        right, left = shifted(coords, dim, 1), shifted(coords, dim, -1)
        dt = sbuf[s][q].dtype
        got(s, q, 0, (0, 2))

        def to_right(n, carry):
            sbuf[s][q][4, n] = (value(s, q, right, n, 0, half) + rbuf[s][q][0, n].astype(jnp.float32)).astype(dt)
            return carry
        lax.fori_loop(0, n_blocks, to_right, 0)
        go(s, q, 2, (4, 1), right)
        got(s, q, 1, (2, 2))

        def to_left(n, carry):
            sbuf[s][q][5, n] = (value(s, q, left, n, half, half) + rbuf[s][q][2, n].astype(jnp.float32)).astype(dt)
            return carry
        lax.fori_loop(0, n_blocks, to_left, 0)
        go(s, q, 3, (5, 1), left)

    def step_three(s, q):
        g, colour, _, width = streams[s]
        half = rows_of(g) // 2
        n_blocks = SIDE ** (2 - q)
        got(s, q, 2, (4, 1))
        got(s, q, 3, (5, 1))

        def body(n, carry):
            def low(i):
                return rbuf[s][q][i, n].astype(jnp.float32)
            acc[s][q][n, pl.ds(0, half), :] = value(s, q, coords, n, 0, half) + low(3) + low(4)
            acc[s][q][n, pl.ds(half, half), :] = value(s, q, coords, n, half, half) + low(1) + low(5)
            return carry
        lax.fori_loop(0, n_blocks, body, 0)

    def rows_of(g):
        return owns[g].shape[3]

    for g in (2, 0, 1):
        gifts[g].wait_recv()
        for s in range(ns):
            if streams[s][0] == g:
                step_one(s, 0)
    for q in range(3):
        for s in range(ns):
            step_two(s, q)
        for s in range(ns):
            step_three(s, q)
            if q < 2:
                step_one(s, q + 1)
    fins = []
    for s in range(ns):
        g, _, off, width = streams[s]
        here = outs[g].at[core, :, pl.ds(off, width)]
        outs[g][core, :, pl.ds(off, width)] = acc[s][2][0]
        copy = pltpu.make_async_remote_copy(acc[s][2].at[0], here, fin_send.at[s], fin_recv.at[s],
                                            device_id=sibling, device_id_type=MESH)
        copy.start()
        fins.append((copy, s))
    for copy, s in fins:
        g, _, off, width = streams[s]
        there = outs[g].at[1 - core, :, pl.ds(off, width)]
        copy.wait_send()
        pltpu.make_async_remote_copy(there, there, fin_send.at[s], fin_recv.at[s],
                                     device_id=sibling, device_id_type=MESH).wait_recv()
    for copy in sent + gifts:
        copy.wait_send()


def scatter_grads(own0, own1, own_g, sib0, sib1, sib_g):
    owns, sibs = (own0, own1, own_g), (sib0, sib1, sib_g)
    streams = [(2, 0, 0, 128)] + list(STREAMS)
    ns = len(streams)
    dma = pltpu.SemaphoreType.DMA
    scratch = [pltpu.VMEM(a.shape, a.dtype) for a in sibs]
    for kind in range(3):
        for g, _, _, width in streams:
            rows = owns[g].shape[3]
            dt = sibs[g].dtype
            for q in range(3):
                n = SIDE ** (2 - q)
                scratch.append(pltpu.VMEM((n, rows, width), jnp.float32) if kind == 0
                               else pltpu.VMEM((6, n, rows // 2, width), dt))
    scratch += [dma((ns, 3, 4))] * 2 + [dma((3,))] * 2 + [dma((ns,))] * 2
    return pl.pallas_call(
        scatter_kernel, name="scatter_grads",
        out_shape=[jax.ShapeDtypeStruct((2,) + a.shape[3:], jnp.float32) for a in owns],
        in_specs=[pl.BlockSpec(memory_space=pltpu.VMEM)] * 3 + [pl.BlockSpec(memory_space=pl.ANY)] * 2
        + [pl.BlockSpec(memory_space=pltpu.VMEM)],
        out_specs=[pl.BlockSpec(memory_space=pltpu.VMEM)] * 3,
        scratch_shapes=scratch,
        compiler_params=pltpu.CompilerParams(collective_id=2, has_side_effects=True, vmem_limit_bytes=VMEM_MAX),
    )(own0, own1, own_g, sib0, sib1, sib_g)


def rope_tables(pos_ids, head_dim):
    half_dim = head_dim // 2
    inv_freq = ROPE_BASE ** (-2.0 * jnp.arange(half_dim, dtype=jnp.float32) / head_dim)
    angles = pos_ids.astype(jnp.float32)[..., None] * inv_freq
    return jnp.cos(angles)[..., None, :], jnp.sin(angles)[..., None, :]


def rotate(values, cos_t, sin_t):
    half_dim = values.shape[-1] // 2
    first_half = values[..., :half_dim].astype(jnp.float32)
    second_half = values[..., half_dim:].astype(jnp.float32)
    rotated = jnp.concatenate([first_half * cos_t - second_half * sin_t,
                               second_half * cos_t + first_half * sin_t], axis=-1)
    return rotated.astype(jnp.bfloat16)


def norm_forward(values, gain_vec):
    values_f = values.astype(jnp.float32)
    inv_rms = lax.rsqrt(jnp.mean(values_f * values_f, axis=-1, keepdims=True) + NORM_EPS)
    normed = values_f * inv_rms * (1.0 + gain_vec.astype(jnp.float32))
    return normed.astype(jnp.bfloat16), inv_rms


def norm_backward(values, inv_rms, gain_vec, grads):
    values_f = values.astype(jnp.float32)
    grads_f = grads.astype(jnp.float32)
    scaled = grads_f * (1.0 + gain_vec.astype(jnp.float32))
    d_values = inv_rms * scaled - values_f * inv_rms ** 3 * jnp.mean(scaled * values_f, axis=-1, keepdims=True)
    d_gain = jnp.sum(grads_f * values_f * inv_rms, axis=0)
    return d_values, d_gain


def dot(a, b, dims):
    return lax.dot_general(a, b, ((dims[:1], dims[1:]), ((), ())), preferred_element_type=jnp.float32)


def solution(mesh):
    tok_spec = P('fsdp', 'cp', None)
    ids_spec = P('fsdp', 'cp')
    in_spec = P('fsdp', None, None)
    out_spec = P(None, None, 'fsdp')
    gain_spec = P('fsdp')
    bf, f32 = jnp.bfloat16, jnp.float32

    def layer_local(hidden, doc_ids, doc_pos, grad_out, w_query, w_key, w_value, w_out, gain_pre, gain_post):
        _, n_tok, model_dim = hidden.shape
        hidden, grad_out = hidden[0], grad_out[0]
        n_heads, head_dim = w_query.shape[1], w_query.shape[2]
        rows = w_query.shape[0]
        q_cols = n_heads * head_dim
        core = lax.axis_index('cp')
        w0 = jnp.concatenate([w_query.reshape(rows, q_cols), w_key.reshape(rows, head_dim),
                              w_value.reshape(rows, head_dim)], axis=1)
        w1 = w_out.reshape(q_cols, rows).T
        gains = lax.all_gather(jnp.stack([gain_pre, gain_post]), 'fsdp', axis=1, tiled=True)
        pre_full, post_full = gains[0], gains[1]
        wqkv, wo_t = gather_weights(w0, w1)
        wqkv = wqkv.reshape(model_dim, q_cols + 2 * head_dim)
        wo_t = wo_t.reshape(model_dim, q_cols)
        q_scale = (head_dim if head_dim >= 256 else model_dim // n_heads) ** -0.5

        normed, inv_pre = norm_forward(hidden, pre_full)
        qkv = dot(normed, wqkv, (1, 0)).astype(bf)
        q_proj = qkv[:, :q_cols].reshape(n_tok, n_heads, head_dim)
        k_proj = qkv[:, q_cols:q_cols + head_dim].reshape(n_tok, 1, head_dim)
        v_proj = qkv[:, q_cols + head_dim:]
        cos_t, sin_t = rope_tables(doc_pos[0], head_dim)
        q_rot = rotate(q_proj, cos_t, sin_t)
        k_rot = rotate(k_proj, cos_t, sin_t)[:, 0]

        k_all = lax.all_gather(k_rot, 'cp', axis=0, tiled=True)
        v_all = lax.all_gather(v_proj, 'cp', axis=0, tiled=True)
        ids_all = lax.all_gather(doc_ids, 'cp', axis=1, tiled=True)
        q_index = core * n_tok + jnp.arange(n_tok)
        k_index = jnp.arange(k_all.shape[0])
        visible = (doc_ids[0][:, None] == ids_all[0][None, :]) & (k_index[None, :] <= q_index[:, None])
        scores = jnp.einsum('qhd,td->hqt', q_rot, k_all, preferred_element_type=f32) * q_scale
        tanh_s = jnp.tanh(scores / SOFT_CAP)
        capped = jnp.where(visible, SOFT_CAP * tanh_s, -1e30)
        row_peak = jnp.max(capped, axis=-1, keepdims=True)
        weights = jnp.exp(capped - row_peak)
        attn_prob = weights / jnp.sum(weights, axis=-1, keepdims=True)
        prob_low = attn_prob.astype(bf)
        attn_out = jnp.einsum('hqt,td->qhd', prob_low, v_all, preferred_element_type=f32).astype(bf)
        attn_flat = attn_out.reshape(n_tok, q_cols)
        proj_out = dot(attn_flat, wo_t, (1, 1)).astype(bf)
        post_out, inv_post = norm_forward(proj_out, post_full)
        out_hidden = (hidden.astype(f32) + post_out.astype(f32)).astype(bf)

        d_proj, d_gain_post = norm_backward(proj_out, inv_post, post_full, grad_out)
        d_proj = d_proj.astype(bf)
        d_attn = dot(d_proj, wo_t, (1, 0)).astype(bf).reshape(n_tok, n_heads, head_dim)

        def halves(grads, acts):
            width = acts.shape[1] // 2
            own = dot(grads, lax.dynamic_slice_in_dim(acts, core * width, width, 1), (0, 0))
            other = dot(grads, lax.dynamic_slice_in_dim(acts, (1 - core) * width, width, 1), (0, 0)).astype(bf)
            shape = (SIDE, SIDE, SIDE, rows, width)
            return own.reshape(shape), other.reshape(shape)

        own1, sib1 = halves(d_proj, attn_flat)

        d_prob = jnp.einsum('qhd,td->hqt', d_attn, v_all, preferred_element_type=f32)
        row_dot = jnp.sum(attn_prob * d_prob, axis=-1, keepdims=True)
        d_score = (attn_prob * (d_prob - row_dot) * (1.0 - tanh_s * tanh_s) * q_scale).astype(bf)
        d_q_rot = jnp.einsum('hqt,td->qhd', d_score, k_all, preferred_element_type=f32).astype(bf)
        d_k_part = jnp.einsum('hqt,qhd->td', d_score, q_rot, preferred_element_type=f32).astype(bf)
        d_v_part = jnp.einsum('hqt,qhd->td', prob_low, d_attn, preferred_element_type=f32).astype(bf)
        d_k_rot = lax.psum_scatter(d_k_part, 'cp', scatter_dimension=0, tiled=True)
        d_v_proj = lax.psum_scatter(d_v_part, 'cp', scatter_dimension=0, tiled=True)
        d_q_proj = rotate(d_q_rot, cos_t, -sin_t)
        d_k_proj = rotate(d_k_rot[:, None], cos_t, -sin_t)[:, 0]
        d_qkv = jnp.concatenate([d_q_proj.reshape(n_tok, q_cols), d_k_proj, d_v_proj], axis=1)

        d_normed = dot(d_qkv, wqkv, (1, 1)).astype(bf)
        own0, sib0 = halves(normed, d_qkv)
        d_hidden, d_gain_pre = norm_backward(hidden, inv_pre, pre_full, d_normed)
        grad_hidden = (grad_out.astype(f32) + d_hidden).astype(bf)
        d_gains = jnp.stack([d_gain_pre, d_gain_post]).reshape(2, SIDE, SIDE, SIDE, 1, rows)
        d_gains = jnp.pad(d_gains, ((0, 0), (0, 0), (0, 0), (0, 0), (0, 15), (0, 128 - rows)))
        own_g = lax.dynamic_index_in_dim(d_gains, core, 0, keepdims=False)
        sib_g = lax.dynamic_index_in_dim(d_gains, 1 - core, 0, keepdims=False)
        g0, g1, gg = scatter_grads(own0, own1, own_g, sib0, sib1, sib_g)
        g0 = jnp.concatenate([g0[0], g0[1]], axis=1)
        g1 = jnp.concatenate([g1[0], g1[1]], axis=1)
        return (out_hidden[None], grad_hidden[None], g0[:, :q_cols].reshape(rows, n_heads, head_dim),
                g0[:, q_cols:q_cols + head_dim].reshape(rows, 1, head_dim),
                g0[:, q_cols + head_dim:].reshape(rows, 1, head_dim),
                g1.T.reshape(n_heads, head_dim, rows), gg[0, 0, :rows], gg[1, 0, :rows])

    return jax.shard_map(layer_local, mesh=mesh,
                         in_specs=(tok_spec, ids_spec, ids_spec, tok_spec, in_spec, in_spec, in_spec, out_spec, gain_spec, gain_spec),
                         out_specs=(tok_spec, tok_spec, in_spec, in_spec, in_spec, out_spec, gain_spec, gain_spec),
                         check_vma=False)
```

time: 1950 us -> 555 us (0.28)
  waiting for transfers between devices: 1260 us -> 0.06 us
  blocking collectives: 490 us -> 157 us
  Pallas kernels: 0 us -> 152 us
  matrix products: 118 us -> 166 us
    reduce_scatter x6 -> x2, waiting for transfers between devices: 1100 us -> 0.02 us  [the longest x1 0.02 us: layer_local(): d_v_proj = lax.psum_scatter(d_v_part, 'cp', scatter_dimension=0, tiled=True)]
    unnamed x2 -> x0, blocking collectives: 454 us -> none
    pallas_call x0 -> x2, Pallas kernels: none -> 152 us  [the longest x1 76.7 us: scatter_grads(): pl.pallas_call(scatter_kernel, name='scatter_grads', out_shape=[jax.Shape...]
    all_gather x2 -> x3, blocking collectives: 32.9 us -> 155 us  [the longest x1 151 us: layer_local(): lax.all_gather(jnp.stack([gain_pre, gain_post]), 'fsdp', axis=1, tiled=True)]
    psum x2 -> x0, waiting for transfers between devices: 91.2 us -> none  [reduce_grad(): lax.psum(lax.psum_scatter(full, 'fsdp', scatter_dimension=axis_pos, tiled...]
    all_gather x4 -> x0, waiting for transfers between devices: 61.3 us -> none  [gather_rows(): return lax.all_gather(shard, 'fsdp', axis=axis_pos, tiled=True)]
    dot_general x18 -> x14, matrix products: 118 us -> 155 us  [the longest x8 63.2 us: dot(): lax.dot_general(a, b, ((dims[:1], dims[1:]), ((), ())), preferred_element...]
  transfers between devices with their start and end apart: 12 -> 2, of which waited for: 8 -> 0; matrix products, arithmetic and copies ran while one was open for 6% -> 13% of each run, Pallas kernels for 0% -> 0%
where the time goes in v1:
time: 555 us; the launch traced here: 547 us
  matrix products  166 us (30%)
  blocking collectives  157 us (28%)
  Pallas kernels  152 us (27%)
  other arithmetic  30.2 us (5%)
  local copies, waits for them, and re-layouts  25.9 us (5%)
  between operations  15 us (3%)
    all_gather x1, blocking collectives, layer_local(): lax.all_gather(jnp.stack([gain_pre, gain_post]), 'fsdp', axis=1, tiled=True)  151 us
    pallas_call x1, Pallas kernels, scatter_grads(): pl.pallas_call(scatter_kernel, name='scatter_grads', out_shape=[jax.Shape...  76.7 us
    pallas_call x1, Pallas kernels, gather_weights(): pl.pallas_call(gather_kernel, name='gather_weights', out_shape=shapes, in...  75.2 us
    dot_general x8, matrix products, dot(): lax.dot_general(a, b, ((dims[:1], dims[1:]), ((), ())), preferred_element...  63.2 us
    dot_general x1, matrix products, layer_local(): jnp.einsum('hqt,td->qhd', d_score, k_all, preferred_element_type=f32)  29.2 us
    dot_general x1, matrix products, layer_local(): jnp.einsum('hqt,qhd->td', d_score, q_rot, preferred_element_type=f32)  28.5 us
    sub x1, matrix products, layer_local(): weights = jnp.exp(capped - row_peak)  11.5 us
  transfers between devices with their start and end apart: 2, of which 0 were waited for; matrix products, arithmetic and copies ran while one was open for 13% of the time, Pallas kernels for 0%

profile of v1, /device:TPU:1, one launch (start us, length us, event | category | flops | bytes accessed | tf_op | source)
XLA Modules:
  0.0 546.5 jit_solution(15106080517122260719)
XLA Ops:
  7.2 0.9 copy.79
  8.2 1.6 copy.78
  9.7 0.7 maximum_bitcast_fusion
  10.4 151.0 %all-gather = bf16[64,32,2]{1,2,0:T(2,128)(2,1)S(1)} all-gather(bf16[1,32,2]{1,2,0:T(2,128)(2,1)S(1)} %maximum_bitcast_fusion), channel_id=1, replica_groups=mesh['fsdp'=64,'cp'=2] {'fsdp'}, dimensions={0}, use_global_device_ids=true | all-gather | bytes 8320 | tf_op jit(solution)/shard_map/all_gather | solution.py:365
  161.6 2.1 fusion.24
  164.2 1.4 pad_maximum_fusion.14.in0
  165.6 75.2 %gather_weights.1 = (bf16[4,4,4,32,2560]{4,3,2,1,0:T(8,128)(2,1)}, bf16[4,4,4,32,2048]{4,3,2,1,0:T(8,128)(2,1)}) custom-call(bf16[32,2560]{1,0:T(8,128)(2,1)} %pad_maximum_fusion.14.in0, bf16[32,2048]{1,0:T(8,128)(2,1)} %bitcast.243), custom_call_target="tpu_custom_call" | custom-call | tf_op jit(solution)/shard_map/gather_weights/pallas_call | solution.py:128
  240.8 9.1 %convolution_convert_fusion.1 = bf16[512,2560]{1,0:T(8,128)(2,1)S(1)} fusion(bf16[2048,2560]{1,0:T(8,128)(2,1)} %bitcast.266, bf16[1,512,2048]{2,1,0:T(8,128)(2,1)} %param.10, f32[2048]{0:T(1024)S(1)} %bitcast.250, f32[512]{0:T(512)S(1)} %get-tuple-element.76), kind=kOutput, calls=%fused_computation.39 | convolution fusion | flops 5374214144 | bytes 15214592 | tf_op jit(solution)/shard_map/dot_general | solution.py:344
  250.2 2.1 all_gather.13
  252.3 1.8 all_gather.14
  255.0 1.8 fusion.118
  256.8 1.2 fusion.115
  258.0 2.2 all_gather.15
  260.2 1.3 fusion.63
  261.5 0.7 fusion.47
  262.2 8.1 %fusion.75 = f32[1024,512,8]{1,0,2:T(8,128)} fusion(bf16[512,8,128]{2,0,1:T(8,128)(2,1)S(1)} %get-tuple-element.51, bf16[512,8,128]{2,0,1:T(8,128)(2,1)S(1)} %get-tuple-element.50, bf16[1024,256]{1,0:T(8,128)(2,1)S(1)} %all_gather.15), kind=kOutput, calls=%fused_computation.104 | convolution fusion | flops 2151677952 | bytes 19398656 | tf_op jit(solution)/shard_map/qhd,td->hqt/dot_general | solution.py:387
  270.4 11.5 %fusion.144 = (f32[8,512]{1,0:T(8,128)S(1)}, f32[8,512,1024]{1,2,0:T(8,128)}) fusion(pred[512,1024]{0,1:T(8,128)(4,1)S(1)} %copy-done.16, bf16[512,8,128]{2,0,1:T(8,128)(2,1)S(1)} %get-tuple-element.51, bf16[512,8,128]{2,0,1:T(8,128)(2,1)S(1)} %get-tuple-element.50, bf16[1024,256]{1,0:T(8,128)(2,1)} %copy-done.10), kind=kOutput, calls=%fused_computation.197 | convolution fusion | flops 2172650496 | bytes 19939328 | tf_op jit(solution)/shard_map/sub | solution.py:391
  281.8 8.2 %fusion.64 = bf16[256,8,512]{2,0,1:T(8,128)(2,1)S(1)} fusion(bf16[1024,256]{1,0:T(8,128)(2,1)S(1)} %copy-done.8, f32[8,512,1024]{1,2,0:T(8,128)} %get-tuple-element.80, f32[8,512]{1,0:T(8,128)S(1)} %get-tuple-element.79), kind=kOutput, calls=%fused_computation.99 | convolution fusion | flops 2156920832 | bytes 19415040 | tf_op jit(solution)/shard_map/hqt,td->qhd/dot_general | solution.py:394
  290.1 9.3 %fusion.35 = (f32[512]{0:T(512)S(1)}, bf16[512,2048]{1,0:T(8,128)(2,1)S(1)}) fusion(bf16[512,2048]{0,1:T(8,128)(2,1)S(1)} %bitcast.272, bf16[2048,2048]{1,0:T(8,128)(2,1)} %bitcast.268), kind=kOutput, calls=%fused_computation.54 | convolution fusion | flops 4299161088 | bytes 12584960 | tf_op jit(solution)/shard_map/dot_general | solution.py:344
  299.4 3.6 fusion.41
  303.0 8.9 %convolution_convert_fusion.3 = bf16[512,2048]{1,0:T(8,128)(2,1)S(1)} fusion(bf16[2048,2048]{1,0:T(8,128)(2,1)} %bitcast.269, bf16[512,2048]{1,0:T(8,128)(2,1)S(1)} %get-tuple-element.82, bf16[1,512,2048]{2,1,0:T(8,128)(2,1)S(1)} %copy-done.2, f32[512]{0:T(512)S(1)} %broadcast_multiply_fusion.1, f32[512]{0:T(512)S(1)} %get-tuple-element.77, ...), kind=kOutput, calls=%fused_computation.66 | convolution fusion | flops 4304404480 | bytes 14694400 | tf_op jit(solution)/shard_map/dot_general | solution.py:344
  311.9 1.3 copy-done.4
  313.2 8.1 %fusion.59 = f32[1024,512,8]{1,0,2:T(8,128)} fusion(bf16[64,8,8,256]{3,2,1,0:T(8,128)(2,1)S(1)} %bitcast.237, bf16[1024,256]{1,0:T(8,128)(2,1)S(1)} %copy-done.9), kind=kOutput, calls=%fused_computation.90 | convolution fusion | flops 2147483648 | bytes 19398656 | tf_op jit(solution)/shard_map/qhd,td->hqt/dot_general | solution.py:413
  321.3 28.5 %fusion.85 = bf16[1024,256]{1,0:T(8,128)(2,1)} fusion(bf16[512,8,128]{2,0,1:T(8,128)(2,1)} %copy-done.5, bf16[512,8,128]{2,0,1:T(8,128)(2,1)S(1)} %get-tuple-element.50, f32[1024,512,8]{1,0,2:T(8,128)} %fusion.59, f32[1024,512,8]{1,0,2:T(8,128)} %fusion.75, f32[8,512,1024]{1,2,0:T(8,128)} %get-tuple-element.80, f32[8,512]{1,0:T(8,128)S(1)} %get-tuple-element.79), kind=kOutput, calls=%fused_computation.110 | convolution fusion | flops 2198082560 | bytes 52969472 | tf_op jit(solution)/shard_map/hqt,qhd->td/dot_general | solution.py:417
  349.8 9.6 %fusion.80 = bf16[1024,256]{1,0:T(8,128)(2,1)} fusion(bf16[64,8,8,256]{3,2,1,0:T(8,128)(2,1)} %bitcast.238, f32[8,512,1024]{1,2,0:T(8,128)} %get-tuple-element.80, f32[8,512]{1,0:T(8,128)S(1)} %get-tuple-element.79), kind=kOutput, calls=%fused_computation.109 | convolution fusion | flops 2156134400 | bytes 19415040 | tf_op jit(solution)/shard_map/hqt,qhd->td/dot_general | solution.py:418
  359.4 29.2 %convert_bitcast_fusion.1 = bf16[512,8,256]{2,0,1:T(8,128)(2,1)} fusion(f32[1024,512,8]{1,0,2:T(8,128)} %fusion.59, f32[1024,512,8]{1,0,2:T(8,128)} %fusion.75, bf16[1024,256]{1,0:T(8,128)(2,1)S(1)} %copy-done.11, f32[8,512,1024]{1,2,0:T(8,128)} %get-tuple-element.80, f32[8,512]{1,0:T(8,128)S(1)} %get-tuple-element.79), kind=kOutput, calls=%fused_computation.94 | convolution fusion | flops 2194674688 | bytes 52969472 | tf_op jit(solution)/shard_map/hqt,td->qhd/dot_general | solution.py:416
  388.6 8.9 %fusion.87 = f32[2048,1024]{1,0:T(8,128)} fusion(bf16[512,2048]{0,1:T(8,128)(2,1)} %bitcast.273, s32[]{:T(128)S(6)} %select_n.25, bf16[512,2048]{1,0:T(8,128)(2,1)} %copy-done.14, bf16[1,512,2048]{2,1,0:T(8,128)(2,1)} %param.13, f32[512]{0:T(512)S(1)} %broadcast_multiply_fusion.1, f32[512]{0:T(512)S(1)} %get-tuple-element.77, f32[2048]{0:T(1024)S(1)} %bitcast.260, ...), kind=kOutput, calls=%fused_computation.115 | convolution fusion | flops 2155872256 | bytes 13645828 | tf_op jit(solution)/shard_map/dot_general | solution.py:344
  397.5 1.7 fusion.51
  399.2 2.8 pad_maximum_fusion.2
  401.9 3.9 copy.59
  405.9 3.9 copy.61
  409.9 7.4 %convolution_convert_fusion.2 = bf16[2048,1024]{1,0:T(8,128)(2,1)} fusion(bf16[512,2048]{0,1:T(8,128)(2,1)} %bitcast.274, s32[]{:T(128)S(6)} %select_n.28, bf16[512,2048]{1,0:T(8,128)(2,1)} %copy-done.14, bf16[1,512,2048]{2,1,0:T(8,128)(2,1)} %param.13, f32[512]{0:T(512)S(1)} %broadcast_multiply_fusion.1, f32[512]{0:T(512)S(1)} %get-tuple-element.77, ...), kind=kOutput, calls=%fused_computation.65 | convolution fusion | flops 2157969408 | bytes 9451524 | tf_op jit(solution)/shard_map/dot_general | solution.py:344
  417.4 2.1 fusion.117
  419.5 9.4 %convolution_convert_fusion.5 = bf16[512,2048]{1,0:T(8,128)(2,1)S(1)} fusion(bf16[2048,2560]{1,0:T(8,128)(2,1)} %bitcast.267, bf16[512,256]{1,0:T(8,128)(2,1)} %reduce-scatter.5.cloned.1.call-done, bf16[512,128]{1,0:T(8,128)(2,1)S(1)} %get-tuple-element.61, bf16[512,128]{1,0:T(8,128)(2,1)S(1)} %get-tuple-element.60, bf16[512,2048]{1,0:T(8,128)(2,1)} %copy.61), kind=kOutput, calls=%fused_computation.68 | convolution fusion | flops 5380243456 | bytes 15204352 | tf_op jit(solution)/shard_map/dot_general | solution.py:344
  428.9 1.4 copy-done.3
  430.3 3.0 fusion.31
  433.9 3.9 copy.62
  437.9 1.7 pad_maximum_fusion
  439.6 4.9 convolution_convert_fusion
  444.5 5.5 %fusion.76.own0 = f32[4,4,4,32,1280]{4,3,2,1,0:T(8,128)} fusion(bf16[4,4,4,32,512]{4,3,2,1,0:T(8,128)(2,1)S(1)} %bitcast.240, bf16[512,2560]{1,0:T(8,128)(2,1)S(1)} %pad_maximum_fusion, s32[]{:T(128)S(6)} %select_n.24), kind=kOutput, calls=%fused_computation.105 | convolution fusion | flops 2684354560 | bytes 13893636 | tf_op jit(solution)/shard_map/dot_general | solution.py:344
  450.2 1.1 dynamic-slice_bitcast_fusion
  451.3 76.7 %scatter_grads.1 = (f32[2,32,1280]{2,1,0:T(8,128)}, f32[2,32,1024]{2,1,0:T(8,128)}, f32[2,16,128]{2,1,0:T(8,128)}) custom-call(f32[4,4,4,32,1280]{4,3,2,1,0:T(8,128)} %fusion.76.own0, f32[4,4,4,32,1024]{4,3,2,1,0:T(8,128)} %bitcast.232, f32[4,4,4,16,128]{4,3,2,1,0:T(8,128)} %get-tuple-element.57.own_g, bf16[4,4,4,32,1280]{4,3,2,1,0:T(8,128)(2,1)} %bitcast.236, ...), custom_call_target="tpu_custom_call" | custom-call | tf_op jit(solution)/shard_map/scatter_grads/pallas_call | solution.py:300
  528.1 1.2 slice_bitcast_fusion.2
  529.3 0.8 copy.81
  531.4 1.0 slice_bitcast_fusion.4
  532.4 0.7 copy.99
  533.1 1.2 slice_bitcast_fusion.7
  534.3 4.9 fusion.54
  (85 shorter events, 4.4 us)
Async XLA Ops:
  7.2 410.2 %reduce-scatter.3.cloned.1.call-start = ((), (), s32[]{:S(2)}) async-start(), calls=%async_computation.2 | async-start | bytes 786432 | tf_op jit(solution)/shard_map/reduce_scatter | solution.py:419
  7.2 249.6 %copy-start.25 = (f32[128]{0:T(128)}, f32[128]{0:T(128)S(1)}, u32[]{:S(2)}) copy-start(f32[128]{0:T(128)S(1)} %multiply_power_fusion) | copy-start | bytes 1540
  161.5 88.3 %copy-start.18 = (f32[1,2048]{1,0:T(1,128)}, f32[1,2048]{1,0:T(1,128)S(1)}, u32[]{:S(2)}) copy-start(f32[1,2048]{1,0:T(1,128)S(1)} %get-tuple-element.71) | copy-start | bytes 24580
  164.2 85.7 %copy-start.22 = (f32[512]{0:T(512)}, f32[512]{0:T(512)S(1)}, u32[]{:S(2)}) copy-start(f32[512]{0:T(512)S(1)} %get-tuple-element.76) | copy-start | bytes 6148
  249.9 2.5 copy-start.24
  249.9 4.3 copy-start.27
  254.2 2.6 copy-start.20
  256.8 5.4 copy-start.6
  260.2 2.0 copy-start.10
  262.2 8.2 %copy-start.5 = (bf16[512,8,128]{2,0,1:T(8,128)(2,1)}, bf16[512,8,128]{2,0,1:T(8,128)(2,1)S(1)}, u32[]{:S(2)}) copy-start(bf16[512,8,128]{2,0,1:T(8,128)(2,1)S(1)} %get-tuple-element.51) | copy-start | bytes 3145732
  262.2 8.2 %copy-start.16 = (pred[512,1024]{0,1:T(8,128)(4,1)S(1)}, pred[512,1024]{0,1:T(8,128)(4,1)}, u32[]{:S(2)}) copy-start(pred[512,1024]{0,1:T(8,128)(4,1)} %fusion.63) | copy-start | bytes 1572868
  270.4 11.5 %copy-start.8 = (bf16[1024,256]{1,0:T(8,128)(2,1)S(1)}, bf16[1024,256]{1,0:T(8,128)(2,1)}, u32[]{:S(2)}) copy-start(bf16[1024,256]{1,0:T(8,128)(2,1)} %all_gather.13) | copy-start | bytes 1572868
  290.0 9.3 %copy-start.28 = (bf16[256,8,512]{2,0,1:T(8,128)(2,1)}, bf16[256,8,512]{2,0,1:T(8,128)(2,1)S(1)}, u32[]{:S(2)}) copy-start(bf16[256,8,512]{2,0,1:T(8,128)(2,1)S(1)} %fusion.64) | copy-start | bytes 6291460
  290.1 9.3 %copy-start = (bf16[1,512,2048]{2,1,0:T(8,128)(2,1)S(1)}, bf16[1,512,2048]{2,1,0:T(8,128)(2,1)}, u32[]{:S(2)}) copy-start(bf16[1,512,2048]{2,1,0:T(8,128)(2,1)} %param.10) | copy-start | bytes 6291460
  290.1 9.3 %copy-start.2 = (bf16[1,512,2048]{2,1,0:T(8,128)(2,1)S(1)}, bf16[1,512,2048]{2,1,0:T(8,128)(2,1)}, u32[]{:S(2)}) copy-start(bf16[1,512,2048]{2,1,0:T(8,128)(2,1)} %param.13) | copy-start | bytes 6291460
  299.3 3.6 copy-start.14
  303.0 10.2 %copy-start.9 = (bf16[1024,256]{1,0:T(8,128)(2,1)S(1)}, bf16[1024,256]{1,0:T(8,128)(2,1)}, u32[]{:S(2)}) copy-start(bf16[1024,256]{1,0:T(8,128)(2,1)} %all_gather.13) | copy-start | bytes 1572868
  311.9 1.3 copy-start.4
  349.8 9.6 %copy-start.11 = (bf16[1024,256]{1,0:T(8,128)(2,1)S(1)}, bf16[1024,256]{1,0:T(8,128)(2,1)}, u32[]{:S(2)}) copy-start(bf16[1024,256]{1,0:T(8,128)(2,1)} %copy-done.10) | copy-start | bytes 1572868
  349.8 69.7 %reduce-scatter.5.cloned.1.call-start = ((), (), s32[]{:S(2)}) async-start(), calls=%async_computation.3 | async-start | bytes 786432 | tf_op jit(solution)/shard_map/reduce_scatter | solution.py:420
  388.6 8.9 %copy-start.7 = (f32[512,128]{1,0:T(8,128)S(1)}, f32[512,128]{1,0:T(8,128)}, u32[]{:S(2)}) copy-start(f32[512,128]{1,0:T(8,128)} %copy-done.6) | copy-start | bytes 786436
  388.6 8.9 %copy-start.12 = (bf16[512,8,256]{2,0,1:T(8,128)(2,1)S(1)}, bf16[512,8,256]{2,0,1:T(8,128)(2,1)}, u32[]{:S(2)}) copy-start(bf16[512,8,256]{2,0,1:T(8,128)(2,1)} %convert_bitcast_fusion.1) | copy-start | bytes 6291460
  388.6 8.9 %copy-start.15 = (f32[512,128]{1,0:T(8,128)S(1)}, f32[512,128]{1,0:T(8,128)}, u32[]{:S(2)}) copy-start(f32[512,128]{1,0:T(8,128)} %get-tuple-element.72) | copy-start | bytes 786436
  409.9 7.4 %copy-start.21 = (f32[1,512]{1,0:T(1,128)S(1)}, f32[1,512]{1,0:T(1,128)}, u32[]{:S(2)}) copy-start(f32[1,512]{1,0:T(1,128)} %copy-done.20) | copy-start | bytes 6148
  409.9 7.4 %copy-start.26 = (f32[128]{0:T(128)S(1)}, f32[128]{0:T(128)}, u32[]{:S(2)}) copy-start(f32[128]{0:T(128)} %copy-done.25) | copy-start | bytes 1540
  419.5 10.8 %copy-start.19 = (f32[1,2048]{1,0:T(1,128)S(1)}, f32[1,2048]{1,0:T(1,128)}, u32[]{:S(2)}) copy-start(f32[1,2048]{1,0:T(1,128)} %copy-done.18) | copy-start | bytes 24580
  419.5 10.8 %copy-start.23 = (f32[512]{0:T(512)S(1)}, f32[512]{0:T(512)}, u32[]{:S(2)}) copy-start(f32[512]{0:T(512)} %copy-done.22) | copy-start | bytes 6148
  428.9 1.4 copy-start.3
  430.3 7.6 %copy-start.17 = (bf16[512,256]{1,0:T(8,128)(2,1)S(1)}, bf16[512,256]{1,0:T(8,128)(2,1)}, u32[]{:S(2)}) copy-start(bf16[512,256]{1,0:T(8,128)(2,1)} %reduce-scatter.5.cloned.1.call-done) | copy-start | bytes 786436
  439.6 4.9 copy-start.13
  528.1 6.3 %copy-start.1 = (bf16[1,512,2048]{2,1,0:T(8,128)(2,1)S(1)}, bf16[1,512,2048]{2,1,0:T(8,128)(2,1)}, u32[]{:S(2)}) copy-start(bf16[1,512,2048]{2,1,0:T(8,128)(2,1)} %param.10) | copy-start | bytes 6291460
Sparse Core Ops, SparseCore 0:
  349.9 9.4 reduce-scatter.2
  361.7 11.8 reduce-scatter.4

commit v2 on v1

--- a/solution.py
+++ b/solution.py
@@ -14,7 +14,8 @@
 SIDE = 4
 VMEM_MAX = 67_043_328
 
-STREAMS = ((0, 0, 0, 512), (0, 1, 512, 384), (0, 2, 896, 384),
+STREAMS = ((2, 0, 0, 128),
+           (0, 0, 0, 512), (0, 1, 512, 384), (0, 2, 896, 384),
            (1, 0, 0, 256), (1, 1, 256, 384), (1, 2, 640, 384))
 
 
@@ -51,25 +52,29 @@
     return ref.at[idx[0], idx[1], idx[2], pl.ds(*rows), pl.ds(*cols)]
 
 
-def gather_kernel(in0, in1, out0, out1, send, recv, sib_send, sib_recv, own_sem):
+def gather_kernel(in0, in1, in2, out0, out1, out2, send, recv, sib_send, sib_recv, own_sem):
     coords, core = place()
     greet(coords, core)
-    ins, outs = (in0, in1), (out0, out1)
+    ins, outs = (in0, in1, in2), (out0, out1, out2)
     owns = []
-    for g in range(2):
+    for g in range(3):
         copy = pltpu.make_async_copy(ins[g], outs[g].at[coords[0], coords[1], coords[2]], own_sem.at[g])
         copy.start()
         owns.append(copy)
-    whole, low, high = (0, 32), (0, 16), (16, 16)
     sent, given = [], []
+
+    def rows_for(s, kind):
+        rows = ins[STREAMS[s][0]].shape[0]
+        return ((0, rows), (0, rows), (0, rows // 2), (rows // 2, rows // 2))[kind]
 
     def cols_of(s, side):
         g, _, off, width = STREAMS[s]
         half = outs[g].shape[-1] // 2
         return (pl.multiple_of(side * half + off, 128), width)
 
-    def send_to(s, p, kind, src, rows, at, to):
+    def send_to(s, p, kind, src, at, to):
         g, colour, _, _ = STREAMS[s]
+        rows = rows_for(s, kind)
         full = order_of(colour)[:p]
         cols = cols_of(s, core)
         dst = region(outs[g], full, at, rows, cols)
@@ -83,7 +88,7 @@
         g, colour, _, _ = STREAMS[s]
         order = order_of(colour)
         at = shifted(coords, order[p], (-1, 1, -2, 2)[kind])
-        rows = (whole, whole, low, high)[kind]
+        rows = rows_for(s, kind)
         here = region(outs[g], order[:p], at, rows, cols_of(s, core))
         pltpu.make_async_remote_copy(here, here, send.at[s, p, kind], recv.at[s, p, kind],
                                      device_id=device(coords, 1 - core), device_id_type=MESH).wait_recv()
@@ -102,15 +107,15 @@
             if p > 0:
                 arrived(s, p - 1, 2)
                 arrived(s, p - 1, 3)
-                if s in (0, 3) and p == 1:
+                if p == 1 and (s == 0 or STREAMS[s - 1][0] != g):
                     owns[g].wait()
             src = ins[g].at[:, pl.ds(*cols_of(s, core))] if p == 0 else None
-            send_to(s, p, 0, src, whole, coords, shifted(coords, dim, 1))
-            send_to(s, p, 1, src, whole, coords, shifted(coords, dim, -1))
+            send_to(s, p, 0, src, coords, shifted(coords, dim, 1))
+            send_to(s, p, 1, src, coords, shifted(coords, dim, -1))
         for s, (g, colour, _, _) in enumerate(STREAMS):
             dim = order_of(colour)[p]
-            send_to(s, p, 2, None, low, arrived(s, p, 0), shifted(coords, dim, 1))
-            send_to(s, p, 3, None, high, arrived(s, p, 1), shifted(coords, dim, -1))
+            send_to(s, p, 2, None, arrived(s, p, 0), shifted(coords, dim, 1))
+            send_to(s, p, 3, None, arrived(s, p, 1), shifted(coords, dim, -1))
     for s in range(len(STREAMS)):
         arrived(s, 2, 2)
         arrived(s, 2, 3)
@@ -121,22 +126,22 @@
         in_copy.wait_recv()
 
 
-def gather_weights(w0, w1):
+def gather_weights(*ws):
     ns = len(STREAMS)
-    shapes = [jax.ShapeDtypeStruct((SIDE, SIDE, SIDE, 32, w.shape[1]), w.dtype) for w in (w0, w1)]
+    shapes = [jax.ShapeDtypeStruct((SIDE, SIDE, SIDE) + w.shape, w.dtype) for w in ws]
     dma = pltpu.SemaphoreType.DMA
     return pl.pallas_call(
         gather_kernel, name="gather_weights",
         out_shape=shapes,
-        in_specs=[pl.BlockSpec(memory_space=pltpu.VMEM)] * 2,
-        out_specs=[pl.BlockSpec(memory_space=pl.ANY)] * 2,
-        scratch_shapes=[dma((ns, 3, 4))] * 4 + [dma((2,))],
+        in_specs=[pl.BlockSpec(memory_space=pltpu.VMEM)] * 3,
+        out_specs=[pl.BlockSpec(memory_space=pl.ANY)] * 3,
+        scratch_shapes=[dma((ns, 3, 4))] * 4 + [dma((3,))],
         compiler_params=pltpu.CompilerParams(collective_id=1, has_side_effects=True),
-    )(w0, w1)
+    )(*ws)
 
 
 def scatter_kernel(own0, own1, own_g, sib0, sib1, sib_g, out0, out1, out_g, *scratch):
-    ns = len(STREAMS) + 1
+    ns = len(STREAMS)
     scratch = list(scratch)
     sib_bufs = scratch[:3]
     acc = [[scratch[3 + s * 3 + q] for q in range(3)] for s in range(ns)]
@@ -156,7 +161,7 @@
                                             device_id=sibling, device_id_type=MESH)
         copy.start()
         gifts.append(copy)
-    streams = [(2, 0, 0, 128)] + list(STREAMS)
+    streams = STREAMS
     sent = []
 
     def lead(order, q, at, n):
@@ -284,7 +289,7 @@
 
 def scatter_grads(own0, own1, own_g, sib0, sib1, sib_g):
     owns, sibs = (own0, own1, own_g), (sib0, sib1, sib_g)
-    streams = [(2, 0, 0, 128)] + list(STREAMS)
+    streams = STREAMS
     ns = len(streams)
     dma = pltpu.SemaphoreType.DMA
     scratch = [pltpu.VMEM(a.shape, a.dtype) for a in sibs]
@@ -308,6 +313,128 @@
     )(own0, own1, own_g, sib0, sib1, sib_g)
 
 
+LOG2E = 1.4426950408889634
+TILE = 256
+
+
+def nt(a, b):
+    return lax.dot_general(a, b, (((1,), (1,)), ((), ())), preferred_element_type=jnp.float32)
+
+
+def nn(a, b):
+    return lax.dot_general(a, b, (((1,), (0,)), ((), ())), preferred_element_type=jnp.float32)
+
+
+def fill_mask(mask, ids_k, ids_q):
+    n_keys, n_q = mask.shape
+    core = lax.axis_index('cp')
+    for c in range(n_keys // TILE):
+        base = jnp.where(c < n_q // TILE, (1 - core) * n_q, core * n_q - n_q) + c * TILE
+        for i in range(n_q // TILE):
+            k_at = base + lax.broadcasted_iota(jnp.int32, (TILE, TILE), 0)
+            q_at = core * n_q + i * TILE + lax.broadcasted_iota(jnp.int32, (TILE, TILE), 1)
+            same = ids_k[pl.ds(c * TILE, TILE), :] == ids_q[:, pl.ds(i * TILE, TILE)]
+            mask[pl.ds(c * TILE, TILE), pl.ds(i * TILE, TILE)] = jnp.where(same & (k_at <= q_at), 1.0, 0.0)
+
+
+def keys_for(i, n_q):
+    return n_q + (i + 1) * TILE
+
+
+def attend_kernel(ratio, q_ref, k_ref, v_ref, ids_k, ids_q, o_ref, inv_ref, mask, v_t, w_scr, p_scr):
+    n_q = q_ref.shape[0]
+    fill_mask(mask, ids_k, ids_q)
+    v_t[...] = v_ref[...].T
+
+    def head(h, carry):
+        cols = pl.ds(pl.multiple_of(h * TILE, TILE), TILE)
+        for i in range(n_q // TILE):
+            qi = q_ref[pl.ds(i * TILE, TILE), cols]
+            n_keys = keys_for(i, n_q)
+            total = jnp.zeros((8, TILE), jnp.float32)
+            for c in range(n_keys // TILE):
+                t = jnp.tanh(nt(k_ref[pl.ds(c * TILE, TILE), :], qi) * ratio)
+                w = jnp.exp2(t * (SOFT_CAP * LOG2E)) * mask[pl.ds(c * TILE, TILE), pl.ds(i * TILE, TILE)]
+                w_scr[i, pl.ds(c * TILE, TILE), :] = w
+                total = total + jnp.sum(w.reshape(TILE // 8, 8, TILE), axis=0)
+            inv = 1.0 / jnp.sum(total, axis=0, keepdims=True)
+            inv_ref[h, :, pl.ds(i * TILE, TILE)] = inv
+            p_scr[i, pl.ds(0, n_keys), :] = (w_scr[i, pl.ds(0, n_keys), :] * inv).astype(jnp.bfloat16)
+            o_t = nn(v_t[:, pl.ds(0, n_keys)], p_scr[i, pl.ds(0, n_keys), :])
+            o_ref[pl.ds(i * TILE, TILE), cols] = o_t.T.astype(jnp.bfloat16)
+        return carry
+    lax.fori_loop(0, q_ref.shape[1] // TILE, head, 0)
+
+
+def attend(q, k, v, ids_k, ids_q, n_heads, ratio):
+    n_q, n_k = q.shape[0], k.shape[0]
+    vmem = pl.BlockSpec(memory_space=pltpu.VMEM)
+    return pl.pallas_call(
+        functools.partial(attend_kernel, ratio), name="attend",
+        out_shape=[jax.ShapeDtypeStruct(q.shape, jnp.bfloat16), jax.ShapeDtypeStruct((n_heads, 1, n_q), jnp.float32)],
+        in_specs=[vmem] * 5, out_specs=[vmem] * 2,
+        scratch_shapes=[pltpu.VMEM((n_k, n_q), jnp.float32), pltpu.VMEM((TILE, n_k), jnp.bfloat16),
+                        pltpu.VMEM((n_q // TILE, n_k, TILE), jnp.float32),
+                        pltpu.VMEM((n_q // TILE, n_k, TILE), jnp.bfloat16)],
+        cost_estimate=pl.CostEstimate(flops=8_000_000_000, bytes_accessed=6_000_000, transcendentals=8_000_000),
+    )(q, k, v, ids_k, ids_q)
+
+
+def attend_back_kernel(ratio, q_ref, do_ref, k_ref, v_ref, ids_k, ids_q, inv_ref, dq_ref, dk_ref, dv_ref,
+                       mask, k_t, g_scr, dp_scr, p_scr, ds_scr, dk_acc, dv_acc):
+    n_q = q_ref.shape[0]
+    fill_mask(mask, ids_k, ids_q)
+    k_t[...] = k_ref[...].T
+    dk_acc[...] = jnp.zeros_like(dk_acc)
+    dv_acc[...] = jnp.zeros_like(dv_acc)
+
+    def head(h, carry):
+        cols = pl.ds(pl.multiple_of(h * TILE, TILE), TILE)
+        for i in range(n_q // TILE):
+            rows = pl.ds(i * TILE, TILE)
+            qi, doi = q_ref[rows, cols], do_ref[rows, cols]
+            inv = inv_ref[h, :, rows]
+            n_keys = keys_for(i, n_q)
+            total = jnp.zeros((8, TILE), jnp.float32)
+            for c in range(n_keys // TILE):
+                at = pl.ds(c * TILE, TILE)
+                t = jnp.tanh(nt(k_ref[at, :], qi) * ratio)
+                p = jnp.exp2(t * (SOFT_CAP * LOG2E)) * (mask[at, rows] * inv)
+                dp = nt(v_ref[at, :], doi)
+                p_scr[i, at, :] = p.astype(jnp.bfloat16)
+                g_scr[i, at, :] = p * ((1.0 - t * t) * (ratio * SOFT_CAP))
+                dp_scr[i, at, :] = dp
+                total = total + jnp.sum((p * dp).reshape(TILE // 8, 8, TILE), axis=0)
+            row_dot = jnp.sum(total, axis=0, keepdims=True)
+            seen = pl.ds(0, n_keys)
+            ds_scr[i, seen, :] = ((dp_scr[i, seen, :] - row_dot) * g_scr[i, seen, :]).astype(jnp.bfloat16)
+            dq_t = nn(k_t[:, seen], ds_scr[i, seen, :])
+            dq_ref[rows, cols] = dq_t.T.astype(jnp.bfloat16)
+            dk_acc[seen, :] += nn(ds_scr[i, seen, :], qi)
+            dv_acc[seen, :] += nn(p_scr[i, seen, :], doi)
+        return carry
+    lax.fori_loop(0, q_ref.shape[1] // TILE, head, 0)
+    dk_ref[...] = dk_acc[...].astype(jnp.bfloat16)
+    dv_ref[...] = dv_acc[...].astype(jnp.bfloat16)
+
+
+def attend_back(q, do, k, v, ids_k, ids_q, inv_sum, n_heads, ratio):
+    n_q, n_k = q.shape[0], k.shape[0]
+    vmem = pl.BlockSpec(memory_space=pltpu.VMEM)
+    tiles = n_q // TILE
+    bf, f32 = jnp.bfloat16, jnp.float32
+    return pl.pallas_call(
+        functools.partial(attend_back_kernel, ratio), name="attend_back",
+        out_shape=[jax.ShapeDtypeStruct(q.shape, bf)] + [jax.ShapeDtypeStruct(k.shape, bf)] * 2,
+        in_specs=[vmem] * 7, out_specs=[vmem] * 3,
+        scratch_shapes=[pltpu.VMEM((n_k, n_q), f32), pltpu.VMEM((TILE, n_k), bf),
+                        pltpu.VMEM((tiles, n_k, TILE), f32), pltpu.VMEM((tiles, n_k, TILE), f32),
+                        pltpu.VMEM((tiles, n_k, TILE), bf), pltpu.VMEM((tiles, n_k, TILE), bf),
+                        pltpu.VMEM((n_k, TILE), f32), pltpu.VMEM((n_k, TILE), f32)],
+        cost_estimate=pl.CostEstimate(flops=16_000_000_000, bytes_accessed=8_000_000, transcendentals=8_000_000),
+    )(q, do, k, v, ids_k, ids_q, inv_sum)
+
+
 def rope_tables(pos_ids, head_dim):
     half_dim = head_dim // 2
     inv_freq = ROPE_BASE ** (-2.0 * jnp.arange(half_dim, dtype=jnp.float32) / head_dim)
@@ -362,9 +489,11 @@
         w0 = jnp.concatenate([w_query.reshape(rows, q_cols), w_key.reshape(rows, head_dim),
                               w_value.reshape(rows, head_dim)], axis=1)
         w1 = w_out.reshape(q_cols, rows).T
-        gains = lax.all_gather(jnp.stack([gain_pre, gain_post]), 'fsdp', axis=1, tiled=True)
-        pre_full, post_full = gains[0], gains[1]
-        wqkv, wo_t = gather_weights(w0, w1)
+        w2 = jnp.pad(jnp.stack([gain_pre, gain_post]).astype(f32), ((0, 0), (0, 128 - rows))).reshape(1, 256)
+        w2 = jnp.pad(w2, ((0, 15), (0, 0)))
+        wqkv, wo_t, gains = gather_weights(w0, w1, w2)
+        gains = gains[..., 0, :].reshape(model_dim // rows, 256)
+        pre_full, post_full = gains[:, :rows].reshape(model_dim), gains[:, 128:128 + rows].reshape(model_dim)
         wqkv = wqkv.reshape(model_dim, q_cols + 2 * head_dim)
         wo_t = wo_t.reshape(model_dim, q_cols)
         q_scale = (head_dim if head_dim >= 256 else model_dim // n_heads) ** -0.5
@@ -378,28 +507,21 @@
         q_rot = rotate(q_proj, cos_t, sin_t)
         k_rot = rotate(k_proj, cos_t, sin_t)[:, 0]
 
-        k_all = lax.all_gather(k_rot, 'cp', axis=0, tiled=True)
-        v_all = lax.all_gather(v_proj, 'cp', axis=0, tiled=True)
-        ids_all = lax.all_gather(doc_ids, 'cp', axis=1, tiled=True)
-        q_index = core * n_tok + jnp.arange(n_tok)
-        k_index = jnp.arange(k_all.shape[0])
-        visible = (doc_ids[0][:, None] == ids_all[0][None, :]) & (k_index[None, :] <= q_index[:, None])
-        scores = jnp.einsum('qhd,td->hqt', q_rot, k_all, preferred_element_type=f32) * q_scale
-        tanh_s = jnp.tanh(scores / SOFT_CAP)
-        capped = jnp.where(visible, SOFT_CAP * tanh_s, -1e30)
-        row_peak = jnp.max(capped, axis=-1, keepdims=True)
-        weights = jnp.exp(capped - row_peak)
-        attn_prob = weights / jnp.sum(weights, axis=-1, keepdims=True)
-        prob_low = attn_prob.astype(bf)
-        attn_out = jnp.einsum('hqt,td->qhd', prob_low, v_all, preferred_element_type=f32).astype(bf)
-        attn_flat = attn_out.reshape(n_tok, q_cols)
+        swap = [(0, 1), (1, 0)]
+        kv_own = jnp.concatenate([k_rot, v_proj], axis=1)
+        kv_all = jnp.concatenate([lax.ppermute(kv_own, 'cp', swap), kv_own], axis=0)
+        k_all, v_all = kv_all[:, :head_dim], kv_all[:, head_dim:]
+        ids_all = jnp.concatenate([lax.ppermute(doc_ids[0], 'cp', swap), doc_ids[0]])[:, None]
+        q_flat = q_rot.reshape(n_tok, q_cols)
+        ratio = q_scale / SOFT_CAP
+        attn_flat, inv_sum = attend(q_flat, k_all, v_all, ids_all, doc_ids, n_heads, ratio)
         proj_out = dot(attn_flat, wo_t, (1, 1)).astype(bf)
         post_out, inv_post = norm_forward(proj_out, post_full)
         out_hidden = (hidden.astype(f32) + post_out.astype(f32)).astype(bf)
 
         d_proj, d_gain_post = norm_backward(proj_out, inv_post, post_full, grad_out)
         d_proj = d_proj.astype(bf)
-        d_attn = dot(d_proj, wo_t, (1, 0)).astype(bf).reshape(n_tok, n_heads, head_dim)
+        d_attn = dot(d_proj, wo_t, (1, 0)).astype(bf)
 
         def halves(grads, acts):
             width = acts.shape[1] // 2
@@ -410,14 +532,11 @@
 
         own1, sib1 = halves(d_proj, attn_flat)
 
-        d_prob = jnp.einsum('qhd,td->hqt', d_attn, v_all, preferred_element_type=f32)
-        row_dot = jnp.sum(attn_prob * d_prob, axis=-1, keepdims=True)
-        d_score = (attn_prob * (d_prob - row_dot) * (1.0 - tanh_s * tanh_s) * q_scale).astype(bf)
-        d_q_rot = jnp.einsum('hqt,td->qhd', d_score, k_all, preferred_element_type=f32).astype(bf)
-        d_k_part = jnp.einsum('hqt,qhd->td', d_score, q_rot, preferred_element_type=f32).astype(bf)
-        d_v_part = jnp.einsum('hqt,qhd->td', prob_low, d_attn, preferred_element_type=f32).astype(bf)
-        d_k_rot = lax.psum_scatter(d_k_part, 'cp', scatter_dimension=0, tiled=True)
-        d_v_proj = lax.psum_scatter(d_v_part, 'cp', scatter_dimension=0, tiled=True)
+        d_q_flat, d_k, d_v = attend_back(q_flat, d_attn, k_all, v_all, ids_all, doc_ids, inv_sum, n_heads, ratio)
+        d_kv = jnp.concatenate([d_k, d_v], axis=1)
+        d_kv = (d_kv[n_tok:].astype(f32) + lax.ppermute(d_kv[:n_tok], 'cp', swap).astype(f32)).astype(bf)
+        d_k_rot, d_v_proj = d_kv[:, :head_dim], d_kv[:, head_dim:]
+        d_q_rot = d_q_flat.reshape(n_tok, n_heads, head_dim)
         d_q_proj = rotate(d_q_rot, cos_t, -sin_t)
         d_k_proj = rotate(d_k_rot[:, None], cos_t, -sin_t)[:, 0]
         d_qkv = jnp.concatenate([d_q_proj.reshape(n_tok, q_cols), d_k_proj, d_v_proj], axis=1)

time: 555 us -> 296 us (0.53)
  blocking collectives: 157 us -> 0 us
  matrix products: 166 us -> 59.4 us
  Pallas kernels: 152 us -> 173 us
  between operations: 15 us -> 1.51 us
    all_gather x4 -> x0, blocking collectives: 157 us -> none  [the longest x1 151 us: layer_local(): lax.all_gather(jnp.stack([gain_pre, gain_post]), 'fsdp', axis=1, tiled=True)]
    dot_general x6 -> x0, matrix products: 91.6 us -> none  [the longest x1 29.2 us: layer_local(): jnp.einsum('hqt,td->qhd', d_score, k_all, preferred_element_type=f32)]
    pallas_call x0 -> x2, Pallas kernels: none -> 37.8 us  [the longest x1 23 us: attend_back(): pl.pallas_call(functools.partial(attend_back_kernel, ratio), name='attend...]
    pallas_call x1, Pallas kernels: 75.2 us -> 58 us  [gather_weights(): pl.pallas_call(gather_kernel, name='gather_weights', out_shape=shapes, in...]
    sub x1 -> x0, matrix products: 11.5 us -> none  [layer_local(): weights = jnp.exp(capped - row_peak)]
  transfers between devices with their start and end apart: 2 -> 3, of which waited for: 0 -> 0; matrix products, arithmetic and copies ran while one was open for 13% -> 8% of each run, Pallas kernels for 0% -> 0%
where the time goes in v2:
time: 296 us; the launch traced here: 290 us
  Pallas kernels  173 us (58%)
  matrix products  59.4 us (20%)
  other arithmetic  29.6 us (10%)
  local copies, waits for them, and re-layouts  26.3 us (9%)
    pallas_call x1, Pallas kernels, scatter_grads(): pl.pallas_call(scatter_kernel, name='scatter_grads', out_shape=[jax.Shape...  76.9 us
    dot_general x8, matrix products, dot(): lax.dot_general(a, b, ((dims[:1], dims[1:]), ((), ())), preferred_element...  59.4 us
    pallas_call x1, Pallas kernels, gather_weights(): pl.pallas_call(gather_kernel, name='gather_weights', out_shape=shapes, in...  58 us
    pallas_call x1, Pallas kernels, attend_back(): pl.pallas_call(functools.partial(attend_back_kernel, ratio), name='attend...  23 us
    pallas_call x1, Pallas kernels, attend(): pl.pallas_call(functools.partial(attend_kernel, ratio), name='attend', ou...  14.8 us
    unnamed x48, local copies, waits for them, and re-layouts  9.69 us
    reduce_sum x2, other arithmetic, norm_backward(): d_gain = jnp.sum(grads_f * values_f * inv_rms, axis=0)  6.54 us
  transfers between devices with their start and end apart: 3, of which 0 were waited for; matrix products, arithmetic and copies ran while one was open for 8% of the time, Pallas kernels for 0%

profile of v2, /device:TPU:1, one launch (start us, length us, event | category | flops | bytes accessed | tf_op | source)
XLA Modules:
  0.0 290.4 jit_solution(10001678019132608738)
XLA Ops:
  0.6 0.7 convert_element_type.141
  1.3 0.9 copy.34
  2.3 1.6 copy.33
  3.8 0.7 fusion.81
  5.1 1.4 pad_maximum_fusion.6.in0
  6.5 58.0 %gather_weights.1 = (bf16[4,4,4,32,2560]{4,3,2,1,0:T(8,128)(2,1)}, bf16[4,4,4,32,2048]{4,3,2,1,0:T(8,128)(2,1)}, f32[4,4,4,16,256]{4,3,2,1,0:T(8,128)}) custom-call(bf16[32,2560]{1,0:T(8,128)(2,1)} %pad_maximum_fusion.6.in0, bf16[32,2048]{1,0:T(8,128)(2,1)} %bitcast.158, f32[16,256]{1,0:T(8,128)} %pad_convert_fusion.in2), custom_call_target="tpu_custom_call" | custom-call | tf_op jit(solution)/shard_map/gather_weights/pallas_call | solution.py:133
  64.5 1.2 slice_reduce_fusion
  65.9 2.1 fusion.11
  68.5 9.0 %convolution_convert_fusion.1 = bf16[512,2560]{1,0:T(8,128)(2,1)S(1)} fusion(bf16[2048,2560]{1,0:T(8,128)(2,1)} %bitcast.173, bf16[1,512,2048]{2,1,0:T(8,128)(2,1)} %param.10, f32[2048]{0:T(1024)S(1)} %add.93, f32[512]{0:T(512)S(1)} %get-tuple-element.82), kind=kOutput, calls=%fused_computation.19 | convolution fusion | flops 5374214144 | bytes 15214592 | tf_op jit(solution)/shard_map/dot_general | solution.py:471
  77.6 1.2 fusion.70
  78.8 0.8 pad_maximum_fusion.3
  80.3 1.8 fusion.73
  82.3 0.7 copy.36
  83.0 0.7 fusion.30
  84.0 2.0 copy.37
  86.1 1.1 copy.24.ids_k
  87.2 1.1 maximum_maximum_fusion
  88.3 1.0 fusion.85
  89.4 14.8 %attend.1 = (bf16[512,2048]{1,0:T(8,128)(2,1)}, f32[8,1,512]{2,1,0:T(1,128)}) custom-call(bf16[512,2048]{1,0:T(8,128)(2,1)} %bitcast.152, bf16[1024,256]{1,0:T(8,128)(2,1)} %get-tuple-element.61.k_ref, bf16[1024,256]{1,0:T(8,128)(2,1)} %get-tuple-element.60.v_ref, s32[1024,1]{1,0:T(8,128)} %copy.24.ids_k, s32[1,512]{1,0:T(1,128)} %ids_q.3), custom_call_target="tpu_custom_call" | custom-call | flops 8000000000 | bytes 6000000 | tf_op jit(solution)/shard_map/attend/pallas_call | solution.py:372
  104.2 8.8 %fusion.22 = (f32[512]{0:T(512)S(1)}, bf16[512,2048]{1,0:T(8,128)(2,1)S(1)}) fusion(bf16[512,2048]{1,0:T(8,128)(2,1)} %get-tuple-element.21, bf16[2048,2048]{1,0:T(8,128)(2,1)} %bitcast.177), kind=kOutput, calls=%fused_computation.34 | convolution fusion | flops 4299161088 | bytes 12584960 | tf_op jit(solution)/shard_map/dot_general | solution.py:471
  113.0 3.6 %fusion.28 = (f32[2048]{0:T(1024)S(1)}, f32[512]{0:T(512)S(1)}, bf16[1,512,2048]{2,1,0:T(8,128)(2,1)}) fusion(bf16[512,2048]{1,0:T(8,128)(2,1)S(1)} %get-tuple-element.86, bf16[1,512,2048]{2,1,0:T(8,128)(2,1)S(1)} %copy-done.2, f32[512]{0:T(512)S(1)} %get-tuple-element.84, f32[2048]{0:T(1024)S(1)} %add.98, bf16[1,512,2048]{2,1,0:T(8,128)(2,1)S(1)} %copy-done), kind=kLoop, calls=%fused_computation.40 | loop fusion | flops 15726080 | bytes 8409088 | tf_op jit(solution)/shard_map/reduce_sum | solution.py:466
  116.6 9.9 %convolution_convert_fusion.3.do_ref = bf16[512,2048]{1,0:T(8,128)(2,1)} fusion(bf16[2048,2048]{1,0:T(8,128)(2,1)} %bitcast.178, bf16[512,2048]{1,0:T(8,128)(2,1)S(1)} %get-tuple-element.86, bf16[1,512,2048]{2,1,0:T(8,128)(2,1)S(1)} %copy-done.2, f32[512]{0:T(512)S(1)} %broadcast_multiply_fusion.1, f32[512]{0:T(512)S(1)} %get-tuple-element.83, ...), kind=kOutput, calls=%fused_computation.42 | convolution fusion | flops 4304404480 | bytes 14694400 | tf_op jit(solution)/shard_map/dot_general | solution.py:471
  126.5 23.0 %attend_back.1 = (bf16[512,2048]{1,0:T(8,128)(2,1)}, bf16[1024,256]{1,0:T(8,128)(2,1)}, bf16[1024,256]{1,0:T(8,128)(2,1)}) custom-call(bf16[512,2048]{1,0:T(8,128)(2,1)} %bitcast.153, bf16[512,2048]{1,0:T(8,128)(2,1)} %convolution_convert_fusion.3.do_ref, bf16[1024,256]{1,0:T(8,128)(2,1)} %get-tuple-element.61.k_ref, ...), custom_call_target="tpu_custom_call" | custom-call | flops 16000000000 | bytes 8000000 | tf_op jit(solution)/shard_map/attend_back/pallas_call | solution.py:426
  149.5 1.2 constant_dynamic-update-slice_fusion.1
  150.7 1.1 constant_dynamic-update-slice_fusion
  151.8 0.8 slice.130
  152.9 0.7 copy.38
  153.6 0.7 fusion.34
  154.5 2.0 copy.39
  156.7 7.6 %convolution_convert_fusion.2 = bf16[2048,1024]{1,0:T(8,128)(2,1)} fusion(bf16[512,2048]{1,0:T(8,128)(2,1)} %get-tuple-element.21, s32[]{:T(128)S(6)} %select_n.23, bf16[512,2048]{1,0:T(8,128)(2,1)} %copy-done.9, bf16[1,512,2048]{2,1,0:T(8,128)(2,1)} %param.13, f32[512]{0:T(512)S(1)} %broadcast_multiply_fusion.1, f32[512]{0:T(512)S(1)} %get-tuple-element.83, ...), kind=kOutput, calls=%fused_computation.41 | convolution fusion | flops 2157969408 | bytes 9451524 | tf_op jit(solution)/shard_map/dot_general | solution.py:471
  164.3 6.4 %fusion.48 = f32[2048,1024]{1,0:T(8,128)} fusion(bf16[512,2048]{1,0:T(8,128)(2,1)S(1)} %copy-done.15, s32[]{:T(128)S(6)} %select_n.20, bf16[512,2048]{1,0:T(8,128)(2,1)S(1)} %copy-done.10, bf16[1,512,2048]{2,1,0:T(8,128)(2,1)S(1)} %copy-done.3, f32[512]{0:T(512)S(1)} %broadcast_multiply_fusion.1, f32[512]{0:T(512)S(1)} %get-tuple-element.83, ...), kind=kOutput, calls=%fused_computation.78 | convolution fusion | flops 2155872256 | bytes 13645828 | tf_op jit(solution)/shard_map/dot_general | solution.py:471
  170.7 1.2 add_convert_fusion
  171.9 1.5 fusion.72
  173.4 5.9 %convolution_convert_fusion.5 = bf16[512,2048]{1,0:T(8,128)(2,1)S(1)} fusion(bf16[2048,2560]{1,0:T(8,128)(2,1)S(1)} %bitcast.176, bf16[512,256]{1,0:T(8,128)(2,1)S(1)} %get-tuple-element.63, bf16[512,128]{1,0:T(8,128)(2,1)S(1)} %get-tuple-element.67, bf16[512,128]{1,0:T(8,128)(2,1)S(1)} %get-tuple-element.66, bf16[512,2048]{1,0:T(8,128)(2,1)S(1)} %bitcast.143), kind=kOutput, calls=%fused_computation.44 | convolution fusion | flops 5380243456 | bytes 15204352 | tf_op jit(solution)/shard_map/dot_general | solution.py:471
  179.3 1.7 pad_maximum_fusion
  181.1 3.0 %fusion.18 = (f32[2048]{0:T(1024)S(1)}, f32[512]{0:T(512)S(1)}, bf16[2048,512]{0,1:T(8,128)(2,1)}) fusion(bf16[1,512,2048]{2,1,0:T(8,128)(2,1)S(1)} %copy-done, bf16[512,2048]{1,0:T(8,128)(2,1)S(1)} %convolution_convert_fusion.5, f32[512]{0:T(512)S(1)} %get-tuple-element.82, f32[2048]{0:T(1024)S(1)} %add.93), kind=kLoop, calls=%fused_computation.30 | loop fusion | flops 11531776 | bytes 6311936 | tf_op jit(solution)/shard_map/reduce_sum | solution.py:466
  184.6 3.9 %copy.26 = bf16[2048,512]{1,0:T(8,128)(2,1)} copy(bf16[2048,512]{0,1:T(8,128)(2,1)} %get-tuple-element.56) | data formatting | bytes 4194304 | tf_op jit(solution)/shard_map/dot_general | solution.py:471
  188.7 6.3 %convolution_convert_fusion = bf16[2048,1280]{1,0:T(8,128)(2,1)} fusion(bf16[512,2560]{1,0:T(8,128)(2,1)} %pad_maximum_fusion, s32[]{:T(128)S(6)} %select_n.22, bf16[1,512,2048]{2,1,0:T(8,128)(2,1)S(1)} %copy-done, f32[2048]{0:T(1024)S(1)} %add.93, f32[512]{0:T(512)S(1)} %get-tuple-element.82), kind=kOutput, calls=%fused_computation.5 | convolution fusion | flops 2691170304 | bytes 8660996 | tf_op jit(solution)/shard_map/dot_general | solution.py:471
  195.0 5.6 %fusion.43.own0 = f32[4,4,4,32,1280]{4,3,2,1,0:T(8,128)} fusion(bf16[4,4,4,32,512]{4,3,2,1,0:T(8,128)(2,1)S(1)} %bitcast.155, bf16[512,2560]{1,0:T(8,128)(2,1)S(1)} %copy-done.6, s32[]{:T(128)S(6)} %select_n.19), kind=kOutput, calls=%fused_computation.69 | convolution fusion | flops 2684354560 | bytes 13893636 | tf_op jit(solution)/shard_map/dot_general | solution.py:471
  200.7 1.1 dynamic-slice_bitcast_fusion
  201.8 76.9 %scatter_grads.1 = (f32[2,32,1280]{2,1,0:T(8,128)}, f32[2,32,1024]{2,1,0:T(8,128)}, f32[2,16,128]{2,1,0:T(8,128)}) custom-call(f32[4,4,4,32,1280]{4,3,2,1,0:T(8,128)} %fusion.43.own0, f32[4,4,4,32,1024]{4,3,2,1,0:T(8,128)} %bitcast.142, f32[4,4,4,16,128]{4,3,2,1,0:T(8,128)} %get-tuple-element.59.own_g, bf16[4,4,4,32,1280]{4,3,2,1,0:T(8,128)(2,1)} %bitcast.150, ...), custom_call_target="tpu_custom_call" | custom-call | tf_op jit(solution)/shard_map/scatter_grads/pallas_call | solution.py:305
  278.7 1.2 slice_bitcast_fusion.3
  279.9 0.8 copy.40
  280.7 0.6 copy.27
  282.0 1.0 slice_bitcast_fusion.5
  283.0 0.7 copy.43
  283.8 1.2 slice_bitcast_fusion.8
  285.0 5.0 %fusion.37 = bf16[1,512,2048]{2,1,0:T(8,128)(2,1)} fusion(bf16[1,512,2048]{2,1,0:T(8,128)(2,1)S(1)} %copy-done.1, bf16[512,2048]{1,0:T(8,128)(2,1)} %copy-done.4, bf16[1,512,2048]{2,1,0:T(8,128)(2,1)} %param.13, f32[512]{0:T(512)} %broadcast_multiply_fusion, f32[512]{0:T(512)} %get-tuple-element.81, f32[2048]{0:T(1024)} %copy-done.12, f32[512]{0:T(512)} %copy-done.13), kind=kLoop, calls=%fused_computation.62 | loop fusion | flops 10485760 | bytes 8402944 | tf_op jit(solution)/shard_map/broadcast_in_dim | solution.py:555
  (69 shorter events, 4.7 us)
Async XLA Ops:
  65.9 122.8 %copy-start.12 = (f32[2048]{0:T(1024)}, f32[2048]{0:T(1024)S(1)}, u32[]{:S(2)}) copy-start(f32[2048]{0:T(1024)S(1)} %add.93) | copy-start | bytes 24580
  68.5 120.2 %copy-start.13 = (f32[512]{0:T(512)}, f32[512]{0:T(512)S(1)}, u32[]{:S(2)}) copy-start(f32[512]{0:T(512)S(1)} %get-tuple-element.82) | copy-start | bytes 6148
  68.5 11.4 %copy-start.14 = (s32[1,512]{1,0:T(1,128)S(1)}, s32[1,512]{1,0:T(1,128)}, u32[]{:S(2)}) copy-start(s32[1,512]{1,0:T(1,128)} %ids_q.3) | copy-start | bytes 6148
  79.7 7.5 %collective-permute-start = (bf16[512,512]{1,0:T(8,128)(2,1)}, bf16[512,512]{1,0:T(8,128)(2,1)}, u32[]{:S(2)}, u32[]{:S(2)}) collective-permute-start(bf16[512,512]{1,0:T(8,128)(2,1)} %pad_maximum_fusion.3), channel_id=1, source_target_pairs={{0,1},{1,0},{2,3},{3,2},{4,5},{5,4},{6,7},{7,6},{8,9},{9,8},{10,11... | collective-permute-start | bytes 1572872 | tf_op jit(solution)/shard_map/ppermute | solution.py:512
  79.9 6.2 %collective-permute-start.1 = (s32[512]{0:T(512)S(1)}, s32[512]{0:T(512)S(1)}, u32[]{:S(2)}, u32[]{:S(2)}) collective-permute-start(s32[512]{0:T(512)S(1)} %bitcast.170), channel_id=1, source_target_pairs={{0,1},{1,0},{2,3},{3,2},{4,5},{5,4},{6,7},{7,6},{8,9},{9,8},{10,11... | collective-permute-start | bytes 6152 | tf_op jit(solution)/shard_map/ppermute | solution.py:514
  104.2 8.8 %copy-start = (bf16[1,512,2048]{2,1,0:T(8,128)(2,1)S(1)}, bf16[1,512,2048]{2,1,0:T(8,128)(2,1)}, u32[]{:S(2)}) copy-start(bf16[1,512,2048]{2,1,0:T(8,128)(2,1)} %param.10) | copy-start | bytes 6291460
  104.2 8.8 %copy-start.2 = (bf16[1,512,2048]{2,1,0:T(8,128)(2,1)S(1)}, bf16[1,512,2048]{2,1,0:T(8,128)(2,1)}, u32[]{:S(2)}) copy-start(bf16[1,512,2048]{2,1,0:T(8,128)(2,1)} %param.13) | copy-start | bytes 6291460
  113.0 3.6 %copy-start.9 = (bf16[512,2048]{1,0:T(8,128)(2,1)}, bf16[512,2048]{1,0:T(8,128)(2,1)S(1)}, u32[]{:S(2)}) copy-start(bf16[512,2048]{1,0:T(8,128)(2,1)S(1)} %get-tuple-element.86) | copy-start | bytes 6291460
  149.5 3.4 %copy-start.7 = (bf16[512,2048]{1,0:T(8,128)(2,1)S(1)}, bf16[512,2048]{1,0:T(8,128)(2,1)}, u32[]{:S(2)}) copy-start(bf16[512,2048]{1,0:T(8,128)(2,1)} %get-tuple-element.24) | copy-start | bytes 6291460
  149.5 4.0 %copy-start.11 = (f32[512,128]{1,0:T(8,128)S(1)}, f32[512,128]{1,0:T(8,128)}, u32[]{:S(2)}) copy-start(f32[512,128]{1,0:T(8,128)} %get-tuple-element.78) | copy-start | bytes 786436
  152.7 18.0 %collective-permute-start.2 = (bf16[512,512]{1,0:T(8,128)(2,1)}, bf16[512,512]{1,0:T(8,128)(2,1)}, u32[]{:S(2)}, u32[]{:S(2)}) collective-permute-start(bf16[512,512]{1,0:T(8,128)(2,1)} %slice.130), channel_id=1, source_target_pairs={{0,1},{1,0},{2,3},{3,2},{4,5},{5,4},{6,7},{7,6},{8,9},{9,8},{10,11... | collective-permute-start | bytes 1572872 | tf_op jit(solution)/shard_map/ppermute | solution.py:537
  156.6 7.6 %copy-start.3 = (bf16[1,512,2048]{2,1,0:T(8,128)(2,1)S(1)}, bf16[1,512,2048]{2,1,0:T(8,128)(2,1)}, u32[]{:S(2)}) copy-start(bf16[1,512,2048]{2,1,0:T(8,128)(2,1)} %param.13) | copy-start | bytes 6291460
  156.6 7.6 %copy-start.10 = (bf16[512,2048]{1,0:T(8,128)(2,1)S(1)}, bf16[512,2048]{1,0:T(8,128)(2,1)}, u32[]{:S(2)}) copy-start(bf16[512,2048]{1,0:T(8,128)(2,1)} %copy-done.9) | copy-start | bytes 6291460
  156.6 7.6 %copy-start.15 = (bf16[512,2048]{1,0:T(8,128)(2,1)S(1)}, bf16[512,2048]{1,0:T(8,128)(2,1)}, u32[]{:S(2)}) copy-start(bf16[512,2048]{1,0:T(8,128)(2,1)} %get-tuple-element.21) | copy-start | bytes 6291460
  156.7 16.7 %slice-start = ((s8[10485760]{0:T(1024)(128)(4,1)}), s8[4194304]{0:T(1024)(128)(4,1)S(1)}, s32[]{:S(2)}) async-start(s8[10485760]{0:T(1024)(128)(4,1)} %bitcast.174), calls=%async_computation | async-start | bytes 8388608
  156.7 16.7 %slice-start.1 = ((s8[10485760]{0:T(1024)(128)(4,1)}), s8[4194304]{0:T(1024)(128)(4,1)S(1)}, s32[]{:S(2)}) async-start(s8[10485760]{0:T(1024)(128)(4,1)} %bitcast.174), calls=%async_computation.1 | async-start | bytes 8388608
  164.3 9.1 %copy-start.5 = (bf16[64,8,8,256]{3,1,2,0:T(8,128)(2,1)S(1)}, bf16[64,8,8,256]{3,1,2,0:T(8,128)(2,1)}, u32[]{:S(2)}) copy-start(bf16[64,8,8,256]{3,1,2,0:T(8,128)(2,1)} %copy.39) | copy-start | bytes 6291460
  164.3 9.1 %slice-start.2 = ((s8[10485760]{0:T(1024)(128)(4,1)}), s8[2097152]{0:T(1024)(128)(4,1)S(1)}, s32[]{:S(2)}) async-start(s8[10485760]{0:T(1024)(128)(4,1)} %bitcast.174), calls=%async_computation.2 | async-start | bytes 4194304
  179.3 4.7 %copy-start.4 = (bf16[512,2048]{1,0:T(8,128)(2,1)}, bf16[512,2048]{1,0:T(8,128)(2,1)S(1)}, u32[]{:S(2)}) copy-start(bf16[512,2048]{1,0:T(8,128)(2,1)S(1)} %convolution_convert_fusion.5) | copy-start | bytes 6291460
  188.7 6.3 %copy-start.6 = (bf16[512,2560]{1,0:T(8,128)(2,1)S(1)}, bf16[512,2560]{1,0:T(8,128)(2,1)}, u32[]{:S(2)}) copy-start(bf16[512,2560]{1,0:T(8,128)(2,1)} %pad_maximum_fusion) | copy-start | bytes 7864324
  188.7 6.3 %copy-start.8 = (bf16[2048,512]{1,0:T(8,128)(2,1)S(1)}, bf16[2048,512]{1,0:T(8,128)(2,1)}, u32[]{:S(2)}) copy-start(bf16[2048,512]{1,0:T(8,128)(2,1)} %copy.26) | copy-start | bytes 6291460
  278.7 6.3 %copy-start.1 = (bf16[1,512,2048]{2,1,0:T(8,128)(2,1)S(1)}, bf16[1,512,2048]{2,1,0:T(8,128)(2,1)}, u32[]{:S(2)}) copy-start(bf16[1,512,2048]{2,1,0:T(8,128)(2,1)} %param.10) | copy-start | bytes 6291460

commit v3 on v2

v3 whole, which is shorter than its diff:
```python
import functools

import jax
import jax.numpy as jnp
from jax import lax
from jax.experimental import pallas as pl
from jax.experimental.pallas import tpu as pltpu
from jax.sharding import PartitionSpec as P

SOFT_CAP = 50.0
NORM_EPS = 1e-6
ROPE_BASE = 10000.0
MESH = pl.DeviceIdType.MESH
SIDE = 4
VMEM_MAX = 67_043_328

QKV = ((0, 0, 512), (1, 512, 384), (2, 896, 384))
OUT = ((0, 0, 256), (1, 256, 384), (2, 640, 384))
GAIN = ((0, 0, 128),)
CHUNK = 256


def place():
    f = lax.axis_index('fsdp')
    return (f // 16, lax.rem(f // 4, 4), lax.rem(f, 4)), lax.axis_index('cp')


def shifted(coords, dim, delta):
    out = list(coords)
    out[dim] = lax.rem(coords[dim] + delta + SIDE, SIDE)
    return tuple(out)


def device(coords, core):
    return (coords[0] * 16 + coords[1] * 4 + coords[2], core)


def greet(coords, core):
    barrier = pltpu.get_barrier_semaphore()
    for dim in range(3):
        for delta in (1, -1):
            pl.semaphore_signal(barrier, inc=1, device_id=device(shifted(coords, dim, delta), core), device_id_type=MESH)
    pl.semaphore_signal(barrier, inc=1, device_id=device(coords, 1 - core), device_id_type=MESH)
    pl.semaphore_wait(barrier, 7)


def order_of(colour):
    return tuple((colour + i) % 3 for i in range(3))


def region(ref, full, coords, rows, cols):
    idx = [pl.ds(0, SIDE) if d in full else coords[d] for d in range(3)]
    return ref.at[idx[0], idx[1], idx[2], pl.ds(*rows), pl.ds(*cols)]


class Gather:
    def __init__(self, streams, src, out, send, recv, sib_send, sib_recv):
        self.streams, self.src, self.out = streams, src, out
        self.sems = (send, recv, sib_send, sib_recv)
        self.coords, self.core = place()
        self.rows = out.shape[3]

    def cols(self, s, side):
        _, off, width = self.streams[s]
        return pl.ds(pl.multiple_of(side * (self.out.shape[4] // 2) + off, 128), width)

    def part(self, s, p, kind, at, side):
        full = order_of(self.streams[s][0])[:p]
        idx = [pl.ds(0, SIDE) if d in full else at[d] for d in range(3)]
        half = self.rows // 2
        r0, nr = ((0, self.rows), (0, self.rows), (0, half), (half, half))[kind]
        return self.out.at[idx[0], idx[1], idx[2], pl.ds(r0, nr), self.cols(s, side)]

    def hop(self, s, p, kind):
        dim = order_of(self.streams[s][0])[p]
        at = shifted(self.coords, dim, (0, 0, -1, 1)[kind])
        to = shifted(self.coords, dim, (1, -1, 1, -1)[kind])
        dst = self.part(s, p, kind, at, self.core)
        src = self.src.at[:, self.cols(s, self.core)] if p == 0 and kind < 2 else dst
        return pltpu.make_async_remote_copy(src, dst, self.sems[0].at[s, p, kind], self.sems[1].at[s, p, kind],
                                            device_id=device(to, self.core), device_id_type=MESH)

    def landed(self, s, p, kind, side):
        dim = order_of(self.streams[s][0])[p]
        return self.part(s, p, kind, shifted(self.coords, dim, (-1, 1, -2, 2)[kind]), side)

    def gift(self, s, p, kind, side):
        here = self.landed(s, p, kind, side)
        return pltpu.make_async_remote_copy(here, here, self.sems[2].at[s, p, kind], self.sems[3].at[s, p, kind],
                                            device_id=device(self.coords, 1 - self.core), device_id_type=MESH)

    def arrive(self, s, p, kind):
        here = self.landed(s, p, kind, self.core)
        pltpu.make_async_remote_copy(here, here, self.sems[0].at[s, p, kind], self.sems[1].at[s, p, kind],
                                     device_id=device(self.coords, 1 - self.core), device_id_type=MESH).wait_recv()

    def start(self, s, p):
        self.hop(s, p, 0).start()
        self.hop(s, p, 1).start()

    def middle(self, s, p):
        for kind in (0, 1):
            self.arrive(s, p, kind)
            self.hop(s, p, kind + 2).start()
            self.gift(s, p, kind, self.core).start()

    def finish(self, s, p):
        for kind in (2, 3):
            self.arrive(s, p, kind)
            self.gift(s, p, kind, self.core).start()

    def drain(self, s, p):
        for kind in range(4):
            self.hop(s, p, kind).wait_send()
            self.gift(s, p, kind, self.core).wait_send()
            self.gift(s, p, kind, 1 - self.core).wait_recv()


def gather_kernel(in0, in1, in2, out0, out1, out2, *sems):
    coords, core = place()
    greet(coords, core)
    own_sem = sems[12]
    ins, outs = (in0, in1, in2), (out0, out1, out2)
    owns = [pltpu.make_async_copy(ins[g], outs[g].at[coords[0], coords[1], coords[2]], own_sem.at[g]) for g in range(3)]
    for copy in owns:
        copy.start()
    qkv, out, gain = (Gather(st, ins[g], outs[g], *sems[4 * g:4 * g + 4]) for g, st in enumerate((QKV, OUT, GAIN)))
    work = [(gain, 0)] + [(qkv, s) for s in range(3)] + [(out, s) for s in range(3)]
    for p in range(3):
        if p == 1:
            for copy in owns:
                copy.wait()
        for gather, s in work:
            if p > 0:
                gather.finish(s, p - 1)
            if p < 2 or gather is not out:
                gather.start(s, p)
        for gather, s in work:
            if p < 2 or gather is not out:
                gather.middle(s, p)
    for gather, s in work[:4]:
        gather.finish(s, 2)
    for gather, s in work:
        for p in range(2 if gather is out else 3):
            gather.drain(s, p)


def gather_weights(*ws):
    shapes = [jax.ShapeDtypeStruct((SIDE, SIDE, SIDE) + w.shape, w.dtype) for w in ws]
    dma = pltpu.SemaphoreType.DMA
    return pl.pallas_call(
        gather_kernel, name="gather_weights",
        out_shape=shapes,
        in_specs=[pl.BlockSpec(memory_space=pltpu.VMEM)] * 3,
        out_specs=[pl.BlockSpec(memory_space=pltpu.HBM)] * 3,
        scratch_shapes=[dma((len(st), 3, 4)) for st in (QKV, OUT, GAIN) for _ in range(4)] + [dma((3,))],
        compiler_params=pltpu.CompilerParams(collective_id=1, has_side_effects=True),
    )(*ws)


class Scatter:
    def __init__(self, streams, own, sib, acc, sbuf, rbuf, send, recv):
        self.streams, self.own, self.sib = streams, own, sib
        self.acc, self.sbuf, self.rbuf, self.sems = acc, sbuf, rbuf, (send, recv)
        self.coords, self.core = place()

    def half(self, s):
        return self.acc[s][0].shape[1] // 2

    def dim(self, s, q):
        return order_of(self.streams[s][0])[2 - q]

    def value(self, s, q, at, n, r0):
        colour, off, width = self.streams[s]
        order = order_of(colour)
        nr = self.half(s)
        idx = list(at)
        full = sorted(order[:2 - q])
        for d, digit in zip(full, (n // SIDE, lax.rem(n, SIDE)) if len(full) == 2 else (n,)):
            idx[d] = digit
        if q == 0:
            where = (idx[0] * 16 + idx[1] * 4 + idx[2], pl.ds(r0, nr), pl.ds(off, width))
            return self.own[where] + self.sib[where].astype(jnp.float32)
        m = 0
        for d in sorted(order[:3 - q]):
            m = m * SIDE + idx[d]
        return self.acc[s][q - 1][m, pl.ds(r0, nr), :]

    def hop(self, s, q, kind):
        lo, n = ((0, 2), (2, 2), (4, 1), (5, 1))[kind]
        to = shifted(self.coords, self.dim(s, q), (1, -1, 1, -1)[kind])
        return pltpu.make_async_remote_copy(
            self.sbuf[s][q].at[pl.ds(lo, n)], self.rbuf[s][q].at[pl.ds(lo, n)],
            self.sems[0].at[s, q, kind], self.sems[1].at[s, q, kind],
            device_id=device(to, self.core), device_id_type=MESH)

    def each(self, q, body):
        n = SIDE ** (2 - q)

        def step(i, carry):
            body(i)
            return carry
        lax.fori_loop(0, n, step, 0, unroll=min(n, 2))

    def one(self, s, q):
        dim, half, buf = self.dim(s, q), self.half(s), self.sbuf[s][q]
        far, right, left = (shifted(self.coords, dim, d) for d in (2, 1, -1))

        def to_right(n):
            buf[0, n] = self.value(s, q, far, n, 0).astype(buf.dtype)
            buf[1, n] = self.value(s, q, right, n, half).astype(buf.dtype)

        def to_left(n):
            buf[2, n] = self.value(s, q, far, n, half).astype(buf.dtype)
            buf[3, n] = self.value(s, q, left, n, 0).astype(buf.dtype)
        self.each(q, to_right)
        self.hop(s, q, 0).start()
        self.each(q, to_left)
        self.hop(s, q, 1).start()

    def two(self, s, q):
        dim, half, buf, got = self.dim(s, q), self.half(s), self.sbuf[s][q], self.rbuf[s][q]
        right, left = (shifted(self.coords, dim, d) for d in (1, -1))

        def to_right(n):
            buf[4, n] = (self.value(s, q, right, n, 0) + got[0, n].astype(jnp.float32)).astype(buf.dtype)

        def to_left(n):
            buf[5, n] = (self.value(s, q, left, n, half) + got[2, n].astype(jnp.float32)).astype(buf.dtype)
        self.hop(s, q, 0).wait_recv()
        self.each(q, to_right)
        self.hop(s, q, 2).start()
        self.hop(s, q, 1).wait_recv()
        self.each(q, to_left)
        self.hop(s, q, 3).start()

    def three(self, s, q):
        half, got, acc = self.half(s), self.rbuf[s][q], self.acc[s][q]
        self.hop(s, q, 2).wait_recv()
        self.hop(s, q, 3).wait_recv()

        def keep(n):
            for r0, i, j in ((0, 3, 4), (half, 1, 5)):
                acc[n, pl.ds(r0, half), :] = (self.value(s, q, self.coords, n, r0) + got[i, n].astype(jnp.float32)
                                              + got[j, n].astype(jnp.float32))
        self.each(q, keep)

    def drain(self, s, q):
        for kind in range(4):
            self.hop(s, q, kind).wait_send()


def transpose_into(dst, src):
    def strip(j, carry):
        at = pl.ds(pl.multiple_of(j * CHUNK, CHUNK), CHUNK)
        dst[at, :] = src[:, at].T
        return carry
    lax.fori_loop(0, src.shape[1] // CHUNK, strip, 0)


def grad_chunk(grads_t, acts, dst, side, j):
    half = dst.shape[2]
    rhs = acts[:, pl.ds(pl.multiple_of(side * half + j * CHUNK, CHUNK), CHUNK)]
    n_rows = 512

    def strip(i, carry):
        at = pl.multiple_of(i * n_rows, n_rows)
        out = nn(grads_t[pl.ds(at, n_rows), :], rhs).astype(dst.dtype)
        dst[pl.ds(i * (n_rows // 32), n_rows // 32), :, pl.ds(j * CHUNK, CHUNK)] = out.reshape(n_rows // 32, 32, CHUNK)
        return carry
    lax.fori_loop(0, grads_t.shape[0] // n_rows, strip, 0)


def chunk_gift(src, dst, send, recv, j):
    coords, core = place()
    at = pl.ds(j * CHUNK, CHUNK)
    return pltpu.make_async_remote_copy(src.at[:, :, at], dst.at[:, :, at], send.at[j], recv.at[j],
                                        device_id=device(coords, 1 - core), device_id_type=MESH)


def wire_shapes(streams, dtype, rows, phases):
    return [pltpu.VMEM((6, SIDE ** (2 - q), rows // 2, width), dtype) for _, _, width in streams for q in phases]


def acc_shapes(streams, rows, phases):
    return [((SIDE ** (2 - q), rows, width), jnp.float32) for _, _, width in streams for q in phases]


def scatter_kernel(normed, d_qkv, own_g, sib_g, acc_o0, acc_o1, acc_o2, out_q, out_o, out_g, *scratch):
    scratch = list(scratch)

    def take(n):
        head = scratch[:n]
        del scratch[:n]
        return head
    normed_t, own_q, sib_out, sib_q, sib_in_g = take(5)
    acc_q, sbuf_q, rbuf_q = take(9), take(9), take(9)
    acc_o, sbuf_o, rbuf_o = take(6), take(6), take(6)
    acc_g, sbuf_g, rbuf_g = take(3), take(3), take(3)
    sems = take(6)
    gift_send, gift_recv, gain_sem, fin_send, fin_recv = take(5)
    coords, core = place()
    sibling = device(coords, 1 - core)
    greet(coords, core)

    def triples(flat):
        return [flat[3 * s:3 * s + 3] for s in range(len(flat) // 3)]

    def tails(flat, heads):
        return [[heads[s]] + flat[2 * s:2 * s + 2] for s in range(3)]
    qkv = Scatter(QKV, own_q, sib_q, triples(acc_q), triples(sbuf_q), triples(rbuf_q), *sems[0:2])
    out = Scatter(OUT, None, None, tails(acc_o, (acc_o0, acc_o1, acc_o2)), tails(sbuf_o, (None,) * 3),
                  tails(rbuf_o, (None,) * 3), *sems[2:4])
    gain = Scatter(GAIN, own_g, sib_in_g, triples(acc_g), triples(sbuf_g), triples(rbuf_g), *sems[4:6])
    gain_gift = pltpu.make_async_remote_copy(sib_g, sib_in_g, gain_sem.at[0], gain_sem.at[1],
                                             device_id=sibling, device_id_type=MESH)
    gain_gift.start()
    for s in range(3):
        out.one(s, 1)
    transpose_into(normed_t, normed)
    chunks = own_q.shape[2] // CHUNK
    gifts = [chunk_gift(sib_out, sib_q, gift_send, gift_recv, j) for j in range(chunks)]
    for j in range(chunks):
        grad_chunk(normed_t, d_qkv, sib_out, 1 - core, j)
        gifts[j].start()
    for s in range(3):
        out.two(s, 1)
    gain_gift.wait_recv()
    gain.one(0, 0)
    done = 0
    for s, (_, off, width) in enumerate(QKV):
        while done * CHUNK < off + width:
            grad_chunk(normed_t, d_qkv, own_q, core, done)
            gifts[done].wait_recv()
            done += 1
        qkv.one(s, 0)
        if s == 0:
            for i in range(3):
                out.three(i, 1)
                out.one(i, 2)
    work = [(qkv, s) for s in range(3)] + [(gain, 0)]
    for q in range(3):
        for scatter, s in work:
            scatter.two(s, q)
        if q == 0:
            for s in range(3):
                out.two(s, 2)
        for scatter, s in work:
            scatter.three(s, q)
            if q < 2:
                scatter.one(s, q + 1)
        if q == 0:
            for s in range(3):
                out.three(s, 2)
    fins = []
    k = 0
    for scatter, ref in ((qkv, out_q), (out, out_o), (gain, out_g)):
        for s, (_, off, width) in enumerate(scatter.streams):
            part = scatter.acc[s][2].at[0]
            ref[core, :, pl.ds(off, width)] = scatter.acc[s][2][0]
            here, there = (ref.at[side, :, pl.ds(off, width)] for side in (core, 1 - core))
            pair = [pltpu.make_async_remote_copy(part, side, fin_send.at[k], fin_recv.at[k],
                                                 device_id=sibling, device_id_type=MESH) for side in (here, there)]
            pair[0].start()
            fins.append(pair)
            k += 1
    for mine, theirs in fins:
        mine.wait_send()
        theirs.wait_recv()
    for copy in gifts + [gain_gift]:
        copy.wait_send()
    for scatter, phases in ((qkv, (0, 1, 2)), (out, (1, 2)), (gain, (0, 1, 2))):
        for s in range(len(scatter.streams)):
            for q in phases:
                scatter.drain(s, q)


def scatter_grads(normed, d_qkv, own_g, sib_g, accs):
    bf, f32 = jnp.bfloat16, jnp.float32
    n_tok, model_dim = normed.shape
    half, rows = d_qkv.shape[1] // 2, 32
    blocks = model_dim // rows
    dma = pltpu.SemaphoreType.DMA
    vmem = pl.BlockSpec(memory_space=pltpu.VMEM)
    scratch = [pltpu.VMEM((model_dim, n_tok), bf), pltpu.VMEM((blocks, rows, half), f32),
               pltpu.VMEM((blocks, rows, half), bf), pltpu.VMEM((blocks, rows, half), bf), pltpu.VMEM(sib_g.shape, f32)]
    for streams, dtype, n_rows, phases in ((QKV, bf, rows, (0, 1, 2)), (OUT, bf, rows, (1, 2)), (GAIN, f32, 16, (0, 1, 2))):
        scratch += [pltpu.VMEM(*a) for a in acc_shapes(streams, n_rows, phases)]
        scratch += wire_shapes(streams, dtype, n_rows, phases) * 2
    scratch += [dma((len(st), 3, 4)) for st in (QKV, OUT, GAIN) for _ in range(2)]
    scratch += [dma((half // CHUNK,))] * 2 + [dma((2,))] + [dma((7,))] * 2
    return pl.pallas_call(
        scatter_kernel, name="scatter_grads",
        out_shape=[jax.ShapeDtypeStruct((2, rows, half), f32), jax.ShapeDtypeStruct((2, rows, 1024), f32),
                   jax.ShapeDtypeStruct((2, 16, 128), f32)],
        in_specs=[vmem] * 7, out_specs=[vmem] * 3, scratch_shapes=scratch,
        compiler_params=pltpu.CompilerParams(collective_id=2, has_side_effects=True, vmem_limit_bytes=VMEM_MAX),
    )(normed, d_qkv, own_g, sib_g, *accs)


LOG2E = 1.4426950408889634
TILE = 256


def nt(a, b):
    return lax.dot_general(a, b, (((1,), (1,)), ((), ())), preferred_element_type=jnp.float32)


def nn(a, b):
    return lax.dot_general(a, b, (((1,), (0,)), ((), ())), preferred_element_type=jnp.float32)


def fill_mask(mask, ids_k, ids_q):
    n_keys, n_q = mask.shape
    core = lax.axis_index('cp')
    for c in range(n_keys // TILE):
        base = jnp.where(c < n_q // TILE, (1 - core) * n_q, core * n_q - n_q) + c * TILE
        for i in range(n_q // TILE):
            k_at = base + lax.broadcasted_iota(jnp.int32, (TILE, TILE), 0)
            q_at = core * n_q + i * TILE + lax.broadcasted_iota(jnp.int32, (TILE, TILE), 1)
            same = ids_k[pl.ds(c * TILE, TILE), :] == ids_q[:, pl.ds(i * TILE, TILE)]
            mask[pl.ds(c * TILE, TILE), pl.ds(i * TILE, TILE)] = jnp.where(same & (k_at <= q_at), 1.0, 0.0)


def keys_for(i, n_q):
    return n_q + (i + 1) * TILE


def attend_kernel(ratio, q_ref, k_ref, v_ref, ids_k, ids_q, w_in, o_ref, inv_ref, w_ref, mask, v_t, w_scr, p_scr, *sems):
    n_q = q_ref.shape[0]
    greet(*place())
    out = Gather(OUT, None, w_ref, *sems)
    for s in range(3):
        out.start(s, 2)
    fill_mask(mask, ids_k, ids_q)
    v_t[...] = v_ref[...].T

    def head(h, carry):
        cols = pl.ds(pl.multiple_of(h * TILE, TILE), TILE)
        for i in range(n_q // TILE):
            qi = q_ref[pl.ds(i * TILE, TILE), cols]
            n_keys = keys_for(i, n_q)
            total = jnp.zeros((8, TILE), jnp.float32)
            for c in range(n_keys // TILE):
                t = jnp.tanh(nt(k_ref[pl.ds(c * TILE, TILE), :], qi) * ratio)
                w = jnp.exp2(t * (SOFT_CAP * LOG2E)) * mask[pl.ds(c * TILE, TILE), pl.ds(i * TILE, TILE)]
                w_scr[i, pl.ds(c * TILE, TILE), :] = w
                total = total + jnp.sum(w.reshape(TILE // 8, 8, TILE), axis=0)
            inv = 1.0 / jnp.sum(total, axis=0, keepdims=True)
            inv_ref[h, :, pl.ds(i * TILE, TILE)] = inv
            p_scr[i, pl.ds(0, n_keys), :] = (w_scr[i, pl.ds(0, n_keys), :] * inv).astype(jnp.bfloat16)
            o_t = nn(v_t[:, pl.ds(0, n_keys)], p_scr[i, pl.ds(0, n_keys), :])
            o_ref[pl.ds(i * TILE, TILE), cols] = o_t.T.astype(jnp.bfloat16)

        @pl.when(h == 4)
        def _():
            for s in range(3):
                out.middle(s, 2)
        return carry
    lax.fori_loop(0, q_ref.shape[1] // TILE, head, 0)
    for s in range(3):
        out.finish(s, 2)
    for s in range(3):
        out.drain(s, 2)


def attend(q, k, v, ids_k, ids_q, w_out, n_heads, ratio):
    n_q, n_k = q.shape[0], k.shape[0]
    vmem, hbm = pl.BlockSpec(memory_space=pltpu.VMEM), pl.BlockSpec(memory_space=pltpu.HBM)
    return pl.pallas_call(
        functools.partial(attend_kernel, ratio), name="attend",
        out_shape=[jax.ShapeDtypeStruct(q.shape, jnp.bfloat16), jax.ShapeDtypeStruct((n_heads, 1, n_q), jnp.float32),
                   jax.ShapeDtypeStruct(w_out.shape, w_out.dtype)],
        in_specs=[vmem] * 5 + [hbm], out_specs=[vmem] * 2 + [hbm], input_output_aliases={5: 2},
        scratch_shapes=[pltpu.VMEM((n_k, n_q), jnp.float32), pltpu.VMEM((TILE, n_k), jnp.bfloat16),
                        pltpu.VMEM((n_q // TILE, n_k, TILE), jnp.float32),
                        pltpu.VMEM((n_q // TILE, n_k, TILE), jnp.bfloat16)]
        + [pltpu.SemaphoreType.DMA((3, 3, 4))] * 4,
        compiler_params=pltpu.CompilerParams(collective_id=3, has_side_effects=True),
    )(q, k, v, ids_k, ids_q, w_out)


def attend_back_kernel(ratio, q_ref, do_ref, k_ref, v_ref, ids_k, ids_q, inv_ref, dz_ref, o_ref,
                       dq_ref, dk_ref, dv_ref, acc0, acc1, acc2,
                       mask, k_t, g_scr, dp_scr, p_scr, ds_scr, dk_acc, dv_acc, dz_t, own, sib_out, sib_in, *scratch):
    n_q = q_ref.shape[0]
    coords, core = place()
    greet(coords, core)
    sbuf, rbuf, sems = scratch[0:3], scratch[3:6], scratch[6:8]
    gift_send, gift_recv = scratch[8:10]
    out = Scatter(OUT, own, sib_in, [[a] for a in (acc0, acc1, acc2)], [[b] for b in sbuf], [[b] for b in rbuf], *sems)
    chunks = own.shape[2] // CHUNK
    transpose_into(dz_t, dz_ref)
    gifts = [chunk_gift(sib_out, sib_in, gift_send, gift_recv, j) for j in range(chunks)]
    for j in range(chunks):
        grad_chunk(dz_t, o_ref, sib_out, 1 - core, j)
        gifts[j].start()
    done = 0
    for s, (_, off, width) in enumerate(OUT):
        while done * CHUNK < off + width:
            grad_chunk(dz_t, o_ref, own, core, done)
            gifts[done].wait_recv()
            done += 1
        out.one(s, 0)
    fill_mask(mask, ids_k, ids_q)
    k_t[...] = k_ref[...].T
    dk_acc[...] = jnp.zeros_like(dk_acc)
    dv_acc[...] = jnp.zeros_like(dv_acc)

    def head(h, carry):
        cols = pl.ds(pl.multiple_of(h * TILE, TILE), TILE)
        for i in range(n_q // TILE):
            rows = pl.ds(i * TILE, TILE)
            qi, doi = q_ref[rows, cols], do_ref[rows, cols]
            inv = inv_ref[h, :, rows]
            n_keys = keys_for(i, n_q)
            total = jnp.zeros((8, TILE), jnp.float32)
            for c in range(n_keys // TILE):
                at = pl.ds(c * TILE, TILE)
                t = jnp.tanh(nt(k_ref[at, :], qi) * ratio)
                p = jnp.exp2(t * (SOFT_CAP * LOG2E)) * (mask[at, rows] * inv)
                dp = nt(v_ref[at, :], doi)
                p_scr[i, at, :] = p.astype(jnp.bfloat16)
                g_scr[i, at, :] = p * ((1.0 - t * t) * (ratio * SOFT_CAP))
                dp_scr[i, at, :] = dp
                total = total + jnp.sum((p * dp).reshape(TILE // 8, 8, TILE), axis=0)
            row_dot = jnp.sum(total, axis=0, keepdims=True)
            seen = pl.ds(0, n_keys)
            ds_scr[i, seen, :] = ((dp_scr[i, seen, :] - row_dot) * g_scr[i, seen, :]).astype(jnp.bfloat16)
            dq_t = nn(k_t[:, seen], ds_scr[i, seen, :])
            dq_ref[rows, cols] = dq_t.T.astype(jnp.bfloat16)
            dk_acc[seen, :] += nn(ds_scr[i, seen, :], qi)
            dv_acc[seen, :] += nn(p_scr[i, seen, :], doi)

        @pl.when(h == 3)
        def _():
            for s in range(3):
                out.two(s, 0)
        return carry
    lax.fori_loop(0, q_ref.shape[1] // TILE, head, 0)
    for s in range(3):
        out.three(s, 0)
    for s in range(3):
        out.drain(s, 0)
    for copy in gifts:
        copy.wait_send()
    dk_ref[...] = dk_acc[...].astype(jnp.bfloat16)
    dv_ref[...] = dv_acc[...].astype(jnp.bfloat16)


def attend_back(q, do, k, v, ids_k, ids_q, inv_sum, dz, o, n_heads, ratio):
    n_q, n_k = q.shape[0], k.shape[0]
    vmem = pl.BlockSpec(memory_space=pltpu.VMEM)
    tiles = n_q // TILE
    bf, f32 = jnp.bfloat16, jnp.float32
    return pl.pallas_call(
        functools.partial(attend_back_kernel, ratio), name="attend_back",
        out_shape=[jax.ShapeDtypeStruct(q.shape, bf)] + [jax.ShapeDtypeStruct(k.shape, bf)] * 2
        + [jax.ShapeDtypeStruct(*a) for a in acc_shapes(OUT, 32, (0,))],
        in_specs=[vmem] * 9, out_specs=[vmem] * 6,
        scratch_shapes=[pltpu.VMEM((n_k, n_q), f32), pltpu.VMEM((TILE, n_k), bf),
                        pltpu.VMEM((tiles, n_k, TILE), f32), pltpu.VMEM((tiles, n_k, TILE), f32),
                        pltpu.VMEM((tiles, n_k, TILE), bf), pltpu.VMEM((tiles, n_k, TILE), bf),
                        pltpu.VMEM((n_k, TILE), f32), pltpu.VMEM((n_k, TILE), f32),
                        pltpu.VMEM((dz.shape[1], n_q), bf), pltpu.VMEM((dz.shape[1] // 32, 32, o.shape[1] // 2), f32)]
        + [pltpu.VMEM((dz.shape[1] // 32, 32, o.shape[1] // 2), bf)] * 2
        + wire_shapes(OUT, bf, 32, (0,)) * 2 + [pltpu.SemaphoreType.DMA((3, 3, 4))] * 2
        + [pltpu.SemaphoreType.DMA((o.shape[1] // 2 // CHUNK,))] * 2,
        compiler_params=pltpu.CompilerParams(collective_id=4, has_side_effects=True, vmem_limit_bytes=VMEM_MAX),
    )(q, do, k, v, ids_k, ids_q, inv_sum, dz, o)


def rope_tables(pos_ids, head_dim):
    half_dim = head_dim // 2
    inv_freq = ROPE_BASE ** (-2.0 * jnp.arange(half_dim, dtype=jnp.float32) / head_dim)
    angles = pos_ids.astype(jnp.float32)[..., None] * inv_freq
    return jnp.cos(angles)[..., None, :], jnp.sin(angles)[..., None, :]


def rotate(values, cos_t, sin_t):
    half_dim = values.shape[-1] // 2
    first_half = values[..., :half_dim].astype(jnp.float32)
    second_half = values[..., half_dim:].astype(jnp.float32)
    rotated = jnp.concatenate([first_half * cos_t - second_half * sin_t,
                               second_half * cos_t + first_half * sin_t], axis=-1)
    return rotated.astype(jnp.bfloat16)


def norm_forward(values, gain_vec):
    values_f = values.astype(jnp.float32)
    inv_rms = lax.rsqrt(jnp.mean(values_f * values_f, axis=-1, keepdims=True) + NORM_EPS)
    normed = values_f * inv_rms * (1.0 + gain_vec.astype(jnp.float32))
    return normed.astype(jnp.bfloat16), inv_rms


def norm_backward(values, inv_rms, gain_vec, grads):
    values_f = values.astype(jnp.float32)
    grads_f = grads.astype(jnp.float32)
    scaled = grads_f * (1.0 + gain_vec.astype(jnp.float32))
    d_values = inv_rms * scaled - values_f * inv_rms ** 3 * jnp.mean(scaled * values_f, axis=-1, keepdims=True)
    d_gain = jnp.sum(grads_f * values_f * inv_rms, axis=0)
    return d_values, d_gain


def dot(a, b, dims):
    return lax.dot_general(a, b, ((dims[:1], dims[1:]), ((), ())), preferred_element_type=jnp.float32)


def solution(mesh):
    tok_spec = P('fsdp', 'cp', None)
    ids_spec = P('fsdp', 'cp')
    in_spec = P('fsdp', None, None)
    out_spec = P(None, None, 'fsdp')
    gain_spec = P('fsdp')
    bf, f32 = jnp.bfloat16, jnp.float32

    def layer_local(hidden, doc_ids, doc_pos, grad_out, w_query, w_key, w_value, w_out, gain_pre, gain_post):
        _, n_tok, model_dim = hidden.shape
        hidden, grad_out = hidden[0], grad_out[0]
        n_heads, head_dim = w_query.shape[1], w_query.shape[2]
        rows = w_query.shape[0]
        q_cols = n_heads * head_dim
        core = lax.axis_index('cp')
        w0 = jnp.concatenate([w_query.reshape(rows, q_cols), w_key.reshape(rows, head_dim),
                              w_value.reshape(rows, head_dim)], axis=1)
        w1 = w_out.reshape(q_cols, rows).T
        w2 = jnp.pad(jnp.stack([gain_pre, gain_post]).astype(f32), ((0, 0), (0, 128 - rows))).reshape(1, 256)
        w2 = jnp.pad(w2, ((0, 15), (0, 0)))
        wqkv, wo_t, gains = gather_weights(w0, w1, w2)
        gains = gains[..., 0, :].reshape(model_dim // rows, 256)
        pre_full, post_full = gains[:, :rows].reshape(model_dim), gains[:, 128:128 + rows].reshape(model_dim)
        wqkv = wqkv.reshape(model_dim, q_cols + 2 * head_dim)
        q_scale = (head_dim if head_dim >= 256 else model_dim // n_heads) ** -0.5

        normed, inv_pre = norm_forward(hidden, pre_full)
        qkv = dot(normed, wqkv, (1, 0)).astype(bf)
        q_proj = qkv[:, :q_cols].reshape(n_tok, n_heads, head_dim)
        k_proj = qkv[:, q_cols:q_cols + head_dim].reshape(n_tok, 1, head_dim)
        v_proj = qkv[:, q_cols + head_dim:]
        cos_t, sin_t = rope_tables(doc_pos[0], head_dim)
        q_rot = rotate(q_proj, cos_t, sin_t)
        k_rot = rotate(k_proj, cos_t, sin_t)[:, 0]

        swap = [(0, 1), (1, 0)]
        kv_own = jnp.concatenate([k_rot, v_proj], axis=1)
        kv_all = jnp.concatenate([lax.ppermute(kv_own, 'cp', swap), kv_own], axis=0)
        k_all, v_all = kv_all[:, :head_dim], kv_all[:, head_dim:]
        ids_all = jnp.concatenate([lax.ppermute(doc_ids[0], 'cp', swap), doc_ids[0]])[:, None]
        q_flat = q_rot.reshape(n_tok, q_cols)
        ratio = q_scale / SOFT_CAP
        attn_flat, inv_sum, wo_t = attend(q_flat, k_all, v_all, ids_all, doc_ids, wo_t, n_heads, ratio)
        wo_t = wo_t.reshape(model_dim, q_cols)
        proj_out = dot(attn_flat, wo_t, (1, 1)).astype(bf)
        post_out, inv_post = norm_forward(proj_out, post_full)
        out_hidden = (hidden.astype(f32) + post_out.astype(f32)).astype(bf)

        d_proj, d_gain_post = norm_backward(proj_out, inv_post, post_full, grad_out)
        d_proj = d_proj.astype(bf)
        d_attn = dot(d_proj, wo_t, (1, 0)).astype(bf)

        d_q_flat, d_k, d_v, *accs = attend_back(q_flat, d_attn, k_all, v_all, ids_all, doc_ids, inv_sum, d_proj, attn_flat,
                                                n_heads, ratio)
        d_kv = jnp.concatenate([d_k, d_v], axis=1)
        d_kv = (d_kv[n_tok:].astype(f32) + lax.ppermute(d_kv[:n_tok], 'cp', swap).astype(f32)).astype(bf)
        d_k_rot, d_v_proj = d_kv[:, :head_dim], d_kv[:, head_dim:]
        d_q_rot = d_q_flat.reshape(n_tok, n_heads, head_dim)
        d_q_proj = rotate(d_q_rot, cos_t, -sin_t)
        d_k_proj = rotate(d_k_rot[:, None], cos_t, -sin_t)[:, 0]
        d_qkv = jnp.concatenate([d_q_proj.reshape(n_tok, q_cols), d_k_proj, d_v_proj], axis=1)

        d_normed = dot(d_qkv, wqkv, (1, 1)).astype(bf)
        d_hidden, d_gain_pre = norm_backward(hidden, inv_pre, pre_full, d_normed)
        grad_hidden = (grad_out.astype(f32) + d_hidden).astype(bf)
        d_gains = jnp.stack([d_gain_pre, d_gain_post]).reshape(2, model_dim // rows, 1, rows)
        d_gains = jnp.pad(d_gains, ((0, 0), (0, 0), (0, 15), (0, 128 - rows)))
        own_g = lax.dynamic_index_in_dim(d_gains, core, 0, keepdims=False)
        sib_g = lax.dynamic_index_in_dim(d_gains, 1 - core, 0, keepdims=False)
        g0, g1, gg = scatter_grads(normed, d_qkv, own_g, sib_g, accs)
        g0 = jnp.concatenate([g0[0], g0[1]], axis=1)
        g1 = jnp.concatenate([g1[0], g1[1]], axis=1)
        return (out_hidden[None], grad_hidden[None], g0[:, :q_cols].reshape(rows, n_heads, head_dim),
                g0[:, q_cols:q_cols + head_dim].reshape(rows, 1, head_dim),
                g0[:, q_cols + head_dim:].reshape(rows, 1, head_dim),
                g1.T.reshape(n_heads, head_dim, rows), gg[0, 0, :rows], gg[1, 0, :rows])

    return jax.shard_map(layer_local, mesh=mesh,
                         in_specs=(tok_spec, ids_spec, ids_spec, tok_spec, in_spec, in_spec, in_spec, out_spec, gain_spec, gain_spec),
                         out_specs=(tok_spec, tok_spec, in_spec, in_spec, in_spec, out_spec, gain_spec, gain_spec),
                         check_vma=False)
```

time: 296 us -> 271 us (0.916)
  matrix products: 59.4 us -> 34.3 us
  other arithmetic: 29.6 us -> 26 us
    dot_general x8 -> x4, matrix products: 59.4 us -> 34.3 us  [dot(): lax.dot_general(a, b, ((dims[:1], dims[1:]), ((), ())), preferred_element...]
    pallas_call x1, Pallas kernels: 23 us -> 41.1 us  [attend_back(): pl.pallas_call(functools.partial(attend_back_kernel, ratio), name='attend...]
    pallas_call x1, Pallas kernels: 76.9 us -> 59 us  [scatter_grads(): pl.pallas_call(scatter_kernel, name='scatter_grads', out_shape=[jax.Shape...]
    pallas_call x1, Pallas kernels: 14.8 us -> 25.4 us  [attend(): pl.pallas_call(functools.partial(attend_kernel, ratio), name='attend', ou...]
    pallas_call x1, Pallas kernels: 58 us -> 49.9 us  [gather_weights(): pl.pallas_call(gather_kernel, name='gather_weights', out_shape=shapes, in...]
    convert_element_type x0 -> x2, other arithmetic: none -> 6.72 us  [the longest x1 3.78 us: norm_forward(): return (normed.astype(jnp.bfloat16), inv_rms)]
    broadcast_in_dim x1 -> x0, other arithmetic: 4.98 us -> none  [layer_local(): grad_hidden[None]]
    reduce_sum x2 -> x1, other arithmetic: 6.54 us -> 2.02 us  [norm_backward(): d_gain = jnp.sum(grads_f * values_f * inv_rms, axis=0)]
  transfers between devices with their start and end apart: 3 -> 3, of which waited for: 0 -> 0; matrix products, arithmetic and copies ran while one was open for 8% -> 12% of each run, Pallas kernels for 0% -> 19%
where the time goes in v3:
time: 271 us; the launch traced here: 266 us
  Pallas kernels  175 us (65%)
  matrix products  34.3 us (13%)
  local copies, waits for them, and re-layouts  26.4 us (10%)
  other arithmetic  26 us (10%)
  starting transfers between devices  2.87 us (1%)
    pallas_call x1, Pallas kernels, scatter_grads(): pl.pallas_call(scatter_kernel, name='scatter_grads', out_shape=[jax.Shape...  59 us
    pallas_call x1, Pallas kernels, gather_weights(): pl.pallas_call(gather_kernel, name='gather_weights', out_shape=shapes, in...  49.9 us
    pallas_call x1, Pallas kernels, attend_back(): pl.pallas_call(functools.partial(attend_back_kernel, ratio), name='attend...  41.1 us
    dot_general x4, matrix products, dot(): lax.dot_general(a, b, ((dims[:1], dims[1:]), ((), ())), preferred_element...  34.3 us
    pallas_call x1, Pallas kernels, attend(): pl.pallas_call(functools.partial(attend_kernel, ratio), name='attend', ou...  25.4 us
    unnamed x58, local copies, waits for them, and re-layouts  13.2 us
  transfers between devices with their start and end apart: 3, of which 0 were waited for; matrix products, arithmetic and copies ran while one was open for 12% of the time, Pallas kernels for 19%

profile of v3, /device:TPU:1, one launch (start us, length us, event | category | flops | bytes accessed | tf_op | source)
XLA Modules:
  0.0 266.3 jit_solution(9880082652884888792)
XLA Ops:
  0.7 1.4 collective-permute-start.1
  2.1 0.7 fusion.68
  2.8 0.7 convert_element_type.134
  3.5 2.1 fusion.11
  6.8 0.9 copy.34
  7.7 1.6 copy.33
  9.3 0.7 pad_maximum_fusion.6.in0
  10.0 49.9 %gather_weights.1 = (bf16[4,4,4,32,2560]{4,3,2,1,0:T(8,128)(2,1)}, bf16[4,4,4,32,2048]{4,3,2,1,0:T(8,128)(2,1)}, f32[4,4,4,16,256]{4,3,2,1,0:T(8,128)}) custom-call(bf16[32,2560]{1,0:T(8,128)(2,1)} %pad_maximum_fusion.6.in0, bf16[32,2048]{1,0:T(8,128)(2,1)} %bitcast.139, f32[16,256]{1,0:T(8,128)} %pad_convert_fusion.in2), custom_call_target="tpu_custom_call" | custom-call | tf_op jit(solution)/shard_map/gather_weights/pallas_call | solution.py:151
  59.9 1.2 slice_reduce_fusion
  61.8 8.4 %convolution_convert_fusion = bf16[512,2560]{1,0:T(8,128)(2,1)S(1)} fusion(bf16[2048,2560]{1,0:T(8,128)(2,1)} %bitcast.154, bf16[1,512,2048]{2,1,0:T(8,128)(2,1)S(1)} %copy-done.2, f32[2048]{0:T(1024)S(1)} %add.81, f32[512]{0:T(512)S(1)} %get-tuple-element.92), kind=kOutput, calls=%fused_computation.18 | convolution fusion | flops 5374214144 | bytes 15214592 | tf_op jit(solution)/shard_map/dot_general | solution.py:606
  70.3 1.2 fusion.61
  72.0 1.8 fusion.64
  74.0 0.7 copy.36
  74.7 0.7 fusion.30
  75.4 1.5 pad_maximum_fusion.1
  77.0 3.6 %copy.37 = bf16[64,8,8,256]{3,1,2,0:T(8,128)(2,1)} copy(bf16[64,8,8,256]{3,2,1,0:T(8,128)(2,1)} %bitcast.132) | data formatting | bytes 4194304
  80.7 1.1 copy.24.ids_k
  81.8 1.1 maximum_maximum_fusion
  82.9 1.0 fusion.69
  83.9 25.4 %attend.1 = (bf16[512,2048]{1,0:T(8,128)(2,1)}, f32[8,1,512]{2,1,0:T(1,128)}, bf16[4,4,4,32,2048]{4,3,2,1,0:T(8,128)(2,1)}) custom-call(bf16[512,2048]{1,0:T(8,128)(2,1)} %bitcast.125, bf16[1024,256]{1,0:T(8,128)(2,1)} %get-tuple-element.71.k_ref, bf16[1024,256]{1,0:T(8,128)(2,1)} %get-tuple-element.70.v_ref, ...), custom_call_target="tpu_custom_call", output_to_operand_aliasing={{2}: (5, {})} | custom-call | tf_op jit(solution)/shard_map/attend/pallas_call | solution.py:470
  109.4 8.8 %fusion.22 = (f32[512]{0:T(512)S(1)}, bf16[512,2048]{1,0:T(8,128)(2,1)S(1)}) fusion(bf16[512,2048]{1,0:T(8,128)(2,1)} %get-tuple-element.26.o_ref, bf16[2048,2048]{1,0:T(8,128)(2,1)} %bitcast.127), kind=kOutput, calls=%fused_computation.33 | convolution fusion | flops 4299161088 | bytes 12584960 | tf_op jit(solution)/shard_map/dot_general | solution.py:606
  118.2 2.0 fusion.28
  120.2 2.9 %fusion.9 = (bf16[512,2048]{1,0:T(8,128)(2,1)S(1)}, bf16[1,512,2048]{2,1,0:T(8,128)(2,1)}) fusion(bf16[512,2048]{1,0:T(8,128)(2,1)S(1)} %get-tuple-element.96, bf16[1,512,2048]{2,1,0:T(8,128)(2,1)S(1)} %copy-done, f32[512]{0:T(512)S(1)} %broadcast_multiply_fusion.1, f32[512]{0:T(512)S(1)} %get-tuple-element.93, f32[2048]{0:T(1024)S(1)} %add.86, ...), kind=kLoop, calls=%fused_computation.20 | loop fusion | flops 15728640 | bytes 10500096 | tf_op jit(solution)/shard_map/convert_element_type | solution.py:658
  123.1 1.7 copy-done.4
  124.8 5.9 %convolution_convert_fusion.1.do_ref = bf16[512,2048]{1,0:T(8,128)(2,1)} fusion(bf16[512,2048]{1,0:T(8,128)(2,1)S(1)} %get-tuple-element.66.dz_ref, bf16[2048,2048]{1,0:T(8,128)(2,1)S(1)} %bitcast.128), kind=kOutput, calls=%fused_computation.40 | convolution fusion | flops 4296015872 | bytes 12582912 | tf_op jit(solution)/shard_map/dot_general | solution.py:606
  130.7 41.1 %attend_back.1 = (bf16[512,2048]{1,0:T(8,128)(2,1)}, bf16[1024,256]{1,0:T(8,128)(2,1)}, bf16[1024,256]{1,0:T(8,128)(2,1)}, f32[16,32,256]{2,1,0:T(8,128)}, f32[1...) custom-call(bf16[512,2048]{1,0:T(8,128)(2,1)} %bitcast.126, bf16[512,2048]{1,0:T(8,128)(2,1)} %convolution_convert_fusion.1.do_ref, ...), custom_call_target="tpu_custom_call" | custom-call | tf_op jit(solution)/shard_map/attend_back/pallas_call | solution.py:556
  171.8 1.2 constant_dynamic-update-slice_fusion.1
  173.1 1.1 constant_dynamic-update-slice_fusion
  174.2 0.8 slice.130
  175.0 1.0 collective-permute-start.2
  176.1 0.7 copy.38
  177.0 0.7 fusion.34
  178.0 0.7 copy.39
  178.7 1.3 add_convert_fusion
  180.1 1.5 fusion.63
  181.6 11.2 %fusion.18 = (f32[2048]{0:T(1024)S(1)}, f32[512]{0:T(512)S(1)}, bf16[512,2048]{1,0:T(8,128)(2,1)}) fusion(bf16[1,512,2048]{2,1,0:T(8,128)(2,1)S(1)} %copy-done.3, f32[512]{0:T(512)S(1)} %copy-done.21, f32[2048]{0:T(1024)S(1)} %copy-done.14, bf16[2048,2560]{1,0:T(8,128)(2,1)} %bitcast.155, bf16[512,256]{1,0:T(8,128)(2,1)S(1)} %get-tuple-element.73, ...), kind=kOutput, calls=%fused_computation.29 | convolution fusion | flops 5388629504 | bytes 17321984 | tf_op jit(solution)/shard_map/dot_general | solution.py:606
  192.8 1.6 pad_maximum_fusion.d_qkv
  194.7 1.6 copy_bitcast_fusion
  196.3 0.7 copy-done.9
  197.1 3.8 %fusion.16 = (bf16[512,2048]{1,0:T(8,128)(2,1)}, bf16[1,512,2048]{2,1,0:T(8,128)(2,1)}) fusion(bf16[1,512,2048]{2,1,0:T(8,128)(2,1)S(1)} %copy-done.3, f32[2048]{0:T(1024)S(1)} %copy-done.14, f32[512]{0:T(512)S(1)} %copy-done.21, f32[512]{0:T(512)S(1)} %broadcast_multiply_fusion, f32[512]{0:T(512)S(1)} %copy-done.19, bf16[512,2048]{1,0:T(8,128)(2,1)S(1)} %copy-done.9, ...), kind=kLoop, calls=%fused_computation.27 | loop fusion | flops 13631488 | bytes 10500096 | tf_op jit(solution)/shard_map/convert_element_type | solution.py:593
  200.9 59.0 %scatter_grads.1 = (f32[2,32,1280]{2,1,0:T(8,128)}, f32[2,32,1024]{2,1,0:T(8,128)}, f32[2,16,128]{2,1,0:T(8,128)}) custom-call(bf16[512,2048]{1,0:T(8,128)(2,1)} %get-tuple-element.64.normed, bf16[512,2560]{1,0:T(8,128)(2,1)} %pad_maximum_fusion.d_qkv, f32[64,16,128]{2,1,0:T(8,128)} %get-tuple-element.99.own_g, f32[64,16,128]{2,1,0:T(8,128)} %get-tuple-element.98.sib_g, ...), custom_call_target="tpu_custom_call" | custom-call | tf_op jit(solution)/shard_map/scatter_grads/pallas_call | solution.py:392
  259.8 1.0 slice_bitcast_fusion.3
  260.9 1.2 slice_bitcast_fusion.8
  262.1 0.8 copy.40
  262.9 0.6 copy.29
  263.5 0.6 copy.28
  264.2 1.0 slice_bitcast_fusion.5
  265.2 0.7 copy.45
  (74 shorter events, 3.8 us)
Async XLA Ops:
  0.6 61.2 %copy-start.2 = (bf16[1,512,2048]{2,1,0:T(8,128)(2,1)S(1)}, bf16[1,512,2048]{2,1,0:T(8,128)(2,1)}, u32[]{:S(2)}) copy-start(bf16[1,512,2048]{2,1,0:T(8,128)(2,1)} %param.10) | copy-start | bytes 6291460
  0.6 8.6 %copy-start.17 = (bf16[32,1,256]{2,0,1:T(8,128)(2,1)S(1)}, bf16[32,1,256]{2,0,1:T(8,128)(2,1)}, u32[]{:S(2)}) copy-start(bf16[32,1,256]{2,0,1:T(8,128)(2,1)} %param.16) | copy-start | bytes 49156
  0.7 8.6 %copy-start.18 = (bf16[32,1,256]{2,0,1:T(8,128)(2,1)S(1)}, bf16[32,1,256]{2,0,1:T(8,128)(2,1)}, u32[]{:S(2)}) copy-start(bf16[32,1,256]{2,0,1:T(8,128)(2,1)} %param.15) | copy-start | bytes 49156
  0.7 80.0 %collective-permute-start.1 = (s32[512]{0:T(512)}, s32[512]{0:T(512)S(1)}, u32[]{:S(2)}, u32[]{:S(2)}) collective-permute-start(s32[512]{0:T(512)} %bitcast.148), channel_id=1, source_target_pairs={{0,1},{1,0},{2,3},{3,2},{4,5},{5,4},{6,7},{7,6},{8,9},{9,8},{10,11... | collective-permute-start | bytes 6152 | tf_op jit(solution)/shard_map/ppermute | solution.py:648
  2.1 69.9 %copy-start.22 = (f32[128]{0:T(128)}, f32[128]{0:T(128)S(1)}, u32[]{:S(2)}) copy-start(f32[128]{0:T(128)S(1)} %multiply_power_fusion) | copy-start | bytes 1540
  3.5 68.5 %copy-start.11 = (f32[1,512]{1,0:T(1,128)}, f32[1,512]{1,0:T(1,128)S(1)}, u32[]{:S(2)}) copy-start(f32[1,512]{1,0:T(1,128)S(1)} %convert_element_type.134) | copy-start | bytes 6148
  6.2 55.0 %copy-start.20 = (f32[512]{0:T(512)}, f32[512]{0:T(512)S(1)}, u32[]{:S(2)}) copy-start(f32[512]{0:T(512)S(1)} %get-tuple-element.92) | copy-start | bytes 6148
  61.2 0.6 copy-start.13
  71.6 10.2 %collective-permute-start = (bf16[512,512]{1,0:T(8,128)(2,1)S(1)}, bf16[512,512]{1,0:T(8,128)(2,1)}, u32[]{:S(2)}, u32[]{:S(2)}) collective-permute-start(bf16[512,512]{1,0:T(8,128)(2,1)S(1)} %pad_maximum_fusion.3), channel_id=1, source_target_pairs={{0,1},{1,0},{2,3},{3,2},{4,5},{5,4},{6,7},{7,6},{8,9},{9,8},{10,11... | collective-permute-start | bytes 1572872 | tf_op jit(solution)/shard_map/ppermute | solution.py:646
  73.8 0.9 copy-start.6
  77.0 3.7 %copy-start.16 = (s32[1,512]{1,0:T(1,128)S(1)}, s32[1,512]{1,0:T(1,128)}, u32[]{:S(2)}) copy-start(s32[1,512]{1,0:T(1,128)} %ids_q.3) | copy-start | bytes 6148
  109.4 8.8 %copy-start = (bf16[1,512,2048]{2,1,0:T(8,128)(2,1)S(1)}, bf16[1,512,2048]{2,1,0:T(8,128)(2,1)}, u32[]{:S(2)}) copy-start(bf16[1,512,2048]{2,1,0:T(8,128)(2,1)} %param.13) | copy-start | bytes 6291460
  120.2 4.6 %copy-start.4 = (bf16[4,4,4,32,2048]{4,3,2,1,0:T(8,128)(2,1)S(1)}, bf16[4,4,4,32,2048]{4,3,2,1,0:T(8,128)(2,1)}, u32[]{:S(2)}) copy-start(bf16[4,4,4,32,2048]{4,3,2,1,0:T(8,128)(2,1)} %get-tuple-element.27) | copy-start | bytes 25165828
  123.1 7.6 %copy-start.5 = (bf16[512,2048]{1,0:T(8,128)(2,1)}, bf16[512,2048]{1,0:T(8,128)(2,1)S(1)}, u32[]{:S(2)}) copy-start(bf16[512,2048]{1,0:T(8,128)(2,1)S(1)} %get-tuple-element.66.dz_ref) | copy-start | bytes 6291460
  171.8 4.2 %copy-start.15 = (f32[2048]{0:T(1024)S(1)}, f32[2048]{0:T(1024)}, u32[]{:S(2)}) copy-start(f32[2048]{0:T(1024)} %get-tuple-element.56) | copy-start | bytes 24580
  171.8 4.2 %copy-start.8 = (bf16[512,2048]{1,0:T(8,128)(2,1)S(1)}, bf16[512,2048]{1,0:T(8,128)(2,1)}, u32[]{:S(2)}) copy-start(bf16[512,2048]{1,0:T(8,128)(2,1)} %get-tuple-element.29) | copy-start | bytes 6291460
  174.2 2.6 copy-start.7
  175.0 3.7 %collective-permute-start.2 = (bf16[512,512]{1,0:T(8,128)(2,1)}, bf16[512,512]{1,0:T(8,128)(2,1)}, u32[]{:S(2)}, u32[]{:S(2)}) collective-permute-start(bf16[512,512]{1,0:T(8,128)(2,1)} %slice.130), channel_id=1, source_target_pairs={{0,1},{1,0},{2,3},{3,2},{4,5},{5,4},{6,7},{7,6},{8,9},{9,8},{10,11... | collective-permute-start | bytes 1572872 | tf_op jit(solution)/shard_map/ppermute | solution.py:664
  176.1 1.0 copy-start.10
  178.0 2.1 copy-start.12
  178.0 2.1 copy-start.23
  178.7 2.9 %copy-start.3 = (bf16[1,512,2048]{2,1,0:T(8,128)(2,1)S(1)}, bf16[1,512,2048]{2,1,0:T(8,128)(2,1)}, u32[]{:S(2)}) copy-start(bf16[1,512,2048]{2,1,0:T(8,128)(2,1)} %param.10) | copy-start | bytes 6291460
  178.7 2.9 %copy-start.14 = (f32[2048]{0:T(1024)S(1)}, f32[2048]{0:T(1024)}, u32[]{:S(2)}) copy-start(f32[2048]{0:T(1024)} %copy-done.13) | copy-start | bytes 24580
  178.7 2.9 %copy-start.21 = (f32[512]{0:T(512)S(1)}, f32[512]{0:T(512)}, u32[]{:S(2)}) copy-start(f32[512]{0:T(512)} %copy-done.20) | copy-start | bytes 6148
  194.5 1.9 copy-start.1
  194.5 2.6 copy-start.9
  194.5 2.6 copy-start.19

commit v4 on v3

--- a/solution.py
+++ b/solution.py
@@ -14,7 +14,8 @@
 SIDE = 4
 VMEM_MAX = 67_043_328
 
-QKV = ((0, 0, 512), (1, 512, 384), (2, 896, 384))
+QKV_IN = ((0, 0, 256), (1, 512, 256), (2, 896, 256), (0, 256, 256), (1, 768, 128), (2, 1152, 128))
+QKV = ((0, 0, 256), (0, 256, 256), (1, 512, 256), (1, 768, 128), (2, 896, 256), (2, 1152, 128))
 OUT = ((0, 0, 256), (1, 256, 384), (2, 640, 384))
 GAIN = ((0, 0, 128),)
 CHUNK = 256
@@ -114,48 +115,6 @@
             self.hop(s, p, kind).wait_send()
             self.gift(s, p, kind, self.core).wait_send()
             self.gift(s, p, kind, 1 - self.core).wait_recv()
-
-
-def gather_kernel(in0, in1, in2, out0, out1, out2, *sems):
-    coords, core = place()
-    greet(coords, core)
-    own_sem = sems[12]
-    ins, outs = (in0, in1, in2), (out0, out1, out2)
-    owns = [pltpu.make_async_copy(ins[g], outs[g].at[coords[0], coords[1], coords[2]], own_sem.at[g]) for g in range(3)]
-    for copy in owns:
-        copy.start()
-    qkv, out, gain = (Gather(st, ins[g], outs[g], *sems[4 * g:4 * g + 4]) for g, st in enumerate((QKV, OUT, GAIN)))
-    work = [(gain, 0)] + [(qkv, s) for s in range(3)] + [(out, s) for s in range(3)]
-    for p in range(3):
-        if p == 1:
-            for copy in owns:
-                copy.wait()
-        for gather, s in work:
-            if p > 0:
-                gather.finish(s, p - 1)
-            if p < 2 or gather is not out:
-                gather.start(s, p)
-        for gather, s in work:
-            if p < 2 or gather is not out:
-                gather.middle(s, p)
-    for gather, s in work[:4]:
-        gather.finish(s, 2)
-    for gather, s in work:
-        for p in range(2 if gather is out else 3):
-            gather.drain(s, p)
-
-
-def gather_weights(*ws):
-    shapes = [jax.ShapeDtypeStruct((SIDE, SIDE, SIDE) + w.shape, w.dtype) for w in ws]
-    dma = pltpu.SemaphoreType.DMA
-    return pl.pallas_call(
-        gather_kernel, name="gather_weights",
-        out_shape=shapes,
-        in_specs=[pl.BlockSpec(memory_space=pltpu.VMEM)] * 3,
-        out_specs=[pl.BlockSpec(memory_space=pltpu.HBM)] * 3,
-        scratch_shapes=[dma((len(st), 3, 4)) for st in (QKV, OUT, GAIN) for _ in range(4)] + [dma((3,))],
-        compiler_params=pltpu.CompilerParams(collective_id=1, has_side_effects=True),
-    )(*ws)
 
 
 class Scatter:
@@ -294,7 +253,8 @@
         del scratch[:n]
         return head
     normed_t, own_q, sib_out, sib_q, sib_in_g = take(5)
-    acc_q, sbuf_q, rbuf_q = take(9), take(9), take(9)
+    nq = len(QKV)
+    acc_q, sbuf_q, rbuf_q = take(3 * nq), take(3 * nq), take(3 * nq)
     acc_o, sbuf_o, rbuf_o = take(6), take(6), take(6)
     acc_g, sbuf_g, rbuf_g = take(3), take(3), take(3)
     sems = take(6)
@@ -338,7 +298,7 @@
             for i in range(3):
                 out.three(i, 1)
                 out.one(i, 2)
-    work = [(qkv, s) for s in range(3)] + [(gain, 0)]
+    work = [(qkv, s) for s in range(nq)] + [(gain, 0)]
     for q in range(3):
         for scatter, s in work:
             scatter.two(s, q)
@@ -388,7 +348,7 @@
         scratch += [pltpu.VMEM(*a) for a in acc_shapes(streams, n_rows, phases)]
         scratch += wire_shapes(streams, dtype, n_rows, phases) * 2
     scratch += [dma((len(st), 3, 4)) for st in (QKV, OUT, GAIN) for _ in range(2)]
-    scratch += [dma((half // CHUNK,))] * 2 + [dma((2,))] + [dma((7,))] * 2
+    scratch += [dma((half // CHUNK,))] * 2 + [dma((2,))] + [dma((len(QKV) + 4,))] * 2
     return pl.pallas_call(
         scatter_kernel, name="scatter_grads",
         out_shape=[jax.ShapeDtypeStruct((2, rows, half), f32), jax.ShapeDtypeStruct((2, rows, 1024), f32),
@@ -410,7 +370,7 @@
     return lax.dot_general(a, b, (((1,), (0,)), ((), ())), preferred_element_type=jnp.float32)
 
 
-def fill_mask(mask, ids_k, ids_q):
+def fill_mask(mask, pos):
     n_keys, n_q = mask.shape
     core = lax.axis_index('cp')
     for c in range(n_keys // TILE):
@@ -418,69 +378,174 @@
         for i in range(n_q // TILE):
             k_at = base + lax.broadcasted_iota(jnp.int32, (TILE, TILE), 0)
             q_at = core * n_q + i * TILE + lax.broadcasted_iota(jnp.int32, (TILE, TILE), 1)
-            same = ids_k[pl.ds(c * TILE, TILE), :] == ids_q[:, pl.ds(i * TILE, TILE)]
-            mask[pl.ds(c * TILE, TILE), pl.ds(i * TILE, TILE)] = jnp.where(same & (k_at <= q_at), 1.0, 0.0)
+            seen = (k_at <= q_at) & (k_at >= q_at - pos[:, pl.ds(i * TILE, TILE)])
+            mask[pl.ds(c * TILE, TILE), pl.ds(i * TILE, TILE)] = jnp.where(seen, 1.0, 0.0)
 
 
 def keys_for(i, n_q):
     return n_q + (i + 1) * TILE
 
 
-def attend_kernel(ratio, q_ref, k_ref, v_ref, ids_k, ids_q, w_in, o_ref, inv_ref, w_ref, mask, v_t, w_scr, p_scr, *sems):
-    n_q = q_ref.shape[0]
-    greet(*place())
-    out = Gather(OUT, None, w_ref, *sems)
-    for s in range(3):
+def forward_kernel(ratio, x_ref, cos_ref, sin_ref, pos, in0, in1, in2,
+                   wq_out, wo_out, gain_out, normed, inv_rms, q_ref, kv_ref, o_ref, inv_ref,
+                   wq, gains, gain_row, mask, v_t, w_scr, p_scr, *sems):
+    n_q, dim = x_ref.shape
+    bf, f32 = jnp.bfloat16, jnp.float32
+    coords, core = place()
+    sibling = device(coords, 1 - core)
+    greet(coords, core)
+    own_sem, swap_send, swap_recv = sems[12:15]
+    qkv, out, gain = (Gather(st, src, dst, *sems[4 * g:4 * g + 4]) for g, (st, src, dst) in enumerate(
+        ((QKV_IN, in0, wq), (OUT, in1, wo_out), (GAIN, in2, gains))))
+    nq = range(len(QKV_IN))
+    gain.start(0, 0)
+    for s in nq:
+        qkv.start(s, 0)
+    for s in range(3):
+        out.start(s, 0)
+    own_out = pltpu.make_async_copy(in1, wo_out.at[coords[0], coords[1], coords[2]], own_sem.at[0])
+    own_out.start()
+    wq[coords[0], coords[1], coords[2]] = in0[...]
+    gains[coords[0], coords[1], coords[2]] = in2[...]
+
+    def stats(i, carry):
+        at = pl.ds(i * 64, 64)
+        v = x_ref[at, :].astype(f32)
+        inv_rms[at, :] = lax.rsqrt(jnp.sum(v * v, axis=1, keepdims=True) * (1.0 / dim) + NORM_EPS)
+        return carry
+    lax.fori_loop(0, n_q // 64, stats, 0)
+    gain.middle(0, 0)
+    for s in nq:
+        qkv.middle(s, 0)
+    gain.finish(0, 0)
+    gain.start(0, 1)
+    for s in nq:
+        qkv.finish(s, 0)
+        qkv.start(s, 1)
+    for s in range(3):
+        out.middle(s, 0)
+    gain.middle(0, 1)
+    for s in nq:
+        qkv.middle(s, 1)
+    gain.finish(0, 1)
+    gain.start(0, 2)
+    for s in range(3):
+        out.finish(s, 0)
+    own_out.wait()
+    for s in nq:
+        qkv.finish(s, 1)
+        qkv.start(s, 2)
+    for s in range(3):
+        out.start(s, 1)
+    gain.middle(0, 2)
+    gain.finish(0, 2)
+    for p in range(3):
+        gain.drain(0, p)
+    for kind in range(2):
+        for j in range(16):
+            row = sum(gains[j // 4, j % 4, x, pl.ds(0, 1), pl.ds(kind * 128, 128)] for x in range(SIDE))
+            gain_row[pl.ds(kind, 1), pl.ds(j * 128, 128)] = row
+    gain_out[...] = gain_row[...]
+    fill_mask(mask, pos)
+
+    def scale(i, carry):
+        at = pl.ds(i * 64, 64)
+        normed[at, :] = (x_ref[at, :].astype(f32) * inv_rms[at, :] * (1.0 + gain_row[pl.ds(0, 1), :])).astype(bf)
+        return carry
+    lax.fori_loop(0, n_q // 64, scale, 0)
+    for s in nq:
+        qkv.middle(s, 2)
+    for s in range(3):
+        out.middle(s, 1)
+    for s in nq:
+        qkv.finish(s, 2)
+    for s in range(3):
+        out.finish(s, 1)
         out.start(s, 2)
-    fill_mask(mask, ids_k, ids_q)
-    v_t[...] = v_ref[...].T
+    for s in nq:
+        for p in range(3):
+            qkv.drain(s, p)
+    keep = pltpu.make_async_copy(wq, wq_out, own_sem.at[1])
+    keep.start()
+
+    def project(n):
+        rhs = wq[:, :, :, :, pl.ds(pl.multiple_of(n * TILE, TILE), TILE)].reshape(dim, TILE)
+        return nn(normed[...], rhs).astype(bf)
+
+    def rope(u):
+        lo, hi = u[:, :TILE // 2].astype(f32), u[:, TILE // 2:].astype(f32)
+        c, s = cos_ref[...], sin_ref[...]
+        return jnp.concatenate([lo * c - hi * s, hi * c + lo * s], axis=1).astype(bf)
+    n_heads = q_ref.shape[1] // TILE
+    mine, other = pl.ds(n_q, n_q), pl.ds(0, n_q)
+    kv_ref[mine, pl.ds(0, TILE)] = rope(project(n_heads))
+    kv_ref[mine, pl.ds(TILE, TILE)] = project(n_heads + 1)
+    swap = pltpu.make_async_remote_copy(kv_ref.at[mine], kv_ref.at[other], swap_send.at[0], swap_recv.at[0],
+                                        device_id=sibling, device_id_type=MESH)
+    swap.start()
+
+    def project_head(h, carry):
+        q_ref[:, pl.ds(pl.multiple_of(h * TILE, TILE), TILE)] = rope(project(h))
+        return carry
+    lax.fori_loop(0, n_heads, project_head, 0)
+    for s in range(3):
+        out.middle(s, 2)
+    swap.wait_recv()
+    k_cols = pl.ds(0, TILE)
+    v_t[...] = kv_ref[:, pl.ds(TILE, TILE)].T
 
     def head(h, carry):
         cols = pl.ds(pl.multiple_of(h * TILE, TILE), TILE)
         for i in range(n_q // TILE):
             qi = q_ref[pl.ds(i * TILE, TILE), cols]
             n_keys = keys_for(i, n_q)
-            total = jnp.zeros((8, TILE), jnp.float32)
+            total = jnp.zeros((8, TILE), f32)
             for c in range(n_keys // TILE):
-                t = jnp.tanh(nt(k_ref[pl.ds(c * TILE, TILE), :], qi) * ratio)
+                t = jnp.tanh(nt(kv_ref[pl.ds(c * TILE, TILE), k_cols], qi) * ratio)
                 w = jnp.exp2(t * (SOFT_CAP * LOG2E)) * mask[pl.ds(c * TILE, TILE), pl.ds(i * TILE, TILE)]
                 w_scr[i, pl.ds(c * TILE, TILE), :] = w
                 total = total + jnp.sum(w.reshape(TILE // 8, 8, TILE), axis=0)
             inv = 1.0 / jnp.sum(total, axis=0, keepdims=True)
             inv_ref[h, :, pl.ds(i * TILE, TILE)] = inv
-            p_scr[i, pl.ds(0, n_keys), :] = (w_scr[i, pl.ds(0, n_keys), :] * inv).astype(jnp.bfloat16)
+            p_scr[i, pl.ds(0, n_keys), :] = (w_scr[i, pl.ds(0, n_keys), :] * inv).astype(bf)
             o_t = nn(v_t[:, pl.ds(0, n_keys)], p_scr[i, pl.ds(0, n_keys), :])
-            o_ref[pl.ds(i * TILE, TILE), cols] = o_t.T.astype(jnp.bfloat16)
-
-        @pl.when(h == 4)
-        def _():
-            for s in range(3):
-                out.middle(s, 2)
+            o_ref[pl.ds(i * TILE, TILE), cols] = o_t.T.astype(bf)
         return carry
-    lax.fori_loop(0, q_ref.shape[1] // TILE, head, 0)
+    lax.fori_loop(0, n_heads, head, 0)
     for s in range(3):
         out.finish(s, 2)
     for s in range(3):
-        out.drain(s, 2)
-
-
-def attend(q, k, v, ids_k, ids_q, w_out, n_heads, ratio):
-    n_q, n_k = q.shape[0], k.shape[0]
+        for p in range(3):
+            out.drain(s, p)
+    swap.wait_send()
+    keep.wait()
+
+
+def forward(x, cos_t, sin_t, pos, w0, w1, w2, n_heads, ratio):
+    n_q, dim = x.shape
+    n_k = 2 * n_q
+    bf, f32 = jnp.bfloat16, jnp.float32
+    dma = pltpu.SemaphoreType.DMA
     vmem, hbm = pl.BlockSpec(memory_space=pltpu.VMEM), pl.BlockSpec(memory_space=pltpu.HBM)
+    grid = (SIDE, SIDE, SIDE)
+    shape = jax.ShapeDtypeStruct
+    tiles = n_q // TILE
     return pl.pallas_call(
-        functools.partial(attend_kernel, ratio), name="attend",
-        out_shape=[jax.ShapeDtypeStruct(q.shape, jnp.bfloat16), jax.ShapeDtypeStruct((n_heads, 1, n_q), jnp.float32),
-                   jax.ShapeDtypeStruct(w_out.shape, w_out.dtype)],
-        in_specs=[vmem] * 5 + [hbm], out_specs=[vmem] * 2 + [hbm], input_output_aliases={5: 2},
-        scratch_shapes=[pltpu.VMEM((n_k, n_q), jnp.float32), pltpu.VMEM((TILE, n_k), jnp.bfloat16),
-                        pltpu.VMEM((n_q // TILE, n_k, TILE), jnp.float32),
-                        pltpu.VMEM((n_q // TILE, n_k, TILE), jnp.bfloat16)]
-        + [pltpu.SemaphoreType.DMA((3, 3, 4))] * 4,
-        compiler_params=pltpu.CompilerParams(collective_id=3, has_side_effects=True),
-    )(q, k, v, ids_k, ids_q, w_out)
-
-
-def attend_back_kernel(ratio, q_ref, do_ref, k_ref, v_ref, ids_k, ids_q, inv_ref, dz_ref, o_ref,
+        functools.partial(forward_kernel, ratio), name="forward",
+        out_shape=[shape(grid + w0.shape, bf), shape(grid + w1.shape, bf), shape((2, dim), f32), shape((n_q, dim), bf),
+                   shape((n_q, 1), f32), shape((n_q, n_heads * TILE), bf), shape((n_k, 2 * TILE), bf),
+                   shape((n_q, n_heads * TILE), bf), shape((n_heads, 1, n_q), f32)],
+        in_specs=[vmem] * 7, out_specs=[hbm] * 2 + [vmem] * 7,
+        scratch_shapes=[pltpu.VMEM(grid + w0.shape, bf), pltpu.VMEM(grid + w2.shape, f32), pltpu.VMEM((2, dim), f32),
+                        pltpu.VMEM((n_k, n_q), f32), pltpu.VMEM((TILE, n_k), bf),
+                        pltpu.VMEM((tiles, n_k, TILE), f32), pltpu.VMEM((tiles, n_k, TILE), bf)]
+        + [dma((len(st), 3, 4)) for st in (QKV_IN, OUT, GAIN) for _ in range(4)]
+        + [dma((2,)), dma((1,)), dma((1,))],
+        compiler_params=pltpu.CompilerParams(collective_id=1, has_side_effects=True, vmem_limit_bytes=VMEM_MAX),
+    )(x, cos_t, sin_t, pos, w0, w1, w2)
+
+
+def attend_back_kernel(ratio, q_ref, do_ref, kv_ref, pos, inv_ref, dz_ref, o_ref,
                        dq_ref, dk_ref, dv_ref, acc0, acc1, acc2,
                        mask, k_t, g_scr, dp_scr, p_scr, ds_scr, dk_acc, dv_acc, dz_t, own, sib_out, sib_in, *scratch):
     n_q = q_ref.shape[0]
@@ -502,8 +567,9 @@
             gifts[done].wait_recv()
             done += 1
         out.one(s, 0)
-    fill_mask(mask, ids_k, ids_q)
-    k_t[...] = k_ref[...].T
+    fill_mask(mask, pos)
+    k_cols, v_cols = pl.ds(0, TILE), pl.ds(TILE, TILE)
+    k_t[...] = kv_ref[:, k_cols].T
     dk_acc[...] = jnp.zeros_like(dk_acc)
     dv_acc[...] = jnp.zeros_like(dv_acc)
 
@@ -517,9 +583,9 @@
             total = jnp.zeros((8, TILE), jnp.float32)
             for c in range(n_keys // TILE):
                 at = pl.ds(c * TILE, TILE)
-                t = jnp.tanh(nt(k_ref[at, :], qi) * ratio)
+                t = jnp.tanh(nt(kv_ref[at, k_cols], qi) * ratio)
                 p = jnp.exp2(t * (SOFT_CAP * LOG2E)) * (mask[at, rows] * inv)
-                dp = nt(v_ref[at, :], doi)
+                dp = nt(kv_ref[at, v_cols], doi)
                 p_scr[i, at, :] = p.astype(jnp.bfloat16)
                 g_scr[i, at, :] = p * ((1.0 - t * t) * (ratio * SOFT_CAP))
                 dp_scr[i, at, :] = dp
@@ -548,16 +614,16 @@
     dv_ref[...] = dv_acc[...].astype(jnp.bfloat16)
 
 
-def attend_back(q, do, k, v, ids_k, ids_q, inv_sum, dz, o, n_heads, ratio):
-    n_q, n_k = q.shape[0], k.shape[0]
+def attend_back(q, do, kv, pos, inv_sum, dz, o, ratio):
+    n_q, n_k = q.shape[0], kv.shape[0]
     vmem = pl.BlockSpec(memory_space=pltpu.VMEM)
     tiles = n_q // TILE
     bf, f32 = jnp.bfloat16, jnp.float32
     return pl.pallas_call(
         functools.partial(attend_back_kernel, ratio), name="attend_back",
-        out_shape=[jax.ShapeDtypeStruct(q.shape, bf)] + [jax.ShapeDtypeStruct(k.shape, bf)] * 2
+        out_shape=[jax.ShapeDtypeStruct(q.shape, bf)] + [jax.ShapeDtypeStruct((n_k, TILE), bf)] * 2
         + [jax.ShapeDtypeStruct(*a) for a in acc_shapes(OUT, 32, (0,))],
-        in_specs=[vmem] * 9, out_specs=[vmem] * 6,
+        in_specs=[vmem] * 7, out_specs=[vmem] * 6,
         scratch_shapes=[pltpu.VMEM((n_k, n_q), f32), pltpu.VMEM((TILE, n_k), bf),
                         pltpu.VMEM((tiles, n_k, TILE), f32), pltpu.VMEM((tiles, n_k, TILE), f32),
                         pltpu.VMEM((tiles, n_k, TILE), bf), pltpu.VMEM((tiles, n_k, TILE), bf),
@@ -567,7 +633,7 @@
         + wire_shapes(OUT, bf, 32, (0,)) * 2 + [pltpu.SemaphoreType.DMA((3, 3, 4))] * 2
         + [pltpu.SemaphoreType.DMA((o.shape[1] // 2 // CHUNK,))] * 2,
         compiler_params=pltpu.CompilerParams(collective_id=4, has_side_effects=True, vmem_limit_bytes=VMEM_MAX),
-    )(q, do, k, v, ids_k, ids_q, inv_sum, dz, o)
+    )(q, do, kv, pos, inv_sum, dz, o)
 
 
 def rope_tables(pos_ids, head_dim):
@@ -624,32 +690,19 @@
         w0 = jnp.concatenate([w_query.reshape(rows, q_cols), w_key.reshape(rows, head_dim),
                               w_value.reshape(rows, head_dim)], axis=1)
         w1 = w_out.reshape(q_cols, rows).T
-        w2 = jnp.pad(jnp.stack([gain_pre, gain_post]).astype(f32), ((0, 0), (0, 128 - rows))).reshape(1, 256)
-        w2 = jnp.pad(w2, ((0, 15), (0, 0)))
-        wqkv, wo_t, gains = gather_weights(w0, w1, w2)
-        gains = gains[..., 0, :].reshape(model_dim // rows, 256)
-        pre_full, post_full = gains[:, :rows].reshape(model_dim), gains[:, 128:128 + rows].reshape(model_dim)
+        lane = lax.rem(lax.axis_index('fsdp'), SIDE) * rows
+        w2 = jnp.zeros((16, 256), f32)
+        for kind, g in enumerate((gain_pre, gain_post)):
+            w2 = lax.dynamic_update_slice(w2, g.astype(f32)[None], (0, kind * 128 + lane))
+        cos_t, sin_t = rope_tables(doc_pos[0], head_dim)
+        q_scale = (head_dim if head_dim >= 256 else model_dim // n_heads) ** -0.5
+        ratio = q_scale / SOFT_CAP
+        wqkv, wo_t, gains, normed, inv_pre, q_flat, kv_all, attn_flat, inv_sum = forward(
+            hidden, cos_t[:, 0], sin_t[:, 0], doc_pos, w0, w1, w2, n_heads, ratio)
+        pre_full, post_full = gains[0], gains[1]
         wqkv = wqkv.reshape(model_dim, q_cols + 2 * head_dim)
-        q_scale = (head_dim if head_dim >= 256 else model_dim // n_heads) ** -0.5
-
-        normed, inv_pre = norm_forward(hidden, pre_full)
-        qkv = dot(normed, wqkv, (1, 0)).astype(bf)
-        q_proj = qkv[:, :q_cols].reshape(n_tok, n_heads, head_dim)
-        k_proj = qkv[:, q_cols:q_cols + head_dim].reshape(n_tok, 1, head_dim)
-        v_proj = qkv[:, q_cols + head_dim:]
-        cos_t, sin_t = rope_tables(doc_pos[0], head_dim)
-        q_rot = rotate(q_proj, cos_t, sin_t)
-        k_rot = rotate(k_proj, cos_t, sin_t)[:, 0]
-
+        wo_t = wo_t.reshape(model_dim, q_cols)
         swap = [(0, 1), (1, 0)]
-        kv_own = jnp.concatenate([k_rot, v_proj], axis=1)
-        kv_all = jnp.concatenate([lax.ppermute(kv_own, 'cp', swap), kv_own], axis=0)
-        k_all, v_all = kv_all[:, :head_dim], kv_all[:, head_dim:]
-        ids_all = jnp.concatenate([lax.ppermute(doc_ids[0], 'cp', swap), doc_ids[0]])[:, None]
-        q_flat = q_rot.reshape(n_tok, q_cols)
-        ratio = q_scale / SOFT_CAP
-        attn_flat, inv_sum, wo_t = attend(q_flat, k_all, v_all, ids_all, doc_ids, wo_t, n_heads, ratio)
-        wo_t = wo_t.reshape(model_dim, q_cols)
         proj_out = dot(attn_flat, wo_t, (1, 1)).astype(bf)
         post_out, inv_post = norm_forward(proj_out, post_full)
         out_hidden = (hidden.astype(f32) + post_out.astype(f32)).astype(bf)
@@ -658,8 +711,7 @@
         d_proj = d_proj.astype(bf)
         d_attn = dot(d_proj, wo_t, (1, 0)).astype(bf)
 
-        d_q_flat, d_k, d_v, *accs = attend_back(q_flat, d_attn, k_all, v_all, ids_all, doc_ids, inv_sum, d_proj, attn_flat,
-                                                n_heads, ratio)
+        d_q_flat, d_k, d_v, *accs = attend_back(q_flat, d_attn, kv_all, doc_pos, inv_sum, d_proj, attn_flat, ratio)
         d_kv = jnp.concatenate([d_k, d_v], axis=1)
         d_kv = (d_kv[n_tok:].astype(f32) + lax.ppermute(d_kv[:n_tok], 'cp', swap).astype(f32)).astype(bf)
         d_k_rot, d_v_proj = d_kv[:, :head_dim], d_kv[:, head_dim:]

time: 271 us -> 252 us (0.930); the launches traced: 266 us -> 251 us
  matrix products: 34.3 us -> 25.7 us
  local copies, waits for them, and re-layouts: 26.4 us -> 18.1 us
  Pallas kernels: 175 us -> 183 us
    dot_general x4 -> x3, matrix products: 34.3 us -> 25.7 us  [dot(): lax.dot_general(a, b, ((dims[:1], dims[1:]), ((), ())), preferred_element...]
    pallas_call x2 -> x1, Pallas kernels: 75.3 us -> 83 us  [forward(): pl.pallas_call(functools.partial(forward_kernel, ratio), name='forward',...]
    broadcast_in_dim x0 -> x3, other arithmetic: none -> 6.31 us  [the longest x1 5 us: layer_local(): grad_hidden[None]]
    unnamed x58 -> x41, local copies, waits for them, and re-layouts: 13.2 us -> 7.56 us
    convert_element_type x1 -> x0, other arithmetic: 3.78 us -> none  [norm_forward(): return (normed.astype(jnp.bfloat16), inv_rms)]
    concatenate x4 -> x2, other arithmetic: 4.45 us -> 1.44 us  [rotate(): jnp.concatenate([first_half * cos_t - second_half * sin_t, second_half *...]
  transfers between devices with their start and end apart: 3 -> 1, of which waited for: 0 -> 0; matrix products, arithmetic and copies ran while one was open for 12% -> 2% of each run, Pallas kernels for 19% -> 0%
where the time goes in v4:
time: 252 us; the launch traced here: 251 us
  Pallas kernels  183 us (73%)
  matrix products  25.7 us (10%)
  other arithmetic  23.4 us (9%)
  local copies, waits for them, and re-layouts  18.1 us (7%)
    pallas_call x1, Pallas kernels, forward(): pl.pallas_call(functools.partial(forward_kernel, ratio), name='forward',...  83 us
    pallas_call x1, Pallas kernels, scatter_grads(): pl.pallas_call(scatter_kernel, name='scatter_grads', out_shape=[jax.Shape...  57.7 us
    pallas_call x1, Pallas kernels, attend_back(): pl.pallas_call(functools.partial(attend_back_kernel, ratio), name='attend...  41.9 us
    dot_general x3, matrix products, dot(): lax.dot_general(a, b, ((dims[:1], dims[1:]), ((), ())), preferred_element...  25.7 us
    unnamed x41, local copies, waits for them, and re-layouts  7.56 us
  transfers between devices with their start and end apart: 1, of which 0 were waited for; matrix products, arithmetic and copies ran while one was open for 2% of the time, Pallas kernels for 0%

profile of v4, /device:TPU:1, one launch (start us, length us, event | category | flops | bytes accessed | tf_op | source)
XLA Modules:
  0.0 251.5 jit_solution(18068519885801357492)
XLA Ops:
  0.7 0.7 bitcast_convert_fusion.1
  1.3 0.7 bitcast_convert_fusion
  2.0 0.7 convert_element_type.87
  2.7 0.9 copy.29
  3.6 1.6 copy.28
  5.2 1.8 fusion.34
  7.0 0.1 dynamic_update_slice.6
  7.2 0.2 dynamic_update_slice.7.in2
  7.4 0.0 copy-start.9
  7.4 1.4 pad_maximum_fusion.4.in0
  8.8 83.0 %forward.1 = (bf16[4,4,4,32,2560]{4,3,2,1,0:T(8,128)(2,1)}, bf16[4,4,4,32,2048]{4,3,2,1,0:T(8,128)(2,1)}, f32[2,2048]{1,0:T(2,128)}, bf16[512,2048]{1,0:T(8,128)...) custom-call(bf16[512,2048]{1,0:T(8,128)(2,1)} %bitcast.76, ...), custom_call_target="tpu_custom_call" | custom-call | tf_op jit(solution)/shard_map/forward/pallas_call | solution.py:533
  91.8 1.4 slice_add_fusion
  93.2 8.8 %fusion.11 = (f32[512]{0:T(512)S(1)}, bf16[512,2048]{1,0:T(8,128)(2,1)S(1)}) fusion(bf16[512,2048]{1,0:T(8,128)(2,1)} %get-tuple-element.26.o_ref, bf16[2048,2048]{1,0:T(8,128)(2,1)} %bitcast.99), kind=kOutput, calls=%fused_computation.23 | convolution fusion | flops 4299161088 | bytes 12584960 | tf_op jit(solution)/shard_map/dot_general | solution.py:672
  102.0 2.0 fusion.17
  104.0 2.9 %fusion.3 = (bf16[512,2048]{1,0:T(8,128)(2,1)S(1)}, bf16[1,512,2048]{2,1,0:T(8,128)(2,1)}) fusion(bf16[512,2048]{1,0:T(8,128)(2,1)S(1)} %get-tuple-element.92, bf16[1,512,2048]{2,1,0:T(8,128)(2,1)S(1)} %copy-done, f32[512]{0:T(512)S(1)} %broadcast_multiply_fusion.1, f32[512]{0:T(512)S(1)} %get-tuple-element.89, f32[2048]{0:T(1024)S(1)} %bitcast.91, ...), kind=kLoop, calls=%fused_computation.15 | loop fusion | flops 15728640 | bytes 10500096 | tf_op jit(solution)/shard_map/convert_element_type | solution.py:711
  107.0 1.6 copy-done.16
  108.6 5.7 %convolution_convert_fusion.do_ref = bf16[512,2048]{1,0:T(8,128)(2,1)} fusion(bf16[512,2048]{1,0:T(8,128)(2,1)S(1)} %get-tuple-element.68.dz_ref, bf16[2048,2048]{1,0:T(8,128)(2,1)S(1)} %bitcast.100), kind=kOutput, calls=%fused_computation.30 | convolution fusion | flops 4296015872 | bytes 12582912 | tf_op jit(solution)/shard_map/dot_general | solution.py:672
  114.3 41.9 %attend_back.1 = (bf16[512,2048]{1,0:T(8,128)(2,1)}, bf16[1024,256]{1,0:T(8,128)(2,1)}, bf16[1024,256]{1,0:T(8,128)(2,1)}, f32[16,32,256]{2,1,0:T(8,128)}, f32[1...) custom-call(bf16[512,2048]{1,0:T(8,128)(2,1)} %get-tuple-element.30.q_ref, bf16[512,2048]{1,0:T(8,128)(2,1)} %convolution_convert_fusion.do_ref, ...), custom_call_target="tpu_custom_call" | custom-call | tf_op jit(solution)/shard_map/attend_back/pallas_call | solution.py:622
  156.3 1.2 constant_dynamic-update-slice_fusion.1
  157.5 1.1 constant_dynamic-update-slice_fusion
  158.6 0.8 slice.79
  159.4 0.9 collective-permute-start
  160.3 0.8 stack.10
  161.1 0.7 copy.30
  161.8 0.3 copy-done.7
  162.0 0.7 fusion.19
  162.7 0.2 pad_maximum_fusion.1
  163.0 0.0 copy-start.15
  163.0 0.7 copy.31
  163.7 0.8 fusion.35
  164.5 1.3 add_convert_fusion
  165.9 1.2 fusion.32
  167.1 1.7 pad_maximum_fusion.d_qkv
  168.8 11.2 %fusion.10 = (f32[2048]{0:T(1024)S(1)}, f32[512]{0:T(512)S(1)}, bf16[512,2048]{1,0:T(8,128)(2,1)}) fusion(f32[512]{0:T(512)S(1)} %get-tuple-element.64, bf16[1,512,2048]{2,1,0:T(8,128)(2,1)S(1)} %copy-done.3, f32[2048]{0:T(1024)S(1)} %bitcast.93, bf16[2048,2560]{1,0:T(8,128)(2,1)} %bitcast.98, bf16[512,256]{1,0:T(8,128)(2,1)S(1)} %get-tuple-element.73, ...), kind=kOutput, calls=%fused_computation.22 | convolution fusion | flops 5388629504 | bytes 17321984 | tf_op jit(solution)/shard_map/dot_general | solution.py:672
  180.0 0.6 broadcast_multiply_fusion
  180.6 0.1 stack.9
  180.7 0.1 select_maximum_fusion
  180.8 0.1 constant_dynamic-slice_fusion
  180.9 1.6 copy_bitcast_fusion
  182.6 57.7 %scatter_grads.1 = (f32[2,32,1280]{2,1,0:T(8,128)}, f32[2,32,1024]{2,1,0:T(8,128)}, f32[2,16,128]{2,1,0:T(8,128)}) custom-call(bf16[512,2048]{1,0:T(8,128)(2,1)} %get-tuple-element.37.normed, bf16[512,2560]{1,0:T(8,128)(2,1)} %pad_maximum_fusion.d_qkv, f32[64,16,128]{2,1,0:T(8,128)} %get-tuple-element.95.own_g, f32[64,16,128]{2,1,0:T(8,128)} %get-tuple-element.94.sib_g, ...), custom_call_target="tpu_custom_call" | custom-call | tf_op jit(solution)/shard_map/scatter_grads/pallas_call | solution.py:352
  240.2 1.2 slice_bitcast_fusion.2
  241.4 1.2 slice_bitcast_fusion.7
  242.7 0.8 copy.32
  243.4 0.6 copy.25
  244.1 0.6 copy.24
  244.7 1.0 slice_bitcast_fusion.4
  245.8 0.7 copy.36
  246.5 5.0 %fusion.23 = bf16[1,512,2048]{2,1,0:T(8,128)(2,1)} fusion(bf16[512,2048]{1,0:T(8,128)(2,1)} %get-tuple-element.93, bf16[1,512,2048]{2,1,0:T(8,128)(2,1)S(1)} %copy-done.1, f32[512]{0:T(512)} %broadcast_multiply_fusion, f32[512]{0:T(512)} %get-tuple-element.65, f32[2048]{0:T(1024)} %bitcast.92, f32[512]{0:T(512)} %copy-done.13, bf16[1,512,2048]{2,1,0:T(8,128)(2,1)} %param.10), kind=kLoop, calls=%fused_computation.43 | loop fusion | flops 10485760 | bytes 8402944 | tf_op jit(solution)/shard_map/broadcast_in_dim | solution.py:733
  (39 shorter events, 0.2 us)
Async XLA Ops:
  0.7 4.5 %copy-start.14 = (f32[128]{0:T(128)}, f32[128]{0:T(128)S(1)}, u32[]{:S(2)}) copy-start(f32[128]{0:T(128)S(1)} %multiply_power_fusion) | copy-start | bytes 1540
  2.7 2.5 copy-start.11
  7.4 1.4 copy-start.9
  93.2 8.8 %copy-start = (bf16[1,512,2048]{2,1,0:T(8,128)(2,1)S(1)}, bf16[1,512,2048]{2,1,0:T(8,128)(2,1)}, u32[]{:S(2)}) copy-start(bf16[1,512,2048]{2,1,0:T(8,128)(2,1)} %param.12) | copy-start | bytes 6291460
  102.0 2.1 copy-start.2
  104.0 4.6 %copy-start.16 = (bf16[4,4,4,32,2048]{4,3,2,1,0:T(8,128)(2,1)S(1)}, bf16[4,4,4,32,2048]{4,3,2,1,0:T(8,128)(2,1)}, u32[]{:S(2)}) copy-start(bf16[4,4,4,32,2048]{4,3,2,1,0:T(8,128)(2,1)} %get-tuple-element.27) | copy-start | bytes 25165828
  107.0 7.4 %copy-start.4 = (bf16[512,2048]{1,0:T(8,128)(2,1)}, bf16[512,2048]{1,0:T(8,128)(2,1)S(1)}, u32[]{:S(2)}) copy-start(bf16[512,2048]{1,0:T(8,128)(2,1)S(1)} %get-tuple-element.68.dz_ref) | copy-start | bytes 6291460
  156.3 4.8 %copy-start.6 = (bf16[512,2048]{1,0:T(8,128)(2,1)S(1)}, bf16[512,2048]{1,0:T(8,128)(2,1)}, u32[]{:S(2)}) copy-start(bf16[512,2048]{1,0:T(8,128)(2,1)} %get-tuple-element.33) | copy-start | bytes 6291460
  156.3 5.5 %copy-start.5 = (f32[512,128]{1,0:T(8,128)S(1)}, f32[512,128]{1,0:T(8,128)}, u32[]{:S(2)}) copy-start(f32[512,128]{1,0:T(8,128)} %get-tuple-element.88.cos_ref) | copy-start | bytes 786436
  159.4 5.1 %collective-permute-start = (bf16[512,512]{1,0:T(8,128)(2,1)}, bf16[512,512]{1,0:T(8,128)(2,1)}, u32[]{:S(2)}, u32[]{:S(2)}) collective-permute-start(bf16[512,512]{1,0:T(8,128)(2,1)} %slice.79), channel_id=1, source_target_pairs={{0,1},{1,0},{2,3},{3,2},{4,5},{5,4},{6,7},{7,6},{8,9},{9,8},{10,11... | collective-permute-start | bytes 1572872 | tf_op jit(solution)/shard_map/ppermute | solution.py:716
  161.1 1.0 copy-start.7
  162.7 1.0 copy-start.8
  163.0 2.9 %copy-start.12 = (f32[1,512]{1,0:T(1,128)S(1)}, f32[1,512]{1,0:T(1,128)}, u32[]{:S(2)}) copy-start(f32[1,512]{1,0:T(1,128)} %copy-done.11) | copy-start | bytes 6148
  163.0 2.9 %copy-start.15 = (f32[128]{0:T(128)S(1)}, f32[128]{0:T(128)}, u32[]{:S(2)}) copy-start(f32[128]{0:T(128)} %copy-done.14) | copy-start | bytes 1540
  164.5 4.3 %copy-start.13 = (f32[512]{0:T(512)}, f32[512]{0:T(512)S(1)}, u32[]{:S(2)}) copy-start(f32[512]{0:T(512)S(1)} %get-tuple-element.64) | copy-start | bytes 6148
  164.5 4.3 %copy-start.3 = (bf16[1,512,2048]{2,1,0:T(8,128)(2,1)S(1)}, bf16[1,512,2048]{2,1,0:T(8,128)(2,1)}, u32[]{:S(2)}) copy-start(bf16[1,512,2048]{2,1,0:T(8,128)(2,1)} %param.10) | copy-start | bytes 6291460
  164.5 4.3 %copy-start.10 = (f32[1,2048]{1,0:T(1,128)S(1)}, f32[1,2048]{1,0:T(1,128)}, u32[]{:S(2)}) copy-start(f32[1,2048]{1,0:T(1,128)} %get-tuple-element.84) | copy-start | bytes 24580
  240.2 6.2 %copy-start.1 = (bf16[1,512,2048]{2,1,0:T(8,128)(2,1)S(1)}, bf16[1,512,2048]{2,1,0:T(8,128)(2,1)}, u32[]{:S(2)}) copy-start(bf16[1,512,2048]{2,1,0:T(8,128)(2,1)} %param.12) | copy-start | bytes 6291460

commit v5 on v4

--- a/solution.py
+++ b/solution.py
@@ -36,13 +36,13 @@
     return (coords[0] * 16 + coords[1] * 4 + coords[2], core)
 
 
-def greet(coords, core):
+def greet(coords, core, steps=(1, -1)):
     barrier = pltpu.get_barrier_semaphore()
     for dim in range(3):
-        for delta in (1, -1):
+        for delta in steps:
             pl.semaphore_signal(barrier, inc=1, device_id=device(shifted(coords, dim, delta), core), device_id_type=MESH)
     pl.semaphore_signal(barrier, inc=1, device_id=device(coords, 1 - core), device_id_type=MESH)
-    pl.semaphore_wait(barrier, 7)
+    pl.semaphore_wait(barrier, 3 * len(steps) + 1)
 
 
 def order_of(colour):
@@ -55,8 +55,8 @@
 
 
 class Gather:
-    def __init__(self, streams, src, out, send, recv, sib_send, sib_recv):
-        self.streams, self.src, self.out = streams, src, out
+    def __init__(self, streams, src, out, direct, send, recv, sib_send, sib_recv):
+        self.streams, self.src, self.out, self.direct = streams, src, out, direct
         self.sems = (send, recv, sib_send, sib_recv)
         self.coords, self.core = place()
         self.rows = out.shape[3]
@@ -69,15 +69,16 @@
         full = order_of(self.streams[s][0])[:p]
         idx = [pl.ds(0, SIDE) if d in full else at[d] for d in range(3)]
         half = self.rows // 2
-        r0, nr = ((0, self.rows), (0, self.rows), (0, half), (half, half))[kind]
+        r0, nr = (0, self.rows) if kind < 2 or p in self.direct else ((kind - 2) * half, half)
         return self.out.at[idx[0], idx[1], idx[2], pl.ds(r0, nr), self.cols(s, side)]
 
     def hop(self, s, p, kind):
         dim = order_of(self.streams[s][0])[p]
-        at = shifted(self.coords, dim, (0, 0, -1, 1)[kind])
-        to = shifted(self.coords, dim, (1, -1, 1, -1)[kind])
+        direct = p in self.direct
+        at = shifted(self.coords, dim, 0 if direct else (0, 0, -1, 1)[kind])
+        to = shifted(self.coords, dim, (1, -1, 2 if direct else 1, -1)[kind])
         dst = self.part(s, p, kind, at, self.core)
-        src = self.src.at[:, self.cols(s, self.core)] if p == 0 and kind < 2 else dst
+        src = self.src.at[:, self.cols(s, self.core)] if p == 0 and (direct or kind < 2) else dst
         return pltpu.make_async_remote_copy(src, dst, self.sems[0].at[s, p, kind], self.sems[1].at[s, p, kind],
                                             device_id=device(to, self.core), device_id_type=MESH)
 
@@ -98,20 +99,27 @@
     def start(self, s, p):
         self.hop(s, p, 0).start()
         self.hop(s, p, 1).start()
+        if p in self.direct:
+            self.hop(s, p, 2).start()
 
     def middle(self, s, p):
+        if p in self.direct:
+            for kind in range(3):
+                self.arrive(s, p, kind)
+                self.gift(s, p, kind, self.core).start()
+            return
         for kind in (0, 1):
             self.arrive(s, p, kind)
             self.hop(s, p, kind + 2).start()
             self.gift(s, p, kind, self.core).start()
 
     def finish(self, s, p):
-        for kind in (2, 3):
+        for kind in () if p in self.direct else (2, 3):
             self.arrive(s, p, kind)
             self.gift(s, p, kind, self.core).start()
 
     def drain(self, s, p):
-        for kind in range(4):
+        for kind in range(3 if p in self.direct else 4):
             self.hop(s, p, kind).wait_send()
             self.gift(s, p, kind, self.core).wait_send()
             self.gift(s, p, kind, 1 - self.core).wait_recv()
@@ -245,20 +253,24 @@
     return [((SIDE ** (2 - q), rows, width), jnp.float32) for _, _, width in streams for q in phases]
 
 
-def scatter_kernel(normed, d_qkv, own_g, sib_g, acc_o0, acc_o1, acc_o2, out_q, out_o, out_g, *scratch):
+def scatter_kernel(normed, d_qkv, w_ref, x_ref, dy_ref, inv_rms, gain, post_row, acc_o0, acc_o1, acc_o2,
+                   dx_ref, grad_q, grad_k, grad_v, grad_o, out_g, *scratch):
     scratch = list(scratch)
 
     def take(n):
         head = scratch[:n]
         del scratch[:n]
         return head
-    normed_t, own_q, sib_out, sib_q, sib_in_g = take(5)
+    normed_t, own_q, sib_out, sib_q, own_g, sib_g, sib_in_g, out_q, out_o, w_buf, dn, pre_row = take(12)
     nq = len(QKV)
     acc_q, sbuf_q, rbuf_q = take(3 * nq), take(3 * nq), take(3 * nq)
     acc_o, sbuf_o, rbuf_o = take(6), take(6), take(6)
     acc_g, sbuf_g, rbuf_g = take(3), take(3), take(3)
     sems = take(6)
-    gift_send, gift_recv, gain_sem, fin_send, fin_recv = take(5)
+    gift_send, gift_recv, gain_sem, fin_send, fin_recv, w_sem = take(6)
+    bf, f32 = jnp.bfloat16, jnp.float32
+    n_tok, dim = x_ref.shape
+    strips = dim // CHUNK
     coords, core = place()
     sibling = device(coords, 1 - core)
     greet(coords, core)
@@ -271,12 +283,16 @@
     qkv = Scatter(QKV, own_q, sib_q, triples(acc_q), triples(sbuf_q), triples(rbuf_q), *sems[0:2])
     out = Scatter(OUT, None, None, tails(acc_o, (acc_o0, acc_o1, acc_o2)), tails(sbuf_o, (None,) * 3),
                   tails(rbuf_o, (None,) * 3), *sems[2:4])
-    gain = Scatter(GAIN, own_g, sib_in_g, triples(acc_g), triples(sbuf_g), triples(rbuf_g), *sems[4:6])
+    gains = Scatter(GAIN, own_g, sib_in_g, triples(acc_g), triples(sbuf_g), triples(rbuf_g), *sems[4:6])
     gain_gift = pltpu.make_async_remote_copy(sib_g, sib_in_g, gain_sem.at[0], gain_sem.at[1],
                                              device_id=sibling, device_id_type=MESH)
-    gain_gift.start()
+    loads = [pltpu.make_async_copy(w_ref.at[pl.ds(8 * j, 8)], w_buf.at[j % 2], w_sem.at[j]) for j in range(strips)]
+    loads[0].start()
+    loads[1].start()
     for s in range(3):
         out.one(s, 1)
+    own_g[...] = jnp.zeros_like(own_g)
+    sib_g[...] = jnp.zeros_like(sib_g)
     transpose_into(normed_t, normed)
     chunks = own_q.shape[2] // CHUNK
     gifts = [chunk_gift(sib_out, sib_q, gift_send, gift_recv, j) for j in range(chunks)]
@@ -285,8 +301,6 @@
         gifts[j].start()
     for s in range(3):
         out.two(s, 1)
-    gain_gift.wait_recv()
-    gain.one(0, 0)
     done = 0
     for s, (_, off, width) in enumerate(QKV):
         while done * CHUNK < off + width:
@@ -298,23 +312,56 @@
             for i in range(3):
                 out.three(i, 1)
                 out.one(i, 2)
-    work = [(qkv, s) for s in range(nq)] + [(gain, 0)]
+    for j in range(strips):
+        loads[j].wait()
+        dn[:, pl.ds(j * CHUNK, CHUNK)] = nt(d_qkv[...], w_buf[j % 2].reshape(CHUNK, d_qkv.shape[1])).astype(bf)
+        if j + 2 < strips:
+            loads[j + 2].start()
+    work = [(qkv, s) for s in range(nq)]
+    for s in range(3):
+        out.two(s, 2)
+    for scatter, s in work:
+        scatter.two(s, 0)
+    pre_row[...] = jnp.zeros_like(pre_row)
+    one_gain = 1.0 + gain[pl.ds(0, 1), :]
+
+    def back(i, carry):
+        at = pl.ds(i * 32, 32)
+        xs, g, inv = x_ref[at, :].astype(f32), dn[at, :].astype(f32), inv_rms[at, :]
+        scaled = g * one_gain
+        mean = jnp.sum(scaled * xs, axis=1, keepdims=True) * (1.0 / dim)
+        dx_ref[at, :] = (dy_ref[at, :].astype(f32) + (inv * scaled - xs * (inv * inv * inv * mean))).astype(bf)
+        pre_row[...] += jnp.sum((g * (xs * inv)).reshape(4, 8, dim), axis=0)
+        return carry
+    lax.fori_loop(0, n_tok // 32, back, 0)
+    pre, post = jnp.sum(pre_row[...], axis=0, keepdims=True), post_row[...]
+    own_row, sib_row = jnp.where(core == 0, pre, post), jnp.where(core == 0, post, pre)
+    for j in range(16):
+        for x in range(SIDE):
+            own_g[SIDE * j + x, pl.ds(0, 1), :] = own_row[:, j * 128:(j + 1) * 128]
+            sib_g[SIDE * j + x, pl.ds(0, 1), :] = sib_row[:, j * 128:(j + 1) * 128]
+    gain_gift.start()
+    for scatter, s in work:
+        scatter.three(s, 0)
+        scatter.one(s, 1)
+    for s in range(3):
+        out.three(s, 2)
+    gain_gift.wait_recv()
+    gains.one(0, 0)
+    work = work + [(gains, 0)]
     for q in range(3):
         for scatter, s in work:
-            scatter.two(s, q)
-        if q == 0:
-            for s in range(3):
-                out.two(s, 2)
+            if q > 0 or scatter is gains:
+                scatter.two(s, q)
         for scatter, s in work:
+            if q == 0 and scatter is not gains:
+                continue
             scatter.three(s, q)
             if q < 2:
                 scatter.one(s, q + 1)
-        if q == 0:
-            for s in range(3):
-                out.three(s, 2)
     fins = []
     k = 0
-    for scatter, ref in ((qkv, out_q), (out, out_o), (gain, out_g)):
+    for scatter, ref in ((qkv, out_q), (out, out_o), (gains, out_g)):
         for s, (_, off, width) in enumerate(scatter.streams):
             part = scatter.acc[s][2].at[0]
             ref[core, :, pl.ds(off, width)] = scatter.acc[s][2][0]
@@ -327,15 +374,25 @@
     for mine, theirs in fins:
         mine.wait_send()
         theirs.wait_recv()
+    n_heads = grad_q.shape[1]
+    per = out_q.shape[2] // TILE
+    for h in range(n_heads + 2):
+        part = out_q[h // per, :, pl.ds(h % per * TILE, TILE)]
+        if h < n_heads:
+            grad_q[:, h, :] = part
+        else:
+            (grad_k, grad_v)[h - n_heads][...] = part
+    for side in range(2):
+        grad_o[pl.ds(side * out_o.shape[2], out_o.shape[2]), :] = out_o[side].T
     for copy in gifts + [gain_gift]:
         copy.wait_send()
-    for scatter, phases in ((qkv, (0, 1, 2)), (out, (1, 2)), (gain, (0, 1, 2))):
+    for scatter, phases in ((qkv, (0, 1, 2)), (out, (1, 2)), (gains, (0, 1, 2))):
         for s in range(len(scatter.streams)):
             for q in phases:
                 scatter.drain(s, q)
 
 
-def scatter_grads(normed, d_qkv, own_g, sib_g, accs):
+def scatter_grads(normed, d_qkv, w, x, dy, inv_rms, gain, post_row, accs, n_heads):
     bf, f32 = jnp.bfloat16, jnp.float32
     n_tok, model_dim = normed.shape
     half, rows = d_qkv.shape[1] // 2, 32
@@ -343,19 +400,25 @@
     dma = pltpu.SemaphoreType.DMA
     vmem = pl.BlockSpec(memory_space=pltpu.VMEM)
     scratch = [pltpu.VMEM((model_dim, n_tok), bf), pltpu.VMEM((blocks, rows, half), f32),
-               pltpu.VMEM((blocks, rows, half), bf), pltpu.VMEM((blocks, rows, half), bf), pltpu.VMEM(sib_g.shape, f32)]
+               pltpu.VMEM((blocks, rows, half), bf), pltpu.VMEM((blocks, rows, half), bf)]
+    scratch += [pltpu.VMEM((blocks, 16, 128), f32)] * 3
+    scratch += [pltpu.VMEM((2, rows, half), f32), pltpu.VMEM((2, rows, 1024), f32),
+                pltpu.VMEM((2, CHUNK // rows, rows, 2 * half), bf), pltpu.VMEM((n_tok, model_dim), bf),
+                pltpu.VMEM((8, model_dim), f32)]
     for streams, dtype, n_rows, phases in ((QKV, bf, rows, (0, 1, 2)), (OUT, bf, rows, (1, 2)), (GAIN, f32, 16, (0, 1, 2))):
         scratch += [pltpu.VMEM(*a) for a in acc_shapes(streams, n_rows, phases)]
         scratch += wire_shapes(streams, dtype, n_rows, phases) * 2
     scratch += [dma((len(st), 3, 4)) for st in (QKV, OUT, GAIN) for _ in range(2)]
-    scratch += [dma((half // CHUNK,))] * 2 + [dma((2,))] + [dma((len(QKV) + 4,))] * 2
+    scratch += [dma((half // CHUNK,))] * 2 + [dma((2,))] + [dma((len(QKV) + 4,))] * 2 + [dma((model_dim // CHUNK,))]
     return pl.pallas_call(
         scatter_kernel, name="scatter_grads",
-        out_shape=[jax.ShapeDtypeStruct((2, rows, half), f32), jax.ShapeDtypeStruct((2, rows, 1024), f32),
-                   jax.ShapeDtypeStruct((2, 16, 128), f32)],
-        in_specs=[vmem] * 7, out_specs=[vmem] * 3, scratch_shapes=scratch,
+        out_shape=[jax.ShapeDtypeStruct((n_tok, model_dim), bf), jax.ShapeDtypeStruct((rows, n_heads, TILE), f32),
+                   jax.ShapeDtypeStruct((rows, TILE), f32), jax.ShapeDtypeStruct((rows, TILE), f32),
+                   jax.ShapeDtypeStruct((n_heads * TILE, rows), f32), jax.ShapeDtypeStruct((2, 16, 128), f32)],
+        in_specs=[vmem] * 2 + [pl.BlockSpec(memory_space=pltpu.HBM)] + [vmem] * 8, out_specs=[vmem] * 6,
+        scratch_shapes=scratch,
         compiler_params=pltpu.CompilerParams(collective_id=2, has_side_effects=True, vmem_limit_bytes=VMEM_MAX),
-    )(normed, d_qkv, own_g, sib_g, *accs)
+    )(normed, d_qkv, w, x, dy, inv_rms, gain, post_row, *accs)
 
 
 LOG2E = 1.4426950408889634
@@ -393,10 +456,10 @@
     bf, f32 = jnp.bfloat16, jnp.float32
     coords, core = place()
     sibling = device(coords, 1 - core)
-    greet(coords, core)
+    greet(coords, core, (1, -1, 2))
     own_sem, swap_send, swap_recv = sems[12:15]
-    qkv, out, gain = (Gather(st, src, dst, *sems[4 * g:4 * g + 4]) for g, (st, src, dst) in enumerate(
-        ((QKV_IN, in0, wq), (OUT, in1, wo_out), (GAIN, in2, gains))))
+    qkv, out, gain = (Gather(st, src, dst, direct, *sems[4 * g:4 * g + 4]) for g, (st, src, dst, direct) in enumerate(
+        ((QKV_IN, in0, wq, (0,)), (OUT, in1, wo_out, (0,)), (GAIN, in2, gains, (0, 1, 2)))))
     nq = range(len(QKV_IN))
     gain.start(0, 0)
     for s in nq:
@@ -415,30 +478,23 @@
         return carry
     lax.fori_loop(0, n_q // 64, stats, 0)
     gain.middle(0, 0)
+    gain.start(0, 1)
     for s in nq:
         qkv.middle(s, 0)
-    gain.finish(0, 0)
-    gain.start(0, 1)
-    for s in nq:
-        qkv.finish(s, 0)
         qkv.start(s, 1)
+    gain.middle(0, 1)
+    gain.start(0, 2)
     for s in range(3):
         out.middle(s, 0)
-    gain.middle(0, 1)
+    own_out.wait()
     for s in nq:
         qkv.middle(s, 1)
-    gain.finish(0, 1)
-    gain.start(0, 2)
-    for s in range(3):
-        out.finish(s, 0)
-    own_out.wait()
+    for s in range(3):
+        out.start(s, 1)
+    gain.middle(0, 2)
     for s in nq:
         qkv.finish(s, 1)
         qkv.start(s, 2)
-    for s in range(3):
-        out.start(s, 1)
-    gain.middle(0, 2)
-    gain.finish(0, 2)
     for p in range(3):
         gain.drain(0, p)
     for kind in range(2):
@@ -545,14 +601,23 @@
     )(x, cos_t, sin_t, pos, w0, w1, w2)
 
 
-def attend_back_kernel(ratio, q_ref, do_ref, kv_ref, pos, inv_ref, dz_ref, o_ref,
-                       dq_ref, dk_ref, dv_ref, acc0, acc1, acc2,
-                       mask, k_t, g_scr, dp_scr, p_scr, ds_scr, dk_acc, dv_acc, dz_t, own, sib_out, sib_in, *scratch):
+def attend_back_kernel(ratio, q_ref, do_ref, kv_ref, pos, inv_ref, dz_ref, o_ref, cos_ref, sin_ref,
+                       dqkv_ref, acc0, acc1, acc2,
+                       mask, k_t, g_scr, dp_scr, p_scr, ds_scr, dk_acc, dv_acc, dkv_out, dkv_in, dz_t, own, sib_out, sib_in,
+                       *scratch):
     n_q = q_ref.shape[0]
     coords, core = place()
     greet(coords, core)
     sbuf, rbuf, sems = scratch[0:3], scratch[3:6], scratch[6:8]
-    gift_send, gift_recv = scratch[8:10]
+    gift_send, gift_recv, swap_sem = scratch[8:11]
+    bf, f32 = jnp.bfloat16, jnp.float32
+    swap = pltpu.make_async_remote_copy(dkv_out, dkv_in, swap_sem.at[0], swap_sem.at[1],
+                                        device_id=device(coords, 1 - core), device_id_type=MESH)
+
+    def rope_back(u):
+        lo, hi = u[:, :TILE // 2].astype(f32), u[:, TILE // 2:].astype(f32)
+        c, s = cos_ref[pl.ds(0, u.shape[0]), :], sin_ref[pl.ds(0, u.shape[0]), :]
+        return jnp.concatenate([lo * c + hi * s, hi * c - lo * s], axis=1).astype(bf)
     out = Scatter(OUT, own, sib_in, [[a] for a in (acc0, acc1, acc2)], [[b] for b in sbuf], [[b] for b in rbuf], *sems)
     chunks = own.shape[2] // CHUNK
     transpose_into(dz_t, dz_ref)
@@ -594,7 +659,10 @@
             seen = pl.ds(0, n_keys)
             ds_scr[i, seen, :] = ((dp_scr[i, seen, :] - row_dot) * g_scr[i, seen, :]).astype(jnp.bfloat16)
             dq_t = nn(k_t[:, seen], ds_scr[i, seen, :])
-            dq_ref[rows, cols] = dq_t.T.astype(jnp.bfloat16)
+            dq = dq_t.T.astype(bf)
+            lo, hi = dq[:, :TILE // 2].astype(f32), dq[:, TILE // 2:].astype(f32)
+            cos, sin = cos_ref[rows, :], sin_ref[rows, :]
+            dqkv_ref[rows, cols] = jnp.concatenate([lo * cos + hi * sin, hi * cos - lo * sin], axis=1).astype(bf)
             dk_acc[seen, :] += nn(ds_scr[i, seen, :], qi)
             dv_acc[seen, :] += nn(p_scr[i, seen, :], doi)
 
@@ -604,36 +672,43 @@
                 out.two(s, 0)
         return carry
     lax.fori_loop(0, q_ref.shape[1] // TILE, head, 0)
+    mine, other = pl.ds(n_q, n_q), pl.ds(0, n_q)
+    dkv_out[:, k_cols] = dk_acc[other, :].astype(bf)
+    dkv_out[:, v_cols] = dv_acc[other, :].astype(bf)
+    swap.start()
     for s in range(3):
         out.three(s, 0)
+    swap.wait_recv()
+    q_cols = q_ref.shape[1]
+    dqkv_ref[:, pl.ds(q_cols, TILE)] = rope_back((dk_acc[mine, :] + dkv_in[:, k_cols].astype(f32)).astype(bf))
+    dqkv_ref[:, pl.ds(q_cols + TILE, TILE)] = (dv_acc[mine, :] + dkv_in[:, v_cols].astype(f32)).astype(bf)
     for s in range(3):
         out.drain(s, 0)
-    for copy in gifts:
+    for copy in gifts + [swap]:
         copy.wait_send()
-    dk_ref[...] = dk_acc[...].astype(jnp.bfloat16)
-    dv_ref[...] = dv_acc[...].astype(jnp.bfloat16)
-
-
-def attend_back(q, do, kv, pos, inv_sum, dz, o, ratio):
+
+
+def attend_back(q, do, kv, pos, inv_sum, dz, o, cos_t, sin_t, ratio):
     n_q, n_k = q.shape[0], kv.shape[0]
     vmem = pl.BlockSpec(memory_space=pltpu.VMEM)
     tiles = n_q // TILE
     bf, f32 = jnp.bfloat16, jnp.float32
     return pl.pallas_call(
         functools.partial(attend_back_kernel, ratio), name="attend_back",
-        out_shape=[jax.ShapeDtypeStruct(q.shape, bf)] + [jax.ShapeDtypeStruct((n_k, TILE), bf)] * 2
+        out_shape=[jax.ShapeDtypeStruct((n_q, q.shape[1] + 2 * TILE), bf)]
         + [jax.ShapeDtypeStruct(*a) for a in acc_shapes(OUT, 32, (0,))],
-        in_specs=[vmem] * 7, out_specs=[vmem] * 6,
+        in_specs=[vmem] * 9, out_specs=[vmem] * 4,
         scratch_shapes=[pltpu.VMEM((n_k, n_q), f32), pltpu.VMEM((TILE, n_k), bf),
                         pltpu.VMEM((tiles, n_k, TILE), f32), pltpu.VMEM((tiles, n_k, TILE), f32),
                         pltpu.VMEM((tiles, n_k, TILE), bf), pltpu.VMEM((tiles, n_k, TILE), bf),
                         pltpu.VMEM((n_k, TILE), f32), pltpu.VMEM((n_k, TILE), f32),
+                        pltpu.VMEM((n_q, 2 * TILE), bf), pltpu.VMEM((n_q, 2 * TILE), bf),
                         pltpu.VMEM((dz.shape[1], n_q), bf), pltpu.VMEM((dz.shape[1] // 32, 32, o.shape[1] // 2), f32)]
         + [pltpu.VMEM((dz.shape[1] // 32, 32, o.shape[1] // 2), bf)] * 2
         + wire_shapes(OUT, bf, 32, (0,)) * 2 + [pltpu.SemaphoreType.DMA((3, 3, 4))] * 2
-        + [pltpu.SemaphoreType.DMA((o.shape[1] // 2 // CHUNK,))] * 2,
+        + [pltpu.SemaphoreType.DMA((o.shape[1] // 2 // CHUNK,))] * 2 + [pltpu.SemaphoreType.DMA((2,))],
         compiler_params=pltpu.CompilerParams(collective_id=4, has_side_effects=True, vmem_limit_bytes=VMEM_MAX),
-    )(q, do, kv, pos, inv_sum, dz, o)
+    )(q, do, kv, pos, inv_sum, dz, o, cos_t, sin_t)
 
 
 def rope_tables(pos_ids, head_dim):
@@ -686,12 +761,11 @@
         n_heads, head_dim = w_query.shape[1], w_query.shape[2]
         rows = w_query.shape[0]
         q_cols = n_heads * head_dim
-        core = lax.axis_index('cp')
         w0 = jnp.concatenate([w_query.reshape(rows, q_cols), w_key.reshape(rows, head_dim),
                               w_value.reshape(rows, head_dim)], axis=1)
         w1 = w_out.reshape(q_cols, rows).T
         lane = lax.rem(lax.axis_index('fsdp'), SIDE) * rows
-        w2 = jnp.zeros((16, 256), f32)
+        w2 = jnp.zeros((8, 256), f32)
         for kind, g in enumerate((gain_pre, gain_post)):
             w2 = lax.dynamic_update_slice(w2, g.astype(f32)[None], (0, kind * 128 + lane))
         cos_t, sin_t = rope_tables(doc_pos[0], head_dim)
@@ -699,10 +773,9 @@
         ratio = q_scale / SOFT_CAP
         wqkv, wo_t, gains, normed, inv_pre, q_flat, kv_all, attn_flat, inv_sum = forward(
             hidden, cos_t[:, 0], sin_t[:, 0], doc_pos, w0, w1, w2, n_heads, ratio)
-        pre_full, post_full = gains[0], gains[1]
-        wqkv = wqkv.reshape(model_dim, q_cols + 2 * head_dim)
+        post_full = gains[1]
+        wqkv = wqkv.reshape(model_dim // rows, rows, q_cols + 2 * head_dim)
         wo_t = wo_t.reshape(model_dim, q_cols)
-        swap = [(0, 1), (1, 0)]
         proj_out = dot(attn_flat, wo_t, (1, 1)).astype(bf)
         post_out, inv_post = norm_forward(proj_out, post_full)
         out_hidden = (hidden.astype(f32) + post_out.astype(f32)).astype(bf)
@@ -711,29 +784,12 @@
         d_proj = d_proj.astype(bf)
         d_attn = dot(d_proj, wo_t, (1, 0)).astype(bf)
 
-        d_q_flat, d_k, d_v, *accs = attend_back(q_flat, d_attn, kv_all, doc_pos, inv_sum, d_proj, attn_flat, ratio)
-        d_kv = jnp.concatenate([d_k, d_v], axis=1)
-        d_kv = (d_kv[n_tok:].astype(f32) + lax.ppermute(d_kv[:n_tok], 'cp', swap).astype(f32)).astype(bf)
-        d_k_rot, d_v_proj = d_kv[:, :head_dim], d_kv[:, head_dim:]
-        d_q_rot = d_q_flat.reshape(n_tok, n_heads, head_dim)
-        d_q_proj = rotate(d_q_rot, cos_t, -sin_t)
-        d_k_proj = rotate(d_k_rot[:, None], cos_t, -sin_t)[:, 0]
-        d_qkv = jnp.concatenate([d_q_proj.reshape(n_tok, q_cols), d_k_proj, d_v_proj], axis=1)
-
-        d_normed = dot(d_qkv, wqkv, (1, 1)).astype(bf)
-        d_hidden, d_gain_pre = norm_backward(hidden, inv_pre, pre_full, d_normed)
-        grad_hidden = (grad_out.astype(f32) + d_hidden).astype(bf)
-        d_gains = jnp.stack([d_gain_pre, d_gain_post]).reshape(2, model_dim // rows, 1, rows)
-        d_gains = jnp.pad(d_gains, ((0, 0), (0, 0), (0, 15), (0, 128 - rows)))
-        own_g = lax.dynamic_index_in_dim(d_gains, core, 0, keepdims=False)
-        sib_g = lax.dynamic_index_in_dim(d_gains, 1 - core, 0, keepdims=False)
-        g0, g1, gg = scatter_grads(normed, d_qkv, own_g, sib_g, accs)
-        g0 = jnp.concatenate([g0[0], g0[1]], axis=1)
-        g1 = jnp.concatenate([g1[0], g1[1]], axis=1)
-        return (out_hidden[None], grad_hidden[None], g0[:, :q_cols].reshape(rows, n_heads, head_dim),
-                g0[:, q_cols:q_cols + head_dim].reshape(rows, 1, head_dim),
-                g0[:, q_cols + head_dim:].reshape(rows, 1, head_dim),
-                g1.T.reshape(n_heads, head_dim, rows), gg[0, 0, :rows], gg[1, 0, :rows])
+        d_qkv, *accs = attend_back(q_flat, d_attn, kv_all, doc_pos, inv_sum, d_proj, attn_flat, cos_t[:, 0], sin_t[:, 0], ratio)
+        dx, g_q, g_k, g_v, g_o, g_g = scatter_grads(normed, d_qkv, wqkv, hidden, grad_out, inv_pre, gains,
+                                                    d_gain_post[None], accs, n_heads)
+        g_g = lax.dynamic_slice(g_g, (0, 0, lane), (2, 1, rows))[:, 0]
+        return (out_hidden[None], dx[None], g_q, g_k[:, None], g_v[:, None], g_o.reshape(n_heads, head_dim, rows),
+                g_g[0], g_g[1])
 
     return jax.shard_map(layer_local, mesh=mesh,
                          in_specs=(tok_spec, ids_spec, ids_spec, tok_spec, in_spec, in_spec, in_spec, out_spec, gain_spec, gain_spec),

time: 252 us -> 230 us (0.913)
  other arithmetic: 23.4 us -> 10.9 us
  matrix products: 25.7 us -> 14.5 us
  Pallas kernels: 183 us -> 189 us
  local copies, waits for them, and re-layouts: 18.1 us -> 14.7 us
    pallas_call x1, Pallas kernels: 57.7 us -> 73.8 us  [scatter_grads(): pl.pallas_call(scatter_kernel, name='scatter_grads', out_shape=[jax.Shape...]
    dot_general x3 -> x2, matrix products: 25.7 us -> 14.5 us  [dot(): lax.dot_general(a, b, ((dims[:1], dims[1:]), ((), ())), preferred_element...]
    pallas_call x1, Pallas kernels: 83 us -> 71.8 us  [forward(): pl.pallas_call(functools.partial(forward_kernel, ratio), name='forward',...]
    broadcast_in_dim x1 -> x0, other arithmetic: 5 us -> none  [layer_local(): grad_hidden[None]]
    unnamed x41 -> x18, local copies, waits for them, and re-layouts: 7.56 us -> 11.5 us
    squeeze x4 -> x1, local copies, waits for them, and re-layouts: 4.98 us -> 1.32 us  [layer_local(): g_g[1]]
    concatenate x5 -> x0, other arithmetic: 3.19 us -> none  [the longest x1 1.7 us: layer_local(): jnp.concatenate([d_q_proj.reshape(n_tok, q_cols), d_k_proj, d_v_proj], ax...]
  transfers between devices with their start and end apart: 1 -> 0, of which waited for: 0 -> 0; matrix products, arithmetic and copies ran while one was open for 2% -> 0% of each run, Pallas kernels for 0% -> 0%
where the time goes in v5:
time: 230 us
  Pallas kernels  189 us (82%)
  local copies, waits for them, and re-layouts  14.7 us (6%)
  matrix products  14.5 us (6%)
  other arithmetic  10.9 us (5%)
    pallas_call x1, Pallas kernels, scatter_grads(): pl.pallas_call(scatter_kernel, name='scatter_grads', out_shape=[jax.Shape...  73.8 us
    pallas_call x1, Pallas kernels, forward(): pl.pallas_call(functools.partial(forward_kernel, ratio), name='forward',...  71.8 us
    pallas_call x1, Pallas kernels, attend_back(): pl.pallas_call(functools.partial(attend_back_kernel, ratio), name='attend...  43.2 us
    dot_general x2, matrix products, dot(): lax.dot_general(a, b, ((dims[:1], dims[1:]), ((), ())), preferred_element...  14.5 us
    unnamed x18, local copies, waits for them, and re-layouts  11.5 us

profile of v5, /device:TPU:1, one launch (start us, length us, event | category | flops | bytes accessed | tf_op | source)
XLA Modules:
  0.0 229.7 jit_solution(13358308837613253001)
XLA Ops:
  0.6 0.7 bitcast_convert_fusion.1
  1.3 0.7 bitcast_convert_fusion
  2.0 0.7 convert_element_type.41
  2.7 0.1 dynamic_update_slice.6
  2.8 0.2 dynamic_update_slice.7.in2
  3.0 0.0 copy-start.4
  3.0 0.9 copy.22
  3.9 1.4 pad_maximum_fusion.in0
  5.4 0.0 copy-done.4
  5.4 1.6 copy.21
  6.9 1.8 multiply_sine_fusion
  8.7 71.8 %forward.1 = (bf16[4,4,4,32,2560]{4,3,2,1,0:T(8,128)(2,1)}, bf16[4,4,4,32,2048]{4,3,2,1,0:T(8,128)(2,1)}, f32[2,2048]{1,0:T(2,128)}, bf16[512,2048]{1,0:T(8,128)...) custom-call(bf16[512,2048]{1,0:T(8,128)(2,1)} %bitcast.40, ...), custom_call_target="tpu_custom_call" | custom-call | tf_op jit(solution)/shard_map/forward/pallas_call | solution.py:589
  80.5 0.7 slice_add_fusion
  81.3 0.0 copy-start
  81.3 8.8 %fusion.3 = (f32[512]{0:T(512)S(1)}, bf16[512,2048]{1,0:T(8,128)(2,1)S(1)}) fusion(bf16[512,2048]{1,0:T(8,128)(2,1)} %get-tuple-element.27.o_ref, bf16[2048,2048]{1,0:T(8,128)(2,1)} %bitcast.57), kind=kOutput, calls=%fused_computation.9 | convolution fusion | flops 4299161088 | bytes 12584960 | tf_op jit(solution)/shard_map/dot_general | solution.py:747
  90.0 0.0 copy-start.1
  90.1 0.0 copy-done
  90.1 2.0 fusion.9
  92.1 0.0 copy-done.1
  92.1 0.0 copy-start.5
  92.1 3.0 %fusion.2 = (bf16[512,2048]{1,0:T(8,128)(2,1)S(1)}, bf16[1,512,2048]{2,1,0:T(8,128)(2,1)}) fusion(bf16[512,2048]{1,0:T(8,128)(2,1)S(1)} %get-tuple-element.65, f32[512]{0:T(512)S(1)} %broadcast_multiply_fusion, f32[512]{0:T(512)S(1)} %get-tuple-element.62, f32[2048]{0:T(1024)S(1)} %bitcast.50, f32[512]{0:T(512)S(1)} %get-tuple-element.63, ...), kind=kLoop, calls=%fused_computation.8 | loop fusion | flops 15728640 | bytes 10500096 | tf_op jit(solution)/shard_map/convert_element_type | solution.py:784
  95.1 0.0 copy-start.2
  95.1 1.4 copy-done.2
  96.4 0.3 copy-done.5
  96.7 5.7 %convolution_convert_fusion.do_ref = bf16[512,2048]{1,0:T(8,128)(2,1)} fusion(bf16[512,2048]{1,0:T(8,128)(2,1)S(1)} %get-tuple-element.56.dz_ref, bf16[2048,2048]{1,0:T(8,128)(2,1)S(1)} %bitcast.58), kind=kOutput, calls=%fused_computation.17 | convolution fusion | flops 4296015872 | bytes 12582912 | tf_op jit(solution)/shard_map/dot_general | solution.py:747
  102.4 43.2 %attend_back.1 = (bf16[512,2560]{1,0:T(8,128)(2,1)}, f32[16,32,256]{2,1,0:T(8,128)}, f32[16,32,384]{2,1,0:T(8,128)}, f32[16,32,384]{2,1,0:T(8,128)}) custom-call(bf16[512,2048]{1,0:T(8,128)(2,1)} %get-tuple-element.31.q_ref, bf16[512,2048]{1,0:T(8,128)(2,1)} %convolution_convert_fusion.do_ref, bf16[1024,512]{1,0:T(8,128)(2,1)} %get-tuple-element.32.kv_ref, ...), custom_call_target="tpu_custom_call" | custom-call | tf_op jit(solution)/shard_map/attend_back/pallas_call | solution.py:696
  145.6 73.8 %scatter_grads.1 = (bf16[512,2048]{1,0:T(8,128)(2,1)}, f32[32,8,256]{2,1,0:T(8,128)}, f32[32,256]{1,0:T(8,128)}, f32[32,256]{1,0:T(8,128)}, f32[2048,32]{1,0:T(8,128)}, /*index=5*/f32[2,16,128]{2,1,0:T(8,128)}) custom-call(bf16[512,2048]{1,0:T(8,128)(2,1)} %get-tuple-element.30.normed, bf16[512,2560]{1,0:T(8,128)(2,1)} %get-tuple-element.34.d_qkv, ...), custom_call_target="tpu_custom_call" | custom-call | tf_op jit(solution)/shard_map/scatter_grads/pallas_call | solution.py:413
  219.4 0.0 copy-start.3
  219.4 1.3 dynamic-slice_bitcast_fusion
  220.7 1.4 copy.18
  222.1 1.4 copy.19
  223.5 2.2 copy.20
  225.8 3.2 %copy.27 = bf16[1,512,2048]{2,1,0:T(8,128)(2,1)} copy(bf16[1,512,2048]{2,1,0:T(8,128)(2,1)} %bitcast.43) | data formatting | bytes 4194304
  228.9 0.0 copy-done.3
  228.9 0.7 copy.28
  (4 shorter events, 0.0 us)
Async XLA Ops:
  3.0 2.4 %copy-start.4 = (f32[8,256]{1,0:T(8,128)}, f32[8,256]{1,0:T(8,128)S(1)}, u32[]{:S(2)}) copy-start(f32[8,256]{1,0:T(8,128)S(1)} %dynamic_update_slice.7.in2) | copy-start | bytes 24580
  81.3 8.8 %copy-start = (bf16[1,512,2048]{2,1,0:T(8,128)(2,1)S(1)}, bf16[1,512,2048]{2,1,0:T(8,128)(2,1)}, u32[]{:S(2)}) copy-start(bf16[1,512,2048]{2,1,0:T(8,128)(2,1)} %param.12) | copy-start | bytes 6291460
  90.0 2.1 copy-start.1
  92.1 4.6 %copy-start.5 = (bf16[4,4,4,32,2048]{4,3,2,1,0:T(8,128)(2,1)S(1)}, bf16[4,4,4,32,2048]{4,3,2,1,0:T(8,128)(2,1)}, u32[]{:S(2)}) copy-start(bf16[4,4,4,32,2048]{4,3,2,1,0:T(8,128)(2,1)} %get-tuple-element.28) | copy-start | bytes 25165828
  95.1 1.4 copy-start.2
  219.4 9.5 %copy-start.3 = (f32[32,8,256]{2,1,0:T(8,128)S(1)}, f32[32,8,256]{2,1,0:T(8,128)}, u32[]{:S(2)}) copy-start(f32[32,8,256]{2,1,0:T(8,128)} %get-tuple-element.76) | copy-start | bytes 786436

commit v6 on v5

--- a/solution.py
+++ b/solution.py
@@ -14,9 +14,8 @@
 SIDE = 4
 VMEM_MAX = 67_043_328
 
-QKV_IN = ((0, 0, 256), (1, 512, 256), (2, 896, 256), (0, 256, 256), (1, 768, 128), (2, 1152, 128))
-QKV = ((0, 0, 256), (0, 256, 256), (1, 512, 256), (1, 768, 128), (2, 896, 256), (2, 1152, 128))
-OUT = ((0, 0, 256), (1, 256, 384), (2, 640, 384))
+QKV = ((0, 0, 256), (1, 256, 256), (2, 512, 256), (0, 768, 256), (1, 1024, 128), (2, 1152, 128))
+OUT = ((0, 0, 256), (1, 256, 256), (2, 512, 256), (1, 768, 128), (2, 896, 128))
 GAIN = ((0, 0, 128),)
 CHUNK = 256
 
@@ -167,7 +166,7 @@
         def step(i, carry):
             body(i)
             return carry
-        lax.fori_loop(0, n, step, 0, unroll=min(n, 2))
+        lax.fori_loop(0, n, step, 0, unroll=min(n, 4))
 
     def one(self, s, q):
         dim, half, buf = self.dim(s, q), self.half(s), self.sbuf[s][q]
@@ -253,8 +252,10 @@
     return [((SIDE ** (2 - q), rows, width), jnp.float32) for _, _, width in streams for q in phases]
 
 
-def scatter_kernel(normed, d_qkv, w_ref, x_ref, dy_ref, inv_rms, gain, post_row, acc_o0, acc_o1, acc_o2,
-                   dx_ref, grad_q, grad_k, grad_v, grad_o, out_g, *scratch):
+def scatter_kernel(normed, d_qkv, w_ref, x_ref, dy_ref, inv_rms, gain, post_row, *refs):
+    no = len(OUT)
+    acc_in, scratch = refs[:no], refs[no + 6:]
+    dx_ref, grad_q, grad_k, grad_v, grad_o, out_g = refs[no:no + 6]
     scratch = list(scratch)
 
     def take(n):
@@ -264,7 +265,7 @@
     normed_t, own_q, sib_out, sib_q, own_g, sib_g, sib_in_g, out_q, out_o, w_buf, dn, pre_row = take(12)
     nq = len(QKV)
     acc_q, sbuf_q, rbuf_q = take(3 * nq), take(3 * nq), take(3 * nq)
-    acc_o, sbuf_o, rbuf_o = take(6), take(6), take(6)
+    acc_o, sbuf_o, rbuf_o = take(2 * no), take(2 * no), take(2 * no)
     acc_g, sbuf_g, rbuf_g = take(3), take(3), take(3)
     sems = take(6)
     gift_send, gift_recv, gain_sem, fin_send, fin_recv, w_sem = take(6)
@@ -279,46 +280,49 @@
         return [flat[3 * s:3 * s + 3] for s in range(len(flat) // 3)]
 
     def tails(flat, heads):
-        return [[heads[s]] + flat[2 * s:2 * s + 2] for s in range(3)]
+        return [[heads[s]] + flat[2 * s:2 * s + 2] for s in range(no)]
     qkv = Scatter(QKV, own_q, sib_q, triples(acc_q), triples(sbuf_q), triples(rbuf_q), *sems[0:2])
-    out = Scatter(OUT, None, None, tails(acc_o, (acc_o0, acc_o1, acc_o2)), tails(sbuf_o, (None,) * 3),
-                  tails(rbuf_o, (None,) * 3), *sems[2:4])
+    out = Scatter(OUT, None, None, tails(acc_o, acc_in), tails(sbuf_o, (None,) * no),
+                  tails(rbuf_o, (None,) * no), *sems[2:4])
     gains = Scatter(GAIN, own_g, sib_in_g, triples(acc_g), triples(sbuf_g), triples(rbuf_g), *sems[4:6])
     gain_gift = pltpu.make_async_remote_copy(sib_g, sib_in_g, gain_sem.at[0], gain_sem.at[1],
                                              device_id=sibling, device_id_type=MESH)
     loads = [pltpu.make_async_copy(w_ref.at[pl.ds(8 * j, 8)], w_buf.at[j % 2], w_sem.at[j]) for j in range(strips)]
     loads[0].start()
     loads[1].start()
-    for s in range(3):
+    for s in range(len(OUT)):
         out.one(s, 1)
     own_g[...] = jnp.zeros_like(own_g)
     sib_g[...] = jnp.zeros_like(sib_g)
     transpose_into(normed_t, normed)
     chunks = own_q.shape[2] // CHUNK
     gifts = [chunk_gift(sib_out, sib_q, gift_send, gift_recv, j) for j in range(chunks)]
+    grad_chunk(normed_t, d_qkv, sib_out, 1 - core, 0)
+    gifts[0].start()
+    ready = 0
     for j in range(chunks):
-        grad_chunk(normed_t, d_qkv, sib_out, 1 - core, j)
-        gifts[j].start()
-    for s in range(3):
-        out.two(s, 1)
-    done = 0
-    for s, (_, off, width) in enumerate(QKV):
-        while done * CHUNK < off + width:
-            grad_chunk(normed_t, d_qkv, own_q, core, done)
-            gifts[done].wait_recv()
-            done += 1
-        qkv.one(s, 0)
-        if s == 0:
-            for i in range(3):
-                out.three(i, 1)
-                out.one(i, 2)
+        if j + 1 < chunks:
+            grad_chunk(normed_t, d_qkv, sib_out, 1 - core, j + 1)
+            gifts[j + 1].start()
+        grad_chunk(normed_t, d_qkv, own_q, core, j)
+        gifts[j].wait_recv()
+        while ready < nq and QKV[ready][1] + QKV[ready][2] <= (j + 1) * CHUNK:
+            qkv.one(ready, 0)
+            ready += 1
+        if j == 1:
+            for s in range(no):
+                out.two(s, 1)
+        if j == 3:
+            for s in range(no):
+                out.three(s, 1)
+                out.one(s, 2)
     for j in range(strips):
         loads[j].wait()
         dn[:, pl.ds(j * CHUNK, CHUNK)] = nt(d_qkv[...], w_buf[j % 2].reshape(CHUNK, d_qkv.shape[1])).astype(bf)
         if j + 2 < strips:
             loads[j + 2].start()
     work = [(qkv, s) for s in range(nq)]
-    for s in range(3):
+    for s in range(len(OUT)):
         out.two(s, 2)
     for scatter, s in work:
         scatter.two(s, 0)
@@ -344,7 +348,7 @@
     for scatter, s in work:
         scatter.three(s, 0)
         scatter.one(s, 1)
-    for s in range(3):
+    for s in range(len(OUT)):
         out.three(s, 2)
     gain_gift.wait_recv()
     gains.one(0, 0)
@@ -381,9 +385,9 @@
         if h < n_heads:
             grad_q[:, h, :] = part
         else:
-            (grad_k, grad_v)[h - n_heads][...] = part
-    for side in range(2):
-        grad_o[pl.ds(side * out_o.shape[2], out_o.shape[2]), :] = out_o[side].T
+            (grad_k, grad_v)[h - n_heads][:, 0, :] = part
+    for h in range(n_heads):
+        grad_o[h] = out_o[h // 4, :, pl.ds(h % 4 * TILE, TILE)]
     for copy in gifts + [gain_gift]:
         copy.wait_send()
     for scatter, phases in ((qkv, (0, 1, 2)), (out, (1, 2)), (gains, (0, 1, 2))):
@@ -409,13 +413,13 @@
         scratch += [pltpu.VMEM(*a) for a in acc_shapes(streams, n_rows, phases)]
         scratch += wire_shapes(streams, dtype, n_rows, phases) * 2
     scratch += [dma((len(st), 3, 4)) for st in (QKV, OUT, GAIN) for _ in range(2)]
-    scratch += [dma((half // CHUNK,))] * 2 + [dma((2,))] + [dma((len(QKV) + 4,))] * 2 + [dma((model_dim // CHUNK,))]
+    scratch += [dma((half // CHUNK,))] * 2 + [dma((2,))] + [dma((len(QKV) + len(OUT) + 1,))] * 2 + [dma((model_dim // CHUNK,))]
     return pl.pallas_call(
         scatter_kernel, name="scatter_grads",
         out_shape=[jax.ShapeDtypeStruct((n_tok, model_dim), bf), jax.ShapeDtypeStruct((rows, n_heads, TILE), f32),
-                   jax.ShapeDtypeStruct((rows, TILE), f32), jax.ShapeDtypeStruct((rows, TILE), f32),
-                   jax.ShapeDtypeStruct((n_heads * TILE, rows), f32), jax.ShapeDtypeStruct((2, 16, 128), f32)],
-        in_specs=[vmem] * 2 + [pl.BlockSpec(memory_space=pltpu.HBM)] + [vmem] * 8, out_specs=[vmem] * 6,
+                   jax.ShapeDtypeStruct((rows, 1, TILE), f32), jax.ShapeDtypeStruct((rows, 1, TILE), f32),
+                   jax.ShapeDtypeStruct((n_heads, rows, TILE), f32), jax.ShapeDtypeStruct((2, 16, 128), f32)],
+        in_specs=[vmem] * 2 + [pl.BlockSpec(memory_space=pltpu.HBM)] + [vmem] * (5 + len(OUT)), out_specs=[vmem] * 6,
         scratch_shapes=scratch,
         compiler_params=pltpu.CompilerParams(collective_id=2, has_side_effects=True, vmem_limit_bytes=VMEM_MAX),
     )(normed, d_qkv, w, x, dy, inv_rms, gain, post_row, *accs)
@@ -459,12 +463,12 @@
     greet(coords, core, (1, -1, 2))
     own_sem, swap_send, swap_recv = sems[12:15]
     qkv, out, gain = (Gather(st, src, dst, direct, *sems[4 * g:4 * g + 4]) for g, (st, src, dst, direct) in enumerate(
-        ((QKV_IN, in0, wq, (0,)), (OUT, in1, wo_out, (0,)), (GAIN, in2, gains, (0, 1, 2)))))
-    nq = range(len(QKV_IN))
+        ((QKV, in0, wq, (0,)), (OUT, in1, wo_out, (0,)), (GAIN, in2, gains, (0, 1, 2)))))
+    nq = range(len(QKV))
     gain.start(0, 0)
     for s in nq:
         qkv.start(s, 0)
-    for s in range(3):
+    for s in range(len(OUT)):
         out.start(s, 0)
     own_out = pltpu.make_async_copy(in1, wo_out.at[coords[0], coords[1], coords[2]], own_sem.at[0])
     own_out.start()
@@ -484,12 +488,12 @@
         qkv.start(s, 1)
     gain.middle(0, 1)
     gain.start(0, 2)
-    for s in range(3):
+    for s in range(len(OUT)):
         out.middle(s, 0)
     own_out.wait()
     for s in nq:
         qkv.middle(s, 1)
-    for s in range(3):
+    for s in range(len(OUT)):
         out.start(s, 1)
     gain.middle(0, 2)
     for s in nq:
@@ -511,11 +515,11 @@
     lax.fori_loop(0, n_q // 64, scale, 0)
     for s in nq:
         qkv.middle(s, 2)
-    for s in range(3):
+    for s in range(len(OUT)):
         out.middle(s, 1)
     for s in nq:
         qkv.finish(s, 2)
-    for s in range(3):
+    for s in range(len(OUT)):
         out.finish(s, 1)
         out.start(s, 2)
     for s in nq:
@@ -544,7 +548,7 @@
         q_ref[:, pl.ds(pl.multiple_of(h * TILE, TILE), TILE)] = rope(project(h))
         return carry
     lax.fori_loop(0, n_heads, project_head, 0)
-    for s in range(3):
+    for s in range(len(OUT)):
         out.middle(s, 2)
     swap.wait_recv()
     k_cols = pl.ds(0, TILE)
@@ -568,9 +572,9 @@
             o_ref[pl.ds(i * TILE, TILE), cols] = o_t.T.astype(bf)
         return carry
     lax.fori_loop(0, n_heads, head, 0)
-    for s in range(3):
+    for s in range(len(OUT)):
         out.finish(s, 2)
-    for s in range(3):
+    for s in range(len(OUT)):
         for p in range(3):
             out.drain(s, p)
     swap.wait_send()
@@ -595,21 +599,23 @@
         scratch_shapes=[pltpu.VMEM(grid + w0.shape, bf), pltpu.VMEM(grid + w2.shape, f32), pltpu.VMEM((2, dim), f32),
                         pltpu.VMEM((n_k, n_q), f32), pltpu.VMEM((TILE, n_k), bf),
                         pltpu.VMEM((tiles, n_k, TILE), f32), pltpu.VMEM((tiles, n_k, TILE), bf)]
-        + [dma((len(st), 3, 4)) for st in (QKV_IN, OUT, GAIN) for _ in range(4)]
+        + [dma((len(st), 3, 4)) for st in (QKV, OUT, GAIN) for _ in range(4)]
         + [dma((2,)), dma((1,)), dma((1,))],
         compiler_params=pltpu.CompilerParams(collective_id=1, has_side_effects=True, vmem_limit_bytes=VMEM_MAX),
     )(x, cos_t, sin_t, pos, w0, w1, w2)
 
 
 def attend_back_kernel(ratio, q_ref, do_ref, kv_ref, pos, inv_ref, dz_ref, o_ref, cos_ref, sin_ref,
-                       dqkv_ref, acc0, acc1, acc2,
-                       mask, k_t, g_scr, dp_scr, p_scr, ds_scr, dk_acc, dv_acc, dkv_out, dkv_in, dz_t, own, sib_out, sib_in,
-                       *scratch):
+                       dqkv_ref, *refs):
+    no = len(OUT)
+    accs = refs[:no]
+    (mask, k_t, g_scr, dp_scr, p_scr, ds_scr, dk_acc, dv_acc, dkv_out, dkv_in, dz_t, own, sib_out, sib_in,
+     *scratch) = refs[no:]
     n_q = q_ref.shape[0]
     coords, core = place()
     greet(coords, core)
-    sbuf, rbuf, sems = scratch[0:3], scratch[3:6], scratch[6:8]
-    gift_send, gift_recv, swap_sem = scratch[8:11]
+    sbuf, rbuf, sems = scratch[:no], scratch[no:2 * no], scratch[2 * no:2 * no + 2]
+    gift_send, gift_recv, swap_sem = scratch[2 * no + 2:]
     bf, f32 = jnp.bfloat16, jnp.float32
     swap = pltpu.make_async_remote_copy(dkv_out, dkv_in, swap_sem.at[0], swap_sem.at[1],
                                         device_id=device(coords, 1 - core), device_id_type=MESH)
@@ -618,20 +624,22 @@
         lo, hi = u[:, :TILE // 2].astype(f32), u[:, TILE // 2:].astype(f32)
         c, s = cos_ref[pl.ds(0, u.shape[0]), :], sin_ref[pl.ds(0, u.shape[0]), :]
         return jnp.concatenate([lo * c + hi * s, hi * c - lo * s], axis=1).astype(bf)
-    out = Scatter(OUT, own, sib_in, [[a] for a in (acc0, acc1, acc2)], [[b] for b in sbuf], [[b] for b in rbuf], *sems)
+    out = Scatter(OUT, own, sib_in, [[a] for a in accs], [[b] for b in sbuf], [[b] for b in rbuf], *sems)
     chunks = own.shape[2] // CHUNK
     transpose_into(dz_t, dz_ref)
     gifts = [chunk_gift(sib_out, sib_in, gift_send, gift_recv, j) for j in range(chunks)]
+    grad_chunk(dz_t, o_ref, sib_out, 1 - core, 0)
+    gifts[0].start()
+    ready = 0
     for j in range(chunks):
-        grad_chunk(dz_t, o_ref, sib_out, 1 - core, j)
-        gifts[j].start()
-    done = 0
-    for s, (_, off, width) in enumerate(OUT):
-        while done * CHUNK < off + width:
-            grad_chunk(dz_t, o_ref, own, core, done)
-            gifts[done].wait_recv()
-            done += 1
-        out.one(s, 0)
+        if j + 1 < chunks:
+            grad_chunk(dz_t, o_ref, sib_out, 1 - core, j + 1)
+            gifts[j + 1].start()
+        grad_chunk(dz_t, o_ref, own, core, j)
+        gifts[j].wait_recv()
+        while ready < no and OUT[ready][1] + OUT[ready][2] <= (j + 1) * CHUNK:
+            out.one(ready, 0)
+            ready += 1
     fill_mask(mask, pos)
     k_cols, v_cols = pl.ds(0, TILE), pl.ds(TILE, TILE)
     k_t[...] = kv_ref[:, k_cols].T
@@ -668,21 +676,24 @@
 
         @pl.when(h == 3)
         def _():
-            for s in range(3):
+            for s in range(no):
                 out.two(s, 0)
+
+        @pl.when(h == 6)
+        def _():
+            for s in range(no):
+                out.three(s, 0)
         return carry
     lax.fori_loop(0, q_ref.shape[1] // TILE, head, 0)
     mine, other = pl.ds(n_q, n_q), pl.ds(0, n_q)
     dkv_out[:, k_cols] = dk_acc[other, :].astype(bf)
     dkv_out[:, v_cols] = dv_acc[other, :].astype(bf)
     swap.start()
-    for s in range(3):
-        out.three(s, 0)
     swap.wait_recv()
     q_cols = q_ref.shape[1]
     dqkv_ref[:, pl.ds(q_cols, TILE)] = rope_back((dk_acc[mine, :] + dkv_in[:, k_cols].astype(f32)).astype(bf))
     dqkv_ref[:, pl.ds(q_cols + TILE, TILE)] = (dv_acc[mine, :] + dkv_in[:, v_cols].astype(f32)).astype(bf)
-    for s in range(3):
+    for s in range(len(OUT)):
         out.drain(s, 0)
     for copy in gifts + [swap]:
         copy.wait_send()
@@ -697,7 +708,7 @@
         functools.partial(attend_back_kernel, ratio), name="attend_back",
         out_shape=[jax.ShapeDtypeStruct((n_q, q.shape[1] + 2 * TILE), bf)]
         + [jax.ShapeDtypeStruct(*a) for a in acc_shapes(OUT, 32, (0,))],
-        in_specs=[vmem] * 9, out_specs=[vmem] * 4,
+        in_specs=[vmem] * 9, out_specs=[vmem] * (1 + len(OUT)),
         scratch_shapes=[pltpu.VMEM((n_k, n_q), f32), pltpu.VMEM((TILE, n_k), bf),
                         pltpu.VMEM((tiles, n_k, TILE), f32), pltpu.VMEM((tiles, n_k, TILE), f32),
                         pltpu.VMEM((tiles, n_k, TILE), bf), pltpu.VMEM((tiles, n_k, TILE), bf),
@@ -705,7 +716,7 @@
                         pltpu.VMEM((n_q, 2 * TILE), bf), pltpu.VMEM((n_q, 2 * TILE), bf),
                         pltpu.VMEM((dz.shape[1], n_q), bf), pltpu.VMEM((dz.shape[1] // 32, 32, o.shape[1] // 2), f32)]
         + [pltpu.VMEM((dz.shape[1] // 32, 32, o.shape[1] // 2), bf)] * 2
-        + wire_shapes(OUT, bf, 32, (0,)) * 2 + [pltpu.SemaphoreType.DMA((3, 3, 4))] * 2
+        + wire_shapes(OUT, bf, 32, (0,)) * 2 + [pltpu.SemaphoreType.DMA((len(OUT), 3, 4))] * 2
         + [pltpu.SemaphoreType.DMA((o.shape[1] // 2 // CHUNK,))] * 2 + [pltpu.SemaphoreType.DMA((2,))],
         compiler_params=pltpu.CompilerParams(collective_id=4, has_side_effects=True, vmem_limit_bytes=VMEM_MAX),
     )(q, do, kv, pos, inv_sum, dz, o, cos_t, sin_t)
@@ -788,7 +799,7 @@
         dx, g_q, g_k, g_v, g_o, g_g = scatter_grads(normed, d_qkv, wqkv, hidden, grad_out, inv_pre, gains,
                                                     d_gain_post[None], accs, n_heads)
         g_g = lax.dynamic_slice(g_g, (0, 0, lane), (2, 1, rows))[:, 0]
-        return (out_hidden[None], dx[None], g_q, g_k[:, None], g_v[:, None], g_o.reshape(n_heads, head_dim, rows),
+        return (out_hidden[None], dx[None], g_q, g_k, g_v, g_o.transpose(0, 2, 1),
                 g_g[0], g_g[1])
 
     return jax.shard_map(layer_local, mesh=mesh,

time: 230 us -> 229 us (level)
  local copies, waits for them, and re-layouts: 14.7 us -> 11.6 us
    unnamed x18 -> x24, local copies, waits for them, and re-layouts: 11.5 us -> 8.37 us
where the time goes in v6:
time: 229 us; the launch traced here: 228 us
  Pallas kernels  191 us (83%)
  matrix products  14.5 us (6%)
  local copies, waits for them, and re-layouts  11.6 us (5%)
  other arithmetic  10.9 us (5%)
    pallas_call x1, Pallas kernels, scatter_grads(): pl.pallas_call(scatter_kernel, name='scatter_grads', out_shape=[jax.Shape...  73.2 us
    pallas_call x1, Pallas kernels, forward(): pl.pallas_call(functools.partial(forward_kernel, ratio), name='forward',...  72.3 us
    pallas_call x1, Pallas kernels, attend_back(): pl.pallas_call(functools.partial(attend_back_kernel, ratio), name='attend...  45 us
    dot_general x2, matrix products, dot(): lax.dot_general(a, b, ((dims[:1], dims[1:]), ((), ())), preferred_element...  14.5 us
    unnamed x24, local copies, waits for them, and re-layouts  8.37 us

profile of v6, /device:TPU:1, one launch (start us, length us, event | category | flops | bytes accessed | tf_op | source)
XLA Modules:
  0.0 228.4 jit_solution(4273856604810577467)
XLA Ops:
  0.6 0.7 bitcast_convert_fusion.1
  1.3 0.7 bitcast_convert_fusion
  2.0 0.7 convert_element_type.41
  2.7 0.1 dynamic_update_slice.6
  2.8 0.2 dynamic_update_slice.7.in2
  3.0 0.0 copy-start.5
  3.0 0.9 copy.19
  3.9 1.4 pad_maximum_fusion.in0
  5.4 0.0 copy-done.5
  5.4 1.6 copy.18
  6.9 1.8 multiply_sine_fusion
  8.7 72.3 %forward.1 = (bf16[4,4,4,32,2560]{4,3,2,1,0:T(8,128)(2,1)}, bf16[4,4,4,32,2048]{4,3,2,1,0:T(8,128)(2,1)}, f32[2,2048]{1,0:T(2,128)}, bf16[512,2048]{1,0:T(8,128)...) custom-call(bf16[512,2048]{1,0:T(8,128)(2,1)} %bitcast.38, ...), custom_call_target="tpu_custom_call" | custom-call | tf_op jit(solution)/shard_map/forward/pallas_call | solution.py:593
  81.1 0.7 slice_add_fusion
  81.8 0.0 copy-start
  81.8 8.8 %fusion.3 = (f32[512]{0:T(512)S(1)}, bf16[512,2048]{1,0:T(8,128)(2,1)S(1)}) fusion(bf16[512,2048]{1,0:T(8,128)(2,1)} %get-tuple-element.29.o_ref, bf16[2048,2048]{1,0:T(8,128)(2,1)} %bitcast.53), kind=kOutput, calls=%fused_computation.9 | convolution fusion | flops 4299161088 | bytes 12584960 | tf_op jit(solution)/shard_map/dot_general | solution.py:758
  90.6 0.0 copy-start.1
  90.6 0.0 copy-done
  90.6 2.0 fusion.9
  92.6 0.0 copy-done.1
  92.7 0.0 copy-start.8
  92.7 3.0 %fusion.2 = (bf16[512,2048]{1,0:T(8,128)(2,1)S(1)}, bf16[1,512,2048]{2,1,0:T(8,128)(2,1)}) fusion(bf16[512,2048]{1,0:T(8,128)(2,1)S(1)} %get-tuple-element.61, f32[512]{0:T(512)S(1)} %broadcast_multiply_fusion, f32[512]{0:T(512)S(1)} %get-tuple-element.58, f32[2048]{0:T(1024)S(1)} %bitcast.48, f32[512]{0:T(512)S(1)} %get-tuple-element.59, ...), kind=kLoop, calls=%fused_computation.8 | loop fusion | flops 15728640 | bytes 10500096 | tf_op jit(solution)/shard_map/convert_element_type | solution.py:795
  95.6 0.0 copy-start.2
  95.6 1.4 copy-done.2
  97.0 0.2 copy-done.8
  97.2 5.7 %convolution_convert_fusion.do_ref = bf16[512,2048]{1,0:T(8,128)(2,1)} fusion(bf16[512,2048]{1,0:T(8,128)(2,1)S(1)} %get-tuple-element.52.dz_ref, bf16[2048,2048]{1,0:T(8,128)(2,1)S(1)} %bitcast.54), kind=kOutput, calls=%fused_computation.17 | convolution fusion | flops 4296015872 | bytes 12582912 | tf_op jit(solution)/shard_map/dot_general | solution.py:758
  102.9 45.0 %attend_back.1 = (bf16[512,2560]{1,0:T(8,128)(2,1)}, f32[16,32,256]{2,1,0:T(8,128)}, f32[16,32,256]{2,1,0:T(8,128)}, f32[16,32,256]{2,1,0:T(8,128)}, f32[16,32,128]{2,1,0:T(8,128)}, /*index=5*/f32[16,32,128]{2,1,0:T(8,128)}) custom-call(bf16[512,2048]{1,0:T(8,128)(2,1)} %get-tuple-element.33.q_ref, bf16[512,2048]{1,0:T(8,128)(2,1)} %convolution_convert_fusion.do_ref, ...), custom_call_target="tpu_custom_call" | custom-call | tf_op jit(solution)/shard_map/attend_back/pallas_call | solution.py:707
  148.0 73.2 %scatter_grads.1 = (bf16[512,2048]{1,0:T(8,128)(2,1)}, f32[32,8,256]{2,1,0:T(8,128)}, f32[32,1,256]{2,1,0:T(1,128)}, f32[32,1,256]{2,1,0:T(1,128)}, f32[8,32,256]{2,1,0:T(8,128)}, /*index=5*/f32[2,16,128]{2,1,0:T(8,128)}) custom-call(bf16[512,2048]{1,0:T(8,128)(2,1)} %get-tuple-element.32.normed, bf16[512,2560]{1,0:T(8,128)(2,1)} %get-tuple-element.36.d_qkv, ...), custom_call_target="tpu_custom_call" | custom-call | tf_op jit(solution)/shard_map/scatter_grads/pallas_call | solution.py:417
  221.2 0.0 copy-start.4
  221.2 0.0 copy-start.7
  221.2 0.0 copy-start.6
  221.2 0.0 copy-start.3
  221.2 1.3 dynamic-slice_bitcast_fusion
  222.6 3.2 %copy.27 = bf16[1,512,2048]{2,1,0:T(8,128)(2,1)} copy(bf16[1,512,2048]{2,1,0:T(8,128)(2,1)} %bitcast.41) | data formatting | bytes 4194304
  225.7 0.0 copy-done.4
  225.7 0.7 copy.28
  226.4 0.0 copy-done.7
  226.4 0.6 copy.29
  227.1 0.0 copy-done.6
  227.1 0.6 copy.30
  227.7 0.0 copy-done.3
  227.7 0.7 copy.31
  (4 shorter events, 0.0 us)
Async XLA Ops:
  3.0 2.4 %copy-start.5 = (f32[8,256]{1,0:T(8,128)}, f32[8,256]{1,0:T(8,128)S(1)}, u32[]{:S(2)}) copy-start(f32[8,256]{1,0:T(8,128)S(1)} %dynamic_update_slice.7.in2) | copy-start | bytes 24580
  81.8 8.8 %copy-start = (bf16[1,512,2048]{2,1,0:T(8,128)(2,1)S(1)}, bf16[1,512,2048]{2,1,0:T(8,128)(2,1)}, u32[]{:S(2)}) copy-start(bf16[1,512,2048]{2,1,0:T(8,128)(2,1)} %param.12) | copy-start | bytes 6291460
  90.6 2.1 copy-start.1
  92.7 4.6 %copy-start.8 = (bf16[4,4,4,32,2048]{4,3,2,1,0:T(8,128)(2,1)S(1)}, bf16[4,4,4,32,2048]{4,3,2,1,0:T(8,128)(2,1)}, u32[]{:S(2)}) copy-start(bf16[4,4,4,32,2048]{4,3,2,1,0:T(8,128)(2,1)} %get-tuple-element.30) | copy-start | bytes 25165828
  95.6 1.4 copy-start.2
  221.2 4.5 %copy-start.4 = (f32[32,8,256]{2,1,0:T(8,128)S(1)}, f32[32,8,256]{2,1,0:T(8,128)}, u32[]{:S(2)}) copy-start(f32[32,8,256]{2,1,0:T(8,128)} %get-tuple-element.72) | copy-start | bytes 786436
  221.2 5.2 %copy-start.7 = (f32[32,1,256]{2,1,0:T(1,128)S(1)}, f32[32,1,256]{2,1,0:T(1,128)}, u32[]{:S(2)}) copy-start(f32[32,1,256]{2,1,0:T(1,128)} %get-tuple-element.73) | copy-start | bytes 98308
  221.2 5.8 %copy-start.6 = (f32[32,1,256]{2,1,0:T(1,128)S(1)}, f32[32,1,256]{2,1,0:T(1,128)}, u32[]{:S(2)}) copy-start(f32[32,1,256]{2,1,0:T(1,128)} %get-tuple-element.74) | copy-start | bytes 98308
  221.2 6.4 %copy-start.3 = (f32[8,32,256]{2,1,0:T(8,128)S(1)}, f32[8,32,256]{2,1,0:T(8,128)}, u32[]{:S(2)}) copy-start(f32[8,32,256]{2,1,0:T(8,128)} %get-tuple-element.48) | copy-start | bytes 786436

commit v7 on v6

--- a/solution.py
+++ b/solution.py
@@ -12,7 +12,6 @@
 ROPE_BASE = 10000.0
 MESH = pl.DeviceIdType.MESH
 SIDE = 4
-VMEM_MAX = 67_043_328
 
 QKV = ((0, 0, 256), (1, 256, 256), (2, 512, 256), (0, 768, 256), (1, 1024, 128), (2, 1152, 128))
 OUT = ((0, 0, 256), (1, 256, 256), (2, 512, 256), (1, 768, 128), (2, 896, 128))
@@ -41,7 +40,10 @@
         for delta in steps:
             pl.semaphore_signal(barrier, inc=1, device_id=device(shifted(coords, dim, delta), core), device_id_type=MESH)
     pl.semaphore_signal(barrier, inc=1, device_id=device(coords, 1 - core), device_id_type=MESH)
-    pl.semaphore_wait(barrier, 3 * len(steps) + 1)
+
+
+def greeted(steps=(1, -1)):
+    pl.semaphore_wait(pltpu.get_barrier_semaphore(), 3 * len(steps) + 1)
 
 
 def order_of(colour):
@@ -125,7 +127,8 @@
 
 
 class Scatter:
-    def __init__(self, streams, own, sib, acc, sbuf, rbuf, send, recv):
+    def __init__(self, streams, own, sib, acc, sbuf, rbuf, direct, send, recv):
+        self.direct = direct
         self.streams, self.own, self.sib = streams, own, sib
         self.acc, self.sbuf, self.rbuf, self.sems = acc, sbuf, rbuf, (send, recv)
         self.coords, self.core = place()
@@ -153,8 +156,11 @@
         return self.acc[s][q - 1][m, pl.ds(r0, nr), :]
 
     def hop(self, s, q, kind):
-        lo, n = ((0, 2), (2, 2), (4, 1), (5, 1))[kind]
-        to = shifted(self.coords, self.dim(s, q), (1, -1, 1, -1)[kind])
+        if q in self.direct:
+            lo, n, step = ((0, 2, 1), (2, 2, 2), (4, 2, -1))[kind]
+        else:
+            lo, n, step = ((0, 2, 1), (2, 2, -1), (4, 1, 1), (5, 1, -1))[kind]
+        to = shifted(self.coords, self.dim(s, q), step)
         return pltpu.make_async_remote_copy(
             self.sbuf[s][q].at[pl.ds(lo, n)], self.rbuf[s][q].at[pl.ds(lo, n)],
             self.sems[0].at[s, q, kind], self.sems[1].at[s, q, kind],
@@ -179,12 +185,24 @@
         def to_left(n):
             buf[2, n] = self.value(s, q, far, n, half).astype(buf.dtype)
             buf[3, n] = self.value(s, q, left, n, 0).astype(buf.dtype)
+
+        def straight(n):
+            for i, at in enumerate((right, far, left)):
+                for j in range(2):
+                    buf[2 * i + j, n] = self.value(s, q, at, n, j * half).astype(buf.dtype)
+        if q in self.direct:
+            self.each(q, straight)
+            for kind in range(3):
+                self.hop(s, q, kind).start()
+            return
         self.each(q, to_right)
         self.hop(s, q, 0).start()
         self.each(q, to_left)
         self.hop(s, q, 1).start()
 
     def two(self, s, q):
+        if q in self.direct:
+            return
         dim, half, buf, got = self.dim(s, q), self.half(s), self.sbuf[s][q], self.rbuf[s][q]
         right, left = (shifted(self.coords, dim, d) for d in (1, -1))
 
@@ -202,17 +220,20 @@
 
     def three(self, s, q):
         half, got, acc = self.half(s), self.rbuf[s][q], self.acc[s][q]
-        self.hop(s, q, 2).wait_recv()
-        self.hop(s, q, 3).wait_recv()
+        direct = q in self.direct
+        for kind in (0, 1, 2) if direct else (2, 3):
+            self.hop(s, q, kind).wait_recv()
 
         def keep(n):
-            for r0, i, j in ((0, 3, 4), (half, 1, 5)):
-                acc[n, pl.ds(r0, half), :] = (self.value(s, q, self.coords, n, r0) + got[i, n].astype(jnp.float32)
-                                              + got[j, n].astype(jnp.float32))
+            for r0, parts in ((0, (0, 2, 4) if direct else (3, 4)), (half, (1, 3, 5) if direct else (1, 5))):
+                total = self.value(s, q, self.coords, n, r0)
+                for i in parts:
+                    total = total + got[i, n].astype(jnp.float32)
+                acc[n, pl.ds(r0, half), :] = total
         self.each(q, keep)
 
     def drain(self, s, q):
-        for kind in range(4):
+        for kind in range(3 if q in self.direct else 4):
             self.hop(s, q, kind).wait_send()
 
 
@@ -274,31 +295,32 @@
     strips = dim // CHUNK
     coords, core = place()
     sibling = device(coords, 1 - core)
-    greet(coords, core)
+    greet(coords, core, (1, -1, 2))
 
     def triples(flat):
         return [flat[3 * s:3 * s + 3] for s in range(len(flat) // 3)]
 
     def tails(flat, heads):
         return [[heads[s]] + flat[2 * s:2 * s + 2] for s in range(no)]
-    qkv = Scatter(QKV, own_q, sib_q, triples(acc_q), triples(sbuf_q), triples(rbuf_q), *sems[0:2])
+    qkv = Scatter(QKV, own_q, sib_q, triples(acc_q), triples(sbuf_q), triples(rbuf_q), (2,), *sems[0:2])
     out = Scatter(OUT, None, None, tails(acc_o, acc_in), tails(sbuf_o, (None,) * no),
-                  tails(rbuf_o, (None,) * no), *sems[2:4])
-    gains = Scatter(GAIN, own_g, sib_in_g, triples(acc_g), triples(sbuf_g), triples(rbuf_g), *sems[4:6])
+                  tails(rbuf_o, (None,) * no), (2,), *sems[2:4])
+    gains = Scatter(GAIN, own_g, sib_in_g, triples(acc_g), triples(sbuf_g), triples(rbuf_g), (0, 1, 2), *sems[4:6])
     gain_gift = pltpu.make_async_remote_copy(sib_g, sib_in_g, gain_sem.at[0], gain_sem.at[1],
                                              device_id=sibling, device_id_type=MESH)
     loads = [pltpu.make_async_copy(w_ref.at[pl.ds(8 * j, 8)], w_buf.at[j % 2], w_sem.at[j]) for j in range(strips)]
     loads[0].start()
     loads[1].start()
-    for s in range(len(OUT)):
-        out.one(s, 1)
+    transpose_into(normed_t, normed)
     own_g[...] = jnp.zeros_like(own_g)
     sib_g[...] = jnp.zeros_like(sib_g)
-    transpose_into(normed_t, normed)
     chunks = own_q.shape[2] // CHUNK
     gifts = [chunk_gift(sib_out, sib_q, gift_send, gift_recv, j) for j in range(chunks)]
     grad_chunk(normed_t, d_qkv, sib_out, 1 - core, 0)
+    greeted((1, -1, 2))
     gifts[0].start()
+    for s in range(no):
+        out.one(s, 1)
     ready = 0
     for j in range(chunks):
         if j + 1 < chunks:
@@ -345,24 +367,25 @@
             own_g[SIDE * j + x, pl.ds(0, 1), :] = own_row[:, j * 128:(j + 1) * 128]
             sib_g[SIDE * j + x, pl.ds(0, 1), :] = sib_row[:, j * 128:(j + 1) * 128]
     gain_gift.start()
-    for scatter, s in work:
-        scatter.three(s, 0)
-        scatter.one(s, 1)
-    for s in range(len(OUT)):
-        out.three(s, 2)
+    for s in range(nq):
+        qkv.three(s, 0)
+        qkv.one(s, 1)
     gain_gift.wait_recv()
     gains.one(0, 0)
-    work = work + [(gains, 0)]
-    for q in range(3):
-        for scatter, s in work:
-            if q > 0 or scatter is gains:
-                scatter.two(s, q)
-        for scatter, s in work:
-            if q == 0 and scatter is not gains:
-                continue
-            scatter.three(s, q)
-            if q < 2:
-                scatter.one(s, q + 1)
+    for s in range(no):
+        out.three(s, 2)
+    for s in range(nq):
+        qkv.two(s, 1)
+    gains.three(0, 0)
+    gains.one(0, 1)
+    for s in range(nq):
+        qkv.three(s, 1)
+        qkv.one(s, 2)
+    gains.three(0, 1)
+    gains.one(0, 2)
+    for s in range(nq):
+        qkv.three(s, 2)
+    gains.three(0, 2)
     fins = []
     k = 0
     for scatter, ref in ((qkv, out_q), (out, out_o), (gains, out_g)):
@@ -421,7 +444,7 @@
                    jax.ShapeDtypeStruct((n_heads, rows, TILE), f32), jax.ShapeDtypeStruct((2, 16, 128), f32)],
         in_specs=[vmem] * 2 + [pl.BlockSpec(memory_space=pltpu.HBM)] + [vmem] * (5 + len(OUT)), out_specs=[vmem] * 6,
         scratch_shapes=scratch,
-        compiler_params=pltpu.CompilerParams(collective_id=2, has_side_effects=True, vmem_limit_bytes=VMEM_MAX),
+        compiler_params=pltpu.CompilerParams(collective_id=2, has_side_effects=True, vmem_limit_bytes=62914560),
     )(normed, d_qkv, w, x, dy, inv_rms, gain, post_row, *accs)
 
 
@@ -465,6 +488,9 @@
     qkv, out, gain = (Gather(st, src, dst, direct, *sems[4 * g:4 * g + 4]) for g, (st, src, dst, direct) in enumerate(
         ((QKV, in0, wq, (0,)), (OUT, in1, wo_out, (0,)), (GAIN, in2, gains, (0, 1, 2)))))
     nq = range(len(QKV))
+    wq[coords[0], coords[1], coords[2]] = in0[...]
+    gains[coords[0], coords[1], coords[2]] = in2[...]
+    greeted((1, -1, 2))
     gain.start(0, 0)
     for s in nq:
         qkv.start(s, 0)
@@ -472,8 +498,6 @@
         out.start(s, 0)
     own_out = pltpu.make_async_copy(in1, wo_out.at[coords[0], coords[1], coords[2]], own_sem.at[0])
     own_out.start()
-    wq[coords[0], coords[1], coords[2]] = in0[...]
-    gains[coords[0], coords[1], coords[2]] = in2[...]
 
     def stats(i, carry):
         at = pl.ds(i * 64, 64)
@@ -601,7 +625,7 @@
                         pltpu.VMEM((tiles, n_k, TILE), f32), pltpu.VMEM((tiles, n_k, TILE), bf)]
         + [dma((len(st), 3, 4)) for st in (QKV, OUT, GAIN) for _ in range(4)]
         + [dma((2,)), dma((1,)), dma((1,))],
-        compiler_params=pltpu.CompilerParams(collective_id=1, has_side_effects=True, vmem_limit_bytes=VMEM_MAX),
+        compiler_params=pltpu.CompilerParams(collective_id=1, has_side_effects=True, vmem_limit_bytes=35651584),
     )(x, cos_t, sin_t, pos, w0, w1, w2)
 
 
@@ -624,11 +648,12 @@
         lo, hi = u[:, :TILE // 2].astype(f32), u[:, TILE // 2:].astype(f32)
         c, s = cos_ref[pl.ds(0, u.shape[0]), :], sin_ref[pl.ds(0, u.shape[0]), :]
         return jnp.concatenate([lo * c + hi * s, hi * c - lo * s], axis=1).astype(bf)
-    out = Scatter(OUT, own, sib_in, [[a] for a in accs], [[b] for b in sbuf], [[b] for b in rbuf], *sems)
+    out = Scatter(OUT, own, sib_in, [[a] for a in accs], [[b] for b in sbuf], [[b] for b in rbuf], (), *sems)
     chunks = own.shape[2] // CHUNK
     transpose_into(dz_t, dz_ref)
     gifts = [chunk_gift(sib_out, sib_in, gift_send, gift_recv, j) for j in range(chunks)]
     grad_chunk(dz_t, o_ref, sib_out, 1 - core, 0)
+    greeted()
     gifts[0].start()
     ready = 0
     for j in range(chunks):
@@ -718,7 +743,7 @@
         + [pltpu.VMEM((dz.shape[1] // 32, 32, o.shape[1] // 2), bf)] * 2
         + wire_shapes(OUT, bf, 32, (0,)) * 2 + [pltpu.SemaphoreType.DMA((len(OUT), 3, 4))] * 2
         + [pltpu.SemaphoreType.DMA((o.shape[1] // 2 // CHUNK,))] * 2 + [pltpu.SemaphoreType.DMA((2,))],
-        compiler_params=pltpu.CompilerParams(collective_id=4, has_side_effects=True, vmem_limit_bytes=VMEM_MAX),
+        compiler_params=pltpu.CompilerParams(collective_id=4, has_side_effects=True, vmem_limit_bytes=50331648),
     )(q, do, kv, pos, inv_sum, dz, o, cos_t, sin_t)
 
 

time: 229 us -> 222 us (0.969)
  Pallas kernels: 191 us -> 176 us
  local copies, waits for them, and re-layouts: 11.6 us -> 20.4 us
    unnamed x24 -> x48, local copies, waits for them, and re-layouts: 8.37 us -> 17.9 us
    pallas_call x1, Pallas kernels: 73.2 us -> 67.4 us  [scatter_grads(): pl.pallas_call(scatter_kernel, name='scatter_grads', out_shape=[jax.Shape...]
    pallas_call x1, Pallas kernels: 72.3 us -> 67 us  [forward(): pl.pallas_call(functools.partial(forward_kernel, ratio), name='forward',...]
    pallas_call x1, Pallas kernels: 45 us -> 41.2 us  [attend_back(): pl.pallas_call(functools.partial(attend_back_kernel, ratio), name='attend...]
where the time goes in v7:
time: 222 us; the launch traced here: 221 us
  Pallas kernels  176 us (79%)
  local copies, waits for them, and re-layouts  20.4 us (9%)
  matrix products  15.6 us (7%)
  other arithmetic  8.92 us (4%)
    pallas_call x1, Pallas kernels, scatter_grads(): pl.pallas_call(scatter_kernel, name='scatter_grads', out_shape=[jax.Shape...  67.4 us
    pallas_call x1, Pallas kernels, forward(): pl.pallas_call(functools.partial(forward_kernel, ratio), name='forward',...  67 us
    pallas_call x1, Pallas kernels, attend_back(): pl.pallas_call(functools.partial(attend_back_kernel, ratio), name='attend...  41.2 us
    unnamed x48, local copies, waits for them, and re-layouts  17.9 us
    dot_general x2, matrix products, dot(): lax.dot_general(a, b, ((dims[:1], dims[1:]), ((), ())), preferred_element...  15.6 us

profile of v7, /device:TPU:1, one launch (start us, length us, event | category | flops | bytes accessed | tf_op | source)
XLA Modules:
  0.0 221.4 jit_solution(12178114167526567640)
XLA Ops:
  0.6 0.7 bitcast_convert_fusion.1
  1.3 0.7 bitcast_convert_fusion
  2.0 0.7 convert_element_type.41
  2.7 0.1 dynamic_update_slice.6
  2.8 0.2 dynamic_update_slice.7.in2
  3.0 0.9 copy.19
  3.9 0.7 pad_maximum_fusion.in0
  4.7 0.9 copy.18
  5.6 1.0 multiply_sine_fusion
  6.6 0.0 copy-start
  6.6 1.6 copy-done
  8.2 0.7 copy-done.11
  8.9 67.0 %forward.1 = (bf16[4,4,4,32,2560]{4,3,2,1,0:T(8,128)(2,1)}, bf16[4,4,4,32,2048]{4,3,2,1,0:T(8,128)(2,1)S(1)}, f32[2,2048]{1,0:T(2,128)S(1)}, bf16[512,2048]{1,0:...) custom-call(bf16[512,2048]{1,0:T(8,128)(2,1)S(1)} %bitcast.38, ...), custom_call_target="tpu_custom_call" | custom-call | tf_op jit(solution)/shard_map/forward/pallas_call | solution.py:617
  75.9 0.0 copy-start.7
  75.9 0.7 copy-done.7
  76.6 3.3 %copy-done.13 = bf16[4,4,4,32,2048]{4,3,2,1,0:T(8,128)(2,1)} copy-done((bf16[4,4,4,32,2048]{4,3,2,1,0:T(8,128)(2,1)}, bf16[4,4,4,32,2048]{4,3,2,1,0:T(8,128)(2,1)S(1)}, u32[]{:S(2)}) %copy-start.13) | copy-done | bytes 8388632
  79.9 0.0 copy-start.15
  79.9 9.8 %fusion.3 = (f32[512]{0:T(512)S(1)}, bf16[512,2048]{1,0:T(8,128)(2,1)S(1)}) fusion(bf16[512,2048]{1,0:T(8,128)(2,1)S(1)} %get-tuple-element.29.o_ref, bf16[2048,2048]{1,0:T(8,128)(2,1)} %bitcast.40), kind=kOutput, calls=%fused_computation.9 | convolution fusion | flops 4299161088 | bytes 12584960 | tf_op jit(solution)/shard_map/dot_general | solution.py:783
  89.8 0.0 copy-done.2
  89.8 0.0 copy-done.3
  89.8 0.0 copy-done.10
  89.8 0.0 copy-start.1
  89.8 0.0 copy-done.15
  89.8 2.0 fusion.9
  91.9 0.0 copy-done.1
  91.9 3.1 %fusion.2 = (bf16[512,2048]{1,0:T(8,128)(2,1)S(1)}, bf16[1,512,2048]{2,1,0:T(8,128)(2,1)}) fusion(bf16[512,2048]{1,0:T(8,128)(2,1)S(1)} %get-tuple-element.61, f32[512]{0:T(512)S(1)} %broadcast_multiply_fusion, f32[512]{0:T(512)S(1)} %get-tuple-element.58, f32[2048]{0:T(1024)S(1)} %bitcast.50, f32[512]{0:T(512)S(1)} %get-tuple-element.59, ...), kind=kLoop, calls=%fused_computation.8 | loop fusion | flops 15728640 | bytes 10500096 | tf_op jit(solution)/shard_map/convert_element_type | solution.py:820
  95.0 1.0 copy-done.14
  96.0 5.8 %convolution_convert_fusion.do_ref = bf16[512,2048]{1,0:T(8,128)(2,1)} fusion(bf16[512,2048]{1,0:T(8,128)(2,1)S(1)} %get-tuple-element.52.dz_ref, bf16[2048,2048]{1,0:T(8,128)(2,1)S(1)} %bitcast.41), kind=kOutput, calls=%fused_computation.17 | convolution fusion | flops 4296015872 | bytes 12582912 | tf_op jit(solution)/shard_map/dot_general | solution.py:783
  101.8 0.0 copy-done.16
  101.8 0.0 copy-done.12
  101.8 41.2 %attend_back.1 = (bf16[512,2560]{1,0:T(8,128)(2,1)}, f32[16,32,256]{2,1,0:T(8,128)S(1)}, f32[16,32,256]{2,1,0:T(8,128)S(1)}, f32[16,32,256]{2,1,0:T(8,128)S(1)},...) custom-call(bf16[512,2048]{1,0:T(8,128)(2,1)S(1)} %get-tuple-element.33.q_ref, ...), custom_call_target="tpu_custom_call" | custom-call | tf_op jit(solution)/shard_map/attend_back/pallas_call | solution.py:732
  143.1 0.0 copy-start.4
  143.1 0.8 copy-done.4
  143.9 0.8 copy-done.5
  144.7 0.8 copy-done.6
  145.5 0.7 copy-done.8
  146.2 0.7 copy-done.9
  146.9 67.4 %scatter_grads.1 = (bf16[512,2048]{1,0:T(8,128)(2,1)}, f32[32,8,256]{2,1,0:T(8,128)}, f32[32,1,256]{2,1,0:T(1,128)}, f32[32,1,256]{2,1,0:T(1,128)}, f32[8,32,256]{2,1,0:T(8,128)}, /*index=5*/f32[2,16,128]{2,1,0:T(8,128)}) custom-call(bf16[512,2048]{1,0:T(8,128)(2,1)} %copy-done.2, bf16[512,2560]{1,0:T(8,128)(2,1)} %get-tuple-element.36.d_qkv, ...), custom_call_target="tpu_custom_call" | custom-call | tf_op jit(solution)/shard_map/scatter_grads/pallas_call | solution.py:440
  214.3 0.0 copy-start.18
  214.3 0.0 copy-start.20
  214.3 1.3 dynamic-slice_bitcast_fusion
  215.6 3.2 %copy.27 = bf16[1,512,2048]{2,1,0:T(8,128)(2,1)} copy(bf16[1,512,2048]{2,1,0:T(8,128)(2,1)} %bitcast.44) | data formatting | bytes 4194304
  218.8 0.0 copy-done.18
  218.8 0.7 copy.28
  219.5 0.6 copy.29
  220.1 0.6 copy.30
  220.7 0.0 copy-done.17
  220.7 0.7 copy.31
  (21 shorter events, 0.1 us)
Async XLA Ops:
  6.6 1.6 copy-start
  8.2 0.7 copy-start.11
  75.9 0.7 copy-start.7
  76.6 3.3 %copy-start.13 = (bf16[4,4,4,32,2048]{4,3,2,1,0:T(8,128)(2,1)}, bf16[4,4,4,32,2048]{4,3,2,1,0:T(8,128)(2,1)S(1)}, u32[]{:S(2)}) copy-start(bf16[4,4,4,32,2048]{4,3,2,1,0:T(8,128)(2,1)S(1)} %get-tuple-element.30) | copy-start | bytes 25165828
  79.9 9.9 %copy-start.2 = (bf16[512,2048]{1,0:T(8,128)(2,1)}, bf16[512,2048]{1,0:T(8,128)(2,1)S(1)}, u32[]{:S(2)}) copy-start(bf16[512,2048]{1,0:T(8,128)(2,1)S(1)} %get-tuple-element.32.normed) | copy-start | bytes 6291460
  79.9 9.9 %copy-start.3 = (bf16[512,2048]{1,0:T(8,128)(2,1)}, bf16[512,2048]{1,0:T(8,128)(2,1)S(1)}, u32[]{:S(2)}) copy-start(bf16[512,2048]{1,0:T(8,128)(2,1)S(1)} %get-tuple-element.29.o_ref) | copy-start | bytes 6291460
  79.9 9.9 %copy-start.10 = (f32[2,2048]{1,0:T(2,128)}, f32[2,2048]{1,0:T(2,128)S(1)}, u32[]{:S(2)}) copy-start(f32[2,2048]{1,0:T(2,128)S(1)} %get-tuple-element.31.gain) | copy-start | bytes 49156
  79.9 9.9 %copy-start.15 = (bf16[1,512,2048]{2,1,0:T(8,128)(2,1)S(1)}, bf16[1,512,2048]{2,1,0:T(8,128)(2,1)}, u32[]{:S(2)}) copy-start(bf16[1,512,2048]{2,1,0:T(8,128)(2,1)} %param.12) | copy-start | bytes 6291460
  89.8 2.1 copy-start.1
  91.9 4.1 %copy-start.14 = (bf16[4,4,4,32,2048]{4,3,2,1,0:T(8,128)(2,1)S(1)}, bf16[4,4,4,32,2048]{4,3,2,1,0:T(8,128)(2,1)}, u32[]{:S(2)}) copy-start(bf16[4,4,4,32,2048]{4,3,2,1,0:T(8,128)(2,1)} %copy-done.13) | copy-start | bytes 25165828
  95.0 6.8 %copy-start.16 = (bf16[512,2048]{1,0:T(8,128)(2,1)}, bf16[512,2048]{1,0:T(8,128)(2,1)S(1)}, u32[]{:S(2)}) copy-start(bf16[512,2048]{1,0:T(8,128)(2,1)S(1)} %get-tuple-element.52.dz_ref) | copy-start | bytes 6291460
  96.0 5.8 %copy-start.12 = (s32[1,512]{1,0:T(1,128)S(1)}, s32[1,512]{1,0:T(1,128)}, u32[]{:S(2)}) copy-start(s32[1,512]{1,0:T(1,128)} %pos.3) | copy-start | bytes 6148
  143.1 0.8 copy-start.4
  143.9 0.8 copy-start.5
  144.7 0.8 copy-start.6
  145.5 0.7 copy-start.8
  146.2 0.7 copy-start.9
  214.3 4.5 %copy-start.18 = (f32[32,8,256]{2,1,0:T(8,128)S(1)}, f32[32,8,256]{2,1,0:T(8,128)}, u32[]{:S(2)}) copy-start(f32[32,8,256]{2,1,0:T(8,128)} %get-tuple-element.72) | copy-start | bytes 786436
  214.3 5.2 %copy-start.20 = (f32[32,1,256]{2,1,0:T(1,128)S(1)}, f32[32,1,256]{2,1,0:T(1,128)}, u32[]{:S(2)}) copy-start(f32[32,1,256]{2,1,0:T(1,128)} %get-tuple-element.73) | copy-start | bytes 98308
  214.3 5.8 %copy-start.19 = (f32[32,1,256]{2,1,0:T(1,128)S(1)}, f32[32,1,256]{2,1,0:T(1,128)}, u32[]{:S(2)}) copy-start(f32[32,1,256]{2,1,0:T(1,128)} %get-tuple-element.74) | copy-start | bytes 98308
  214.3 6.4 %copy-start.17 = (f32[8,32,256]{2,1,0:T(8,128)S(1)}, f32[8,32,256]{2,1,0:T(8,128)}, u32[]{:S(2)}) copy-start(f32[8,32,256]{2,1,0:T(8,128)} %get-tuple-element.48) | copy-start | bytes 786436

commit v8 on v7

--- a/solution.py
+++ b/solution.py
@@ -338,16 +338,21 @@
             for s in range(no):
                 out.three(s, 1)
                 out.one(s, 2)
-    for j in range(strips):
+
+    def strip(j):
         loads[j].wait()
         dn[:, pl.ds(j * CHUNK, CHUNK)] = nt(d_qkv[...], w_buf[j % 2].reshape(CHUNK, d_qkv.shape[1])).astype(bf)
         if j + 2 < strips:
             loads[j + 2].start()
-    work = [(qkv, s) for s in range(nq)]
-    for s in range(len(OUT)):
-        out.two(s, 2)
-    for scatter, s in work:
-        scatter.two(s, 0)
+    for j in range(strips // 2):
+        strip(j)
+    for s in range(nq):
+        qkv.two(s, 0)
+    for j in range(strips // 2, strips):
+        strip(j)
+    for s in range(nq):
+        qkv.three(s, 0)
+        qkv.one(s, 1)
     pre_row[...] = jnp.zeros_like(pre_row)
     one_gain = 1.0 + gain[pl.ds(0, 1), :]
 
@@ -368,28 +373,21 @@
             sib_g[SIDE * j + x, pl.ds(0, 1), :] = sib_row[:, j * 128:(j + 1) * 128]
     gain_gift.start()
     for s in range(nq):
-        qkv.three(s, 0)
-        qkv.one(s, 1)
+        qkv.two(s, 1)
     gain_gift.wait_recv()
     gains.one(0, 0)
     for s in range(no):
         out.three(s, 2)
     for s in range(nq):
-        qkv.two(s, 1)
+        qkv.three(s, 1)
+        qkv.one(s, 2)
     gains.three(0, 0)
     gains.one(0, 1)
-    for s in range(nq):
-        qkv.three(s, 1)
-        qkv.one(s, 2)
-    gains.three(0, 1)
-    gains.one(0, 2)
-    for s in range(nq):
-        qkv.three(s, 2)
-    gains.three(0, 2)
     fins = []
-    k = 0
-    for scatter, ref in ((qkv, out_q), (out, out_o), (gains, out_g)):
+
+    def give(scatter, ref):
         for s, (_, off, width) in enumerate(scatter.streams):
+            k = len(fins)
             part = scatter.acc[s][2].at[0]
             ref[core, :, pl.ds(off, width)] = scatter.acc[s][2][0]
             here, there = (ref.at[side, :, pl.ds(off, width)] for side in (core, 1 - core))
@@ -397,7 +395,14 @@
                                                  device_id=sibling, device_id_type=MESH) for side in (here, there)]
             pair[0].start()
             fins.append(pair)
-            k += 1
+    give(out, out_o)
+    for s in range(nq):
+        qkv.three(s, 2)
+    give(qkv, out_q)
+    gains.three(0, 1)
+    gains.one(0, 2)
+    gains.three(0, 2)
+    give(gains, out_g)
     for mine, theirs in fins:
         mine.wait_send()
         theirs.wait_recv()
@@ -625,7 +630,7 @@
                         pltpu.VMEM((tiles, n_k, TILE), f32), pltpu.VMEM((tiles, n_k, TILE), bf)]
         + [dma((len(st), 3, 4)) for st in (QKV, OUT, GAIN) for _ in range(4)]
         + [dma((2,)), dma((1,)), dma((1,))],
-        compiler_params=pltpu.CompilerParams(collective_id=1, has_side_effects=True, vmem_limit_bytes=35651584),
+        compiler_params=pltpu.CompilerParams(collective_id=1, has_side_effects=True, vmem_limit_bytes=48234496),
     )(x, cos_t, sin_t, pos, w0, w1, w2)
 
 
@@ -743,7 +748,7 @@
         + [pltpu.VMEM((dz.shape[1] // 32, 32, o.shape[1] // 2), bf)] * 2
         + wire_shapes(OUT, bf, 32, (0,)) * 2 + [pltpu.SemaphoreType.DMA((len(OUT), 3, 4))] * 2
         + [pltpu.SemaphoreType.DMA((o.shape[1] // 2 // CHUNK,))] * 2 + [pltpu.SemaphoreType.DMA((2,))],
-        compiler_params=pltpu.CompilerParams(collective_id=4, has_side_effects=True, vmem_limit_bytes=50331648),
+        compiler_params=pltpu.CompilerParams(collective_id=4, has_side_effects=True, vmem_limit_bytes=56623104),
     )(q, do, kv, pos, inv_sum, dz, o, cos_t, sin_t)
 
 

time: 222 us -> 218 us (0.982)
  local copies, waits for them, and re-layouts: 20.4 us -> 11.6 us
  Pallas kernels: 176 us -> 180 us
    unnamed x48 -> x40, local copies, waits for them, and re-layouts: 17.9 us -> 9.03 us
    pallas_call x1, Pallas kernels: 67 us -> 70.3 us  [forward(): pl.pallas_call(functools.partial(forward_kernel, ratio), name='forward',...]
where the time goes in v8:
time: 218 us; the launch traced here: 217 us
  Pallas kernels  180 us (83%)
  matrix products  16.3 us (7%)
  local copies, waits for them, and re-layouts  11.6 us (5%)
  other arithmetic  8.75 us (4%)
    pallas_call x1, Pallas kernels, forward(): pl.pallas_call(functools.partial(forward_kernel, ratio), name='forward',...  70.3 us
    pallas_call x1, Pallas kernels, scatter_grads(): pl.pallas_call(scatter_kernel, name='scatter_grads', out_shape=[jax.Shape...  66.4 us
    pallas_call x1, Pallas kernels, attend_back(): pl.pallas_call(functools.partial(attend_back_kernel, ratio), name='attend...  42.8 us
    dot_general x2, matrix products, dot(): lax.dot_general(a, b, ((dims[:1], dims[1:]), ((), ())), preferred_element...  16.3 us
    unnamed x40, local copies, waits for them, and re-layouts  9.03 us

profile of v8, /device:TPU:1, one launch (start us, length us, event | category | flops | bytes accessed | tf_op | source)
XLA Modules:
  0.0 217.2 jit_solution(1872930465367753222)
XLA Ops:
  0.6 0.7 bitcast_convert_fusion.1
  1.3 0.7 bitcast_convert_fusion
  2.0 0.7 convert_element_type.41
  2.7 0.1 dynamic_update_slice.6
  2.8 0.2 dynamic_update_slice.7.in2
  3.0 0.9 copy.19
  3.9 0.7 pad_maximum_fusion.in0
  4.7 0.9 copy.18
  5.6 1.0 multiply_sine_fusion
  6.6 0.0 copy-start
  6.6 0.0 copy-start.1
  6.6 0.0 copy-start.7
  6.6 0.7 copy-done.7
  7.3 70.3 %forward.1 = (bf16[4,4,4,32,2560]{4,3,2,1,0:T(8,128)(2,1)}, bf16[4,4,4,32,2048]{4,3,2,1,0:T(8,128)(2,1)}, f32[2,2048]{1,0:T(2,128)S(1)}, bf16[512,2048]{1,0:T(8,...) custom-call(bf16[512,2048]{1,0:T(8,128)(2,1)} %bitcast.39, ...), custom_call_target="tpu_custom_call" | custom-call | tf_op jit(solution)/shard_map/forward/pallas_call | solution.py:622
  77.7 0.0 copy-start.2
  77.7 0.0 copy-start.3
  77.7 0.0 copy-start.4
  77.7 0.0 copy-start.5
  77.7 0.0 copy-start.6
  77.7 0.0 copy-start.8
  77.8 0.0 copy-start.9
  77.8 10.6 %fusion.3 = (f32[512]{0:T(512)S(1)}, bf16[512,2048]{1,0:T(8,128)(2,1)S(1)}) fusion(bf16[512,2048]{1,0:T(8,128)(2,1)} %get-tuple-element.29.o_ref, bf16[2048,2048]{1,0:T(8,128)(2,1)} %bitcast.53), kind=kOutput, calls=%fused_computation.9 | convolution fusion | flops 4299161088 | bytes 12584960 | tf_op jit(solution)/shard_map/dot_general | solution.py:788
  88.3 0.0 copy-done
  88.3 0.0 copy-done.1
  88.3 0.0 copy-done.2
  88.4 0.0 copy-done.3
  88.4 0.0 copy-done.4
  88.4 0.0 copy-done.5
  88.4 0.0 copy-done.6
  88.4 0.0 copy-done.8
  88.4 0.0 copy-start.10
  88.4 0.0 copy-done.9
  88.4 2.0 fusion.9
  90.5 0.0 copy-done.10
  90.5 3.0 %fusion.2 = (bf16[512,2048]{1,0:T(8,128)(2,1)S(1)}, bf16[1,512,2048]{2,1,0:T(8,128)(2,1)}) fusion(bf16[512,2048]{1,0:T(8,128)(2,1)S(1)} %get-tuple-element.61, f32[512]{0:T(512)S(1)} %broadcast_multiply_fusion, f32[512]{0:T(512)S(1)} %get-tuple-element.58, f32[2048]{0:T(1024)S(1)} %bitcast.48, f32[512]{0:T(512)S(1)} %get-tuple-element.59, ...), kind=kLoop, calls=%fused_computation.8 | loop fusion | flops 15728640 | bytes 10500096 | tf_op jit(solution)/shard_map/convert_element_type | solution.py:825
  93.4 1.3 copy-done.11
  94.8 0.2 copy-done.16
  95.0 5.7 %convolution_convert_fusion.do_ref = bf16[512,2048]{1,0:T(8,128)(2,1)} fusion(bf16[512,2048]{1,0:T(8,128)(2,1)S(1)} %get-tuple-element.52.dz_ref, bf16[2048,2048]{1,0:T(8,128)(2,1)S(1)} %bitcast.54), kind=kOutput, calls=%fused_computation.17 | convolution fusion | flops 4296015872 | bytes 12582912 | tf_op jit(solution)/shard_map/dot_general | solution.py:788
  100.7 42.8 %attend_back.1 = (bf16[512,2560]{1,0:T(8,128)(2,1)}, f32[16,32,256]{2,1,0:T(8,128)}, f32[16,32,256]{2,1,0:T(8,128)}, f32[16,32,256]{2,1,0:T(8,128)}, f32[16,32,128]{2,1,0:T(8,128)}, /*index=5*/f32[16,32,128]{2,1,0:T(8,128)}) custom-call(bf16[512,2048]{1,0:T(8,128)(2,1)} %copy-done.3, bf16[512,2048]{1,0:T(8,128)(2,1)} %convolution_convert_fusion.do_ref, ...), custom_call_target="tpu_custom_call" | custom-call | tf_op jit(solution)/shard_map/attend_back/pallas_call | solution.py:737
  143.6 66.4 %scatter_grads.1 = (bf16[512,2048]{1,0:T(8,128)(2,1)}, f32[32,8,256]{2,1,0:T(8,128)}, f32[32,1,256]{2,1,0:T(1,128)}, f32[32,1,256]{2,1,0:T(1,128)}, f32[8,32,256]{2,1,0:T(8,128)}, /*index=5*/f32[2,16,128]{2,1,0:T(8,128)}) custom-call(bf16[512,2048]{1,0:T(8,128)(2,1)} %copy-done.2, bf16[512,2560]{1,0:T(8,128)(2,1)} %get-tuple-element.36.d_qkv, ...), custom_call_target="tpu_custom_call" | custom-call | tf_op jit(solution)/shard_map/scatter_grads/pallas_call | solution.py:445
  210.0 0.0 copy-start.13
  210.0 1.3 dynamic-slice_bitcast_fusion
  211.3 3.2 %copy.27 = bf16[1,512,2048]{2,1,0:T(8,128)(2,1)} copy(bf16[1,512,2048]{2,1,0:T(8,128)(2,1)} %bitcast.42) | data formatting | bytes 4194304
  214.5 0.7 copy.28
  215.2 0.0 copy-done.15
  215.2 0.6 copy.29
  215.8 0.6 copy.30
  216.5 0.7 copy.31
  (13 shorter events, 0.1 us)
Async XLA Ops:
  6.6 81.7 %copy-start = (f32[512,128]{1,0:T(8,128)}, f32[512,128]{1,0:T(8,128)S(1)}, u32[]{:S(2)}) copy-start(f32[512,128]{1,0:T(8,128)S(1)} %get-tuple-element.56.sin_ref) | copy-start | bytes 786436
  6.6 81.7 %copy-start.1 = (f32[512,128]{1,0:T(8,128)}, f32[512,128]{1,0:T(8,128)S(1)}, u32[]{:S(2)}) copy-start(f32[512,128]{1,0:T(8,128)S(1)} %get-tuple-element.57.cos_ref) | copy-start | bytes 786436
  6.6 0.7 copy-start.7
  77.7 10.7 %copy-start.2 = (bf16[512,2048]{1,0:T(8,128)(2,1)}, bf16[512,2048]{1,0:T(8,128)(2,1)S(1)}, u32[]{:S(2)}) copy-start(bf16[512,2048]{1,0:T(8,128)(2,1)S(1)} %get-tuple-element.32.normed) | copy-start | bytes 6291460
  77.7 10.7 %copy-start.3 = (bf16[512,2048]{1,0:T(8,128)(2,1)}, bf16[512,2048]{1,0:T(8,128)(2,1)S(1)}, u32[]{:S(2)}) copy-start(bf16[512,2048]{1,0:T(8,128)(2,1)S(1)} %get-tuple-element.33.q_ref) | copy-start | bytes 6291460
  77.7 10.7 %copy-start.4 = (bf16[1024,512]{1,0:T(8,128)(2,1)}, bf16[1024,512]{1,0:T(8,128)(2,1)S(1)}, u32[]{:S(2)}) copy-start(bf16[1024,512]{1,0:T(8,128)(2,1)S(1)} %get-tuple-element.34.kv_ref) | copy-start | bytes 3145732
  77.7 10.7 %copy-start.5 = (f32[512,1]{1,0:T(8,128)}, f32[512,1]{1,0:T(8,128)S(1)}, u32[]{:S(2)}) copy-start(f32[512,1]{1,0:T(8,128)S(1)} %get-tuple-element.38.inv_rms) | copy-start | bytes 6148
  77.7 10.7 %copy-start.6 = (f32[2,2048]{1,0:T(2,128)}, f32[2,2048]{1,0:T(2,128)S(1)}, u32[]{:S(2)}) copy-start(f32[2,2048]{1,0:T(2,128)S(1)} %get-tuple-element.31.gain) | copy-start | bytes 49156
  77.7 10.7 %copy-start.8 = (f32[8,1,512]{2,1,0:T(1,128)}, f32[8,1,512]{2,1,0:T(1,128)S(1)}, u32[]{:S(2)}) copy-start(f32[8,1,512]{2,1,0:T(1,128)S(1)} %get-tuple-element.35.inv_ref) | copy-start | bytes 49156
  77.8 10.7 %copy-start.9 = (bf16[1,512,2048]{2,1,0:T(8,128)(2,1)S(1)}, bf16[1,512,2048]{2,1,0:T(8,128)(2,1)}, u32[]{:S(2)}) copy-start(bf16[1,512,2048]{2,1,0:T(8,128)(2,1)} %param.12) | copy-start | bytes 6291460
  88.4 2.1 copy-start.10
  90.5 4.5 %copy-start.16 = (bf16[4,4,4,32,2048]{4,3,2,1,0:T(8,128)(2,1)S(1)}, bf16[4,4,4,32,2048]{4,3,2,1,0:T(8,128)(2,1)}, u32[]{:S(2)}) copy-start(bf16[4,4,4,32,2048]{4,3,2,1,0:T(8,128)(2,1)} %get-tuple-element.30) | copy-start | bytes 25165828
  93.4 1.4 copy-start.11
  210.0 4.5 %copy-start.13 = (f32[32,8,256]{2,1,0:T(8,128)S(1)}, f32[32,8,256]{2,1,0:T(8,128)}, u32[]{:S(2)}) copy-start(f32[32,8,256]{2,1,0:T(8,128)} %get-tuple-element.72) | copy-start | bytes 786436
  210.0 5.2 %copy-start.15 = (f32[32,1,256]{2,1,0:T(1,128)S(1)}, f32[32,1,256]{2,1,0:T(1,128)}, u32[]{:S(2)}) copy-start(f32[32,1,256]{2,1,0:T(1,128)} %get-tuple-element.73) | copy-start | bytes 98308
  210.0 5.8 %copy-start.14 = (f32[32,1,256]{2,1,0:T(1,128)S(1)}, f32[32,1,256]{2,1,0:T(1,128)}, u32[]{:S(2)}) copy-start(f32[32,1,256]{2,1,0:T(1,128)} %get-tuple-element.74) | copy-start | bytes 98308
  210.0 6.4 %copy-start.12 = (f32[8,32,256]{2,1,0:T(8,128)S(1)}, f32[8,32,256]{2,1,0:T(8,128)}, u32[]{:S(2)}) copy-start(f32[8,32,256]{2,1,0:T(8,128)} %get-tuple-element.48) | copy-start | bytes 786436
